TPU v7x, 256 devices: a whole 4x4x8 slice. The times are simulated.
256 devices in a mesh: seq: 32 (over z, x), chan: 8 (over y, core).
Axes of the slice: x: 4, y: 4, z: 8, core: 2. Of those that a mesh axis runs over, the one named last changes fastest.
Arguments:
- hidden: bfloat16 [8, 8192], replicated, may hold values from -6 to 6
- norm_gain: float32 [3, 8192], replicated, may hold values from 0.25 to 1.75
- in_weight: bfloat16 [2, 8192, 2, 16384], P(None, None, None, ('seq', 'chan')), may hold values from -0.25 to 0.25
- conv_weight: float32 [2, 4, 16384], P(None, None, ('seq', 'chan')), may hold values from -3 to 3
- conv_bias: float32 [2, 16384], P(None, ('seq', 'chan')), may hold values from -3 to 3
- conv_state: bfloat16 [2, 8, 3, 16384], P(None, None, None, ('seq', 'chan')), may hold values from -6 to 6
- xproj_weight: bfloat16 [2, 16384, 544], P(None, ('seq', 'chan')), may hold values from -0.09375 to 0.09375
- dt_weight: bfloat16 [2, 512, 16384], P(None, None, ('seq', 'chan')), may hold values from -0.25 to 0.25
- dt_bias: float32 [2, 16384], P(None, ('seq', 'chan')), may hold values from -4.6 to -2.3
- a_log: float32 [2, 16, 16384], P(None, None, ('seq', 'chan')), may hold values from 0 to 2.77
- skip_gain: float32 [2, 16384], P(None, ('seq', 'chan')), may hold values from 0.5 to 1.5
- ssm_state: float32 [2, 8, 16, 16384], P(None, None, None, ('seq', 'chan')), may hold values from -6 to 6
- out_weight: bfloat16 [2, 16384, 8192], P(None, ('seq', 'chan')), may hold values from -0.1875 to 0.1875
- asker_lookup_matrix: bfloat16 [8192, 8, 1280], P('seq', 'chan'), may hold values from -0.0625 to 0.0625
- o_weight: bfloat16 [8, 1024, 8192], P('chan', None, 'seq'), may hold values from -0.09375 to 0.09375
- kv_cache: bfloat16 [256, 256, 2, 8, 128], P('seq', None, None, 'chan'), may hold values from -64 to 64
- lengths: int32 [8], replicated, may hold values from 1 to 8192, as said below
- page_table: int32 [8, 32], replicated, may hold values from -1 to 255, as said below
Outputs:
- hidden_out: bfloat16 [8, 8192], P(None, ('seq', 'chan'))
- new_ssm: float32 [2, 8, 16, 16384], P(None, None, None, ('seq', 'chan'))
- new_conv: bfloat16 [2, 8, 3, 16384], P(None, None, None, ('seq', 'chan'))
- newest_pair: bfloat16 [8, 8, 2, 128], P(None, 'chan')
Inputs may be any that keep to these rules, and one draw needn't show every extreme that they name: `lengths`: each request's context holds 1 to 8192 tokens; one request holds exactly 8192. page_table[b, j] for j < ceil(lengths[b] / 256) is the cache slot (index along seq times 8 plus the local slot) holding block j of request b; these slots are all different; every other entry is -1. Used slots are spread very unevenly: some devices along seq have all 8 of theirs used, others few or none.
All inputs are finite; a program needn't handle non-finite values.
Results may differ from a plain program's by a relative error of at most 0.018.
Values may be sent and summed in bfloat16 or wider, within the bound.
No kernel may reach another device: no remote copies, remote signals or barrier semaphores. Data moves between devices by JAX's collectives and lax.ppermute only.
A program may use at most 64 MiB of HBM per device.

v0:
```python
import jax
import jax.numpy as jnp
from jax import lax
from jax.sharding import Mesh
from jax.sharding import PartitionSpec as P

SEQ_CHAN = ("seq_0", "seq_1", "chan_0", "chan_1")
SEQ = ("seq_0", "seq_1")
CHAN = ("chan_0", "chan_1")


norm_eps = 1e-06
lowest_score = -1e30


def copy_for_each(x, axis):
    copies = jnp.broadcast_to(x, (lax.axis_size(axis), *x.shape))
    return lax.all_to_all(copies, axis, split_axis=0, concat_axis=0, tiled=True)


def of_everyone(x, axis):
    return copy_for_each(x, axis).sum(axis=0)


def one_axis_at_a_time(x, axes):
    far, near = axes
    return of_everyone(of_everyone(x, near), far)


def split_up(x, dim, length):
    dims = x.shape
    blocks = x.reshape(*dims[:dim], length, dims[dim] // length, *dims[dim + 1 :])
    return jnp.moveaxis(blocks, dim, 0)


def sum_at_owner(x, axis, dim):
    blocks = split_up(x, dim, lax.axis_size(axis))
    arrived = lax.all_to_all(blocks, axis, split_axis=0, concat_axis=0, tiled=True)
    return arrived.sum(axis=0)


def sum_in_two_steps(x, axes, dim):
    far, near = axes
    own = sum_at_owner(split_up(x, dim, lax.axis_size(far)), near, dim + 1)
    return jnp.sum(lax.all_to_all(own, far, 0, 0, tiled=True), axis=0)


def gathered_once(x, axis):
    leaves = jax.tree.leaves(x)
    order = sorted(range(len(leaves)), key=lambda k: -leaves[k].size)
    width = (1, *leaves[order[0]].shape)[-1]
    lines = [
        jnp.pad(leaves[k].reshape(-1), (0, -leaves[k].size % width)).reshape(-1, width)
        for k in order
    ]
    both, at, found = (lax.all_gather(jnp.concatenate(lines), axis), 0, {})
    for k, line in zip(order, lines):
        slab = both[:, at : at + len(line)].reshape(len(both), -1)
        found[k] = slab[:, : leaves[k].size].reshape(-1, *leaves[k].shape)
        at += len(line)
    numbers = iter(range(len(leaves)))
    return jax.tree.map(lambda _: found[next(numbers)], x)


def merged_by_axis(x, axes, combine):
    for axis in axes:
        pieces = gathered_once(
            jax.tree.map(
                lambda part, kind: part.astype(kind), x, (jnp.bfloat16, jnp.bfloat16, jnp.bfloat16)
            ),
            axis,
        )
        widened = [
            jax.tree.map(lambda part, own: part[k].astype(own.dtype), pieces, x)
            for k in range(lax.axis_size(axis))
        ]
        x = widened[0]
        for received in widened[1:]:
            x = combine(x, received)
    return x


def joined_along(blocks, dim):
    dims = list(blocks.shape[1:])
    dims[dim] *= blocks.shape[0]
    return jnp.moveaxis(blocks, 0, dim).reshape(dims)


def gather_directly(x, axis, dim):
    blocks = copy_for_each(x, axis)
    return joined_along(blocks, dim)


def gather_axes(x, axes, dim):
    far, near = axes
    blocks = copy_for_each(copy_for_each(x, far), near)
    return joined_along(blocks.swapaxes(0, 1).reshape(-1, *x.shape), dim)


def normalize(stream, gain_row):
    widened = stream.astype(jnp.float32)
    inv_rms = lax.rsqrt(jnp.mean(widened * widened, axis=1) + norm_eps)
    return (widened * inv_rms[:, None] * gain_row[None, :]).astype(jnp.bfloat16)


def unite_pieces(left_part, latter_piece):
    joint_top = jnp.maximum(left_part[0], latter_piece[0])
    left_scale = jnp.exp(left_part[0] - joint_top)
    right_scale = jnp.exp(latter_piece[0] - joint_top)
    return (
        joint_top,
        left_part[1] * left_scale + latter_piece[1] * right_scale,
        left_part[2] * left_scale[..., None] + latter_piece[2] * right_scale[..., None],
    )


def mamba_mix(normed, layer, params):
    (
        in_weight,
        conv_weight,
        conv_bias,
        conv_state,
        xproj_weight,
        dt_weight,
        dt_bias,
        a_log,
        skip_gain,
        ssm_state,
    ) = params
    channels = in_weight.shape[3]
    both_proj = jnp.dot(
        normed,
        in_weight[layer].reshape(in_weight.shape[1], 2 * channels),
        preferred_element_type=jnp.float32,
    ).astype(jnp.bfloat16)
    inputs = both_proj[:, :channels]
    gate_half = both_proj[:, channels:]
    window = jnp.concatenate([conv_state[layer], inputs[:, None, :]], axis=1)
    conv_sum = (
        jnp.sum(window.astype(jnp.float32) * conv_weight[layer][None], axis=1)
        + conv_bias[layer][None, :]
    )
    signal = lax.optimization_barrier(jax.nn.silu(conv_sum).astype(jnp.bfloat16))
    x_terms = jnp.dot(signal, xproj_weight[layer], preferred_element_type=jnp.float32)
    mapped_vectors = one_axis_at_a_time(x_terms, (("seq_0", "seq_1"), ("chan_0", "chan_1")))
    low_rank = dt_weight.shape[1]
    state_size = a_log.shape[1]
    dt_low = mapped_vectors[:, :low_rank].astype(jnp.bfloat16)
    b_in = mapped_vectors[:, low_rank : low_rank + state_size]
    c_out = mapped_vectors[:, low_rank + state_size :]
    dt_step = jax.nn.softplus(
        jnp.dot(dt_low, dt_weight[layer], preferred_element_type=jnp.float32)
        + dt_bias[layer][None, :]
    )
    widened = signal.astype(jnp.float32)
    decay_rate = jnp.exp(-dt_step[:, None, :] * jnp.exp(a_log[layer])[None])
    fresh_state = decay_rate * ssm_state[layer] + (dt_step * widened)[:, None, :] * b_in[:, :, None]
    readout = jnp.sum(fresh_state * c_out[:, :, None], axis=1) + skip_gain[layer][None, :] * widened
    gated_out = (readout * jax.nn.silu(gate_half.astype(jnp.float32))).astype(jnp.bfloat16)
    return (gated_out, fresh_state, window[:, 1:, :])


def mix_out(gated_out, out_weight, layer):
    weights_now = out_weight[layer]
    return sum_in_two_steps(
        lax.dot_general(
            weights_now, gated_out, (((0,), (1,)), ((), ())), preferred_element_type=jnp.float32
        ),
        (("seq_0", "seq_1"), ("chan_0", "chan_1")),
        0,
    ).T


def attend(normed, asker_lookup_matrix, kv_cache, lengths, page_table):
    requests = normed.shape[0]
    heads_kv = asker_lookup_matrix.shape[1]
    per_lens_width = kv_cache.shape[4]
    group_size = asker_lookup_matrix.shape[2] // per_lens_width - 2
    inv_sqrt = per_lens_width ** (-0.5)
    qkv_terms = jnp.einsum(
        "bd,dkc->bkc", normed, asker_lookup_matrix, preferred_element_type=jnp.float32
    )
    qkv_all = lax.optimization_barrier(of_everyone(qkv_terms, SEQ).astype(jnp.bfloat16))
    every_question = qkv_all[:, :, : group_size * per_lens_width].reshape(
        requests, heads_kv, group_size, per_lens_width
    )
    newest_pair = qkv_all[:, :, group_size * per_lens_width :].reshape(
        requests, heads_kv, 2, per_lens_width
    )
    pages_dev = kv_cache.shape[0]
    block_len = kv_cache.shape[1]
    slot_ids = lax.axis_index(SEQ) * pages_dev + jnp.arange(pages_dev, dtype=jnp.int32)
    matches = page_table[:, :, None] == slot_ids[None, None, :]
    belongs = jnp.any(matches, axis=1)
    in_use = jnp.any(belongs, axis=0)
    owner_req = jnp.sum(
        jnp.where(belongs, jnp.arange(requests, dtype=jnp.int32)[:, None], 0), axis=0
    )
    page_index = jnp.sum(
        jnp.where(matches, jnp.arange(page_table.shape[1], dtype=jnp.int32)[None, :, None], 0),
        axis=(0, 1),
    )
    filled = jnp.where(
        in_use, jnp.clip(lengths[owner_req] - page_index * block_len, 0, block_len), 0
    )
    live_count = jnp.sum(in_use.astype(jnp.int32))
    per_step = max(1, 512 // block_len)
    padded = -(-pages_dev // per_step) * per_step
    slot_order = jnp.argsort(
        jnp.where(in_use, 0, pages_dev) + jnp.arange(pages_dev, dtype=jnp.int32)
    )
    slot_order = jnp.concatenate([slot_order, jnp.zeros((padded - pages_dev,), jnp.int32)])
    live_lane = jnp.arange(padded, dtype=jnp.int32) < live_count
    lane_fill = jnp.where(live_lane, filled[slot_order], 0)
    lane_owner = owner_req[slot_order]

    def visit(index_step, carried):
        page_tops, page_sums, page_accs = carried
        first_lane = index_step * per_step
        slots_now = lax.dynamic_slice_in_dim(slot_order, first_lane, per_step)
        fills_now = lax.dynamic_slice_in_dim(lane_fill, first_lane, per_step)
        owners_now = lax.dynamic_slice_in_dim(lane_owner, first_lane, per_step)
        page_rows = kv_cache[slots_now]
        queries = every_question[owners_now]
        scores = (
            jnp.einsum(
                "pkgd,ptkd->pkgt", queries, page_rows[:, :, 0], preferred_element_type=jnp.float32
            )
            * inv_sqrt
        )
        visible = (
            jnp.arange(block_len, dtype=jnp.int32)[None, None, None, :]
            < fills_now[:, None, None, None]
        )
        scores = jnp.where(visible, scores, lowest_score)
        block_top = jnp.max(scores, axis=3)
        weight = jnp.where(visible, jnp.exp(scores - block_top[..., None]), 0.0)
        block_sum = jnp.sum(weight, axis=3)
        values = jnp.einsum(
            "pkgt,ptkd->pkgd",
            weight.astype(jnp.bfloat16),
            page_rows[:, :, 1],
            preferred_element_type=jnp.float32,
        )
        return (
            lax.dynamic_update_slice_in_dim(page_tops, block_top, first_lane, 0),
            lax.dynamic_update_slice_in_dim(page_sums, block_sum, first_lane, 0),
            lax.dynamic_update_slice_in_dim(page_accs, values, first_lane, 0),
        )

    start_state = (
        jnp.full((padded, heads_kv, group_size), lowest_score, jnp.float32),
        jnp.zeros((padded, heads_kv, group_size), jnp.float32),
        jnp.zeros((padded, heads_kv, group_size, per_lens_width), jnp.float32),
    )
    step_count = (live_count + per_step - 1) // per_step
    page_tops, page_sums, page_accs = lax.fori_loop(0, step_count, visit, start_state)
    selects = (lane_owner[None, :] == jnp.arange(requests, dtype=jnp.int32)[:, None]) & live_lane[
        None, :
    ]
    chosen = selects[:, :, None, None]
    local_top = jnp.max(jnp.where(chosen, page_tops[None], lowest_score), axis=1)
    factor = jnp.where(chosen, jnp.exp(page_tops[None] - local_top[:, None]), 0.0)
    local_sum = jnp.sum(factor * page_sums[None], axis=1)
    local_acc = jnp.einsum("bpkg,pkgd->bkgd", factor, page_accs)
    grand_top, weight_total, value_total = merged_by_axis(
        (local_top, local_sum, local_acc), SEQ, unite_pieces
    )
    fresh_score = (
        jnp.einsum(
            "ujqf,ujf->ujq",
            every_question,
            newest_pair[:, :, 0],
            preferred_element_type=jnp.float32,
        )
        * inv_sqrt
    )
    final_top = jnp.maximum(grand_top, fresh_score)
    carry_old = jnp.exp(grand_top - final_top)
    fresh_weight = jnp.exp(fresh_score - final_top)
    denominator = weight_total * carry_old + fresh_weight
    numerator = value_total * carry_old[..., None] + fresh_weight[..., None] * newest_pair[:, :, 1][
        :, :, None, :
    ].astype(jnp.float32)
    attended = (numerator / denominator[..., None]).astype(jnp.bfloat16)
    return (attended.reshape(requests, heads_kv, group_size * per_lens_width), newest_pair)


def shards(
    hidden,
    norm_gain,
    in_weight,
    conv_weight,
    conv_bias,
    conv_state,
    xproj_weight,
    dt_weight,
    dt_bias,
    a_log,
    skip_gain,
    ssm_state,
    out_weight,
    asker_lookup_matrix,
    o_weight,
    kv_cache,
    lengths,
    page_table,
):
    layer_params = (
        in_weight,
        conv_weight,
        conv_bias,
        conv_state,
        xproj_weight,
        dt_weight,
        dt_bias,
        a_log,
        skip_gain,
        ssm_state,
    )
    model_dim = hidden.shape[1]
    share_cols = model_dim // lax.axis_size(SEQ_CHAN)
    seq_index = lax.axis_index(SEQ)
    share_index = seq_index * lax.axis_size(CHAN) + lax.axis_index(CHAN)
    normed = normalize(hidden, norm_gain[0])
    gated_first, state_first, conv_first = mamba_mix(normed, 0, layer_params)
    own_cols = lax.dynamic_slice_in_dim(hidden, share_index * share_cols, share_cols, 1)
    stream_one = (own_cols.astype(jnp.float32) + mix_out(gated_first, out_weight, 0)).astype(
        jnp.bfloat16
    )
    widened = stream_one.astype(jnp.float32)
    squares = one_axis_at_a_time(
        jnp.sum(widened * widened, axis=1), (("seq_0", "seq_1"), ("chan_0", "chan_1"))
    )
    inv_rms = lax.rsqrt(squares / model_dim + norm_eps)
    gain_share = lax.dynamic_slice_in_dim(norm_gain[1], share_index * share_cols, share_cols, 0)
    attn_in = gather_directly(
        (widened * inv_rms[:, None] * gain_share[None, :]).astype(jnp.bfloat16), CHAN, 1
    )
    attended, newest_pair = attend(attn_in, asker_lookup_matrix, kv_cache, lengths, page_table)
    attn_share = sum_at_owner(
        jnp.einsum("khc,bkh->cb", o_weight, attended, preferred_element_type=jnp.float32), CHAN, 0
    )
    stream_two = (stream_one.astype(jnp.float32) + attn_share.T).astype(jnp.bfloat16)
    normed_two = normalize(
        gather_axes(stream_two, (("seq_0", "seq_1"), ("chan_0", "chan_1")), 1), norm_gain[2]
    )
    gated_two, state_two, conv_two = mamba_mix(normed_two, 1, layer_params)
    added = mix_out(gated_two, out_weight, 1)
    hidden_out = (stream_two.astype(jnp.float32) + added).astype(jnp.bfloat16)
    return (
        hidden_out,
        jnp.stack([state_first, state_two]),
        jnp.stack([conv_first, conv_two]),
        newest_pair,
    )


def solution(mesh):
    split = Mesh(mesh.devices.reshape(8, 4, 4, 2), ("seq_0", "seq_1", "chan_0", "chan_1"))
    placed = (
        P(),
        P(),
        P(None, None, None, SEQ_CHAN),
        P(None, None, SEQ_CHAN),
        P(None, SEQ_CHAN),
        P(None, None, None, SEQ_CHAN),
        P(None, SEQ_CHAN, None),
        P(None, None, SEQ_CHAN),
        P(None, SEQ_CHAN),
        P(None, None, SEQ_CHAN),
        P(None, SEQ_CHAN),
        P(None, None, None, SEQ_CHAN),
        P(None, SEQ_CHAN, None),
        P(SEQ, CHAN, None),
        P(CHAN, None, SEQ),
        P(SEQ, None, None, CHAN, None),
        P(),
        P(),
    )
    return jax.shard_map(
        shards,
        mesh=split,
        in_specs=placed,
        out_specs=(
            P(None, SEQ_CHAN),
            P(None, None, None, SEQ_CHAN),
            P(None, None, None, SEQ_CHAN),
            P(None, CHAN, None, None),
        ),
        check_vma=False,
    )
```

profile of v0, /device:TPU:1, one launch (start us, length us, event | category | flops | bytes accessed | tf_op | source)
XLA Modules:
  0.0 321.6 jit_solution(6034430674015665886)
XLA Ops:
  0.6 2.4 slice_reduce_fusion
  3.1 2.7 fusion.153
  9.2 11.3 %all_to_all.77 = f32[8,8,544]{2,1,0:T(8,128)S(1)} all-to-all(f32[8,8,544]{2,1,0:T(8,128)S(1)} %broadcast_in_dim.200), channel_id=1, replica_groups=mesh['seq_0'=8,'seq_1'=4,'chan_0'=4,'chan_1'=2] {'chan_0','chan_1'}, dimensions={0} | all-to-all | bytes 278528 | tf_op jit(solution)/shard_map/all_to_all | solution.py:18
  20.5 0.9 broadcast_in_dim.201
  21.4 11.0 %all-to-all-start.1 = ((f32[32,8,544]{2,1,0:T(8,128)}), f32[32,8,544]{2,1,0:T(8,128)S(1)}, u32[]{:S(2)}, u32[]{:S(2)}) async-start(f32[32,8,544]{2,1,0:T(8,128)} %broadcast_in_dim.201), calls=%async_computation.1 | async-start | bytes 1310720 | tf_op jit(solution)/shard_map/all_to_all | solution.py:18
  34.3 16.7 %all-to-all-done.1 = f32[32,8,544]{2,1,0:T(8,128)S(1)} async-done(((f32[32,8,544]{2,1,0:T(8,128)}), f32[32,8,544]{2,1,0:T(8,128)S(1)}, u32[]{:S(2)}, u32[]{:S(2)}) %all-to-all-start.1) | async-done | bytes 557088 | tf_op jit(solution)/shard_map/all_to_all | solution.py:18
  52.4 1.0 fusion.159
  53.4 0.9 fusion.37
  54.4 1.6 convolution_bitcast_fusion.2
  56.0 1.3 reshape_reshape.8
  57.3 2.5 copy.141
  59.8 1.7 reshape.1480
  61.5 11.6 %all_to_all.78 = f32[8,1,8192]{2,1,0:T(1,128)S(1)} all-to-all(f32[8,1,8192]{2,1,0:T(1,128)S(1)} %reshape.1480), channel_id=1, replica_groups=mesh['seq_0'=8,'seq_1'=4,'chan_0'=4,'chan_1'=2] {'chan_0','chan_1'}, dimensions={0} | all-to-all | bytes 524288 | tf_op jit(solution)/shard_map/all_to_all | solution.py:38
  73.5 1.2 reduce.48
  74.7 1.3 reshape.1481
  76.1 1.3 bitcast_reduce_fusion.1
  78.2 4.7 %all-to-all-start.3 = ((f32[32,1,256]{2,1,0:T(1,128)}), f32[32,1,256]{2,1,0:T(1,128)S(1)}, u32[]{:S(2)}, u32[]{:S(2)}) async-start(f32[32,1,256]{2,1,0:T(1,128)} %reshape.1482), calls=%async_computation.3 | async-start | bytes 65536 | tf_op jit(solution)/shard_map/all_to_all | solution.py:45
  82.9 8.7 %all-to-all-done.3 = f32[32,1,256]{2,1,0:T(1,128)S(1)} async-done(((f32[32,1,256]{2,1,0:T(1,128)}), f32[32,1,256]{2,1,0:T(1,128)S(1)}, u32[]{:S(2)}, u32[]{:S(2)}) %all-to-all-start.3) | async-done | bytes 32800 | tf_op jit(solution)/shard_map/all_to_all | solution.py:45
  92.7 9.4 %all_to_all.79 = f32[8,1,8]{2,1,0:T(1,128)S(1)} all-to-all(f32[8,1,8]{2,1,0:T(1,128)S(1)} %broadcast_in_dim.214), channel_id=1, replica_groups=mesh['seq_0'=8,'seq_1'=4,'chan_0'=4,'chan_1'=2] {'chan_0','chan_1'}, dimensions={0} | all-to-all | bytes 512 | tf_op jit(solution)/shard_map/all_to_all | solution.py:18
  102.7 3.8 %all-to-all-start.5 = ((f32[32,1,8]{2,1,0:T(1,128)}), f32[32,1,8]{2,1,0:T(1,128)S(1)}, u32[]{:S(2)}, u32[]{:S(2)}) async-start(f32[32,1,8]{2,1,0:T(1,128)} %broadcast_in_dim.215), calls=%async_computation.5 | async-start | bytes 32768 | tf_op jit(solution)/shard_map/all_to_all | solution.py:18
  107.2 7.9 %all-to-all-done.5 = f32[32,1,8]{2,1,0:T(1,128)S(1)} async-done(((f32[32,1,8]{2,1,0:T(1,128)}), f32[32,1,8]{2,1,0:T(1,128)S(1)}, u32[]{:S(2)}, u32[]{:S(2)}) %all-to-all-start.5) | async-done | bytes 1056 | tf_op jit(solution)/shard_map/all_to_all | solution.py:18
  115.4 8.6 %all_to_all.80 = bf16[8,2,128]{2,1,0:T(2,128)(2,1)S(1)} all-to-all(bf16[8,2,128]{2,1,0:T(2,128)(2,1)S(1)} %reshape.1484), channel_id=1, replica_groups=mesh['seq_0'=8,'seq_1'=4,'chan_0'=4,'chan_1'=2] {'chan_0','chan_1'}, dimensions={0} | all-to-all | bytes 8192 | tf_op jit(solution)/shard_map/all_to_all | solution.py:18
  124.4 1.2 broadcast_in_dim.217
  125.6 4.7 %all-to-all-start.7 = ((f32[32,8,1,1280]{3,1,2,0:T(8,128)}), f32[32,8,1,1280]{3,1,2,0:T(8,128)}, u32[]{:S(2)}, u32[]{:S(2)}) async-start(f32[32,8,1,1280]{3,1,2,0:T(8,128)} %broadcast_in_dim.217), calls=%async_computation.7 | async-start | bytes 2621440 | tf_op jit(solution)/shard_map/all_to_all | solution.py:18
  132.8 1.0 sort.17
  135.1 2.4 copy.91
  137.5 1.0 copy.98
  139.9 22.7 %all-to-all-done.7 = f32[32,8,1,1280]{3,1,2,0:T(8,128)} async-done(((f32[32,8,1,1280]{3,1,2,0:T(8,128)}), f32[32,8,1,1280]{3,1,2,0:T(8,128)}, u32[]{:S(2)}, u32[]{:S(2)}) %all-to-all-start.7) | async-done | bytes 1310752 | tf_op jit(solution)/shard_map/all_to_all | solution.py:18
  162.6 1.4 reduce_sum.234
  165.1 28.2 %all-gather.2 = bf16[8,66,128]{2,1,0:T(8,128)(2,1)S(1)} all-gather(bf16[1,66,128]{2,1,0:T(8,128)(2,1)S(1)} %maximum_bitcast_fusion), channel_id=2, replica_groups=mesh['seq_0'=8,'seq_1'=4,'chan_0'=4,'chan_1'=2] {'seq_0'}, dimensions={0}, use_global_device_ids=true | all-gather | bytes 152064 | tf_op jit(solution)/shard_map/all_gather | solution.py:56
  193.7 11.6 %all-gather.3 = bf16[4,66,128]{2,1,0:T(8,128)(2,1)S(1)} all-gather(bf16[1,66,128]{2,1,0:T(8,128)(2,1)S(1)} %maximum_bitcast_fusion.1), channel_id=3, replica_groups=mesh['seq_0'=8,'seq_1'=4,'chan_0'=4,'chan_1'=2] {'seq_1'}, dimensions={0}, use_global_device_ids=true | all-gather | bytes 84480 | tf_op jit(solution)/shard_map/all_gather | solution.py:56
  206.3 1.5 fusion.160
  207.8 17.5 %all_to_all.81 = f32[8,1,256]{2,1,0:T(1,128)S(1)} all-to-all(f32[8,1,256]{2,1,0:T(1,128)S(1)} %reshape.1486), channel_id=1, replica_groups=mesh['seq_0'=8,'seq_1'=4,'chan_0'=4,'chan_1'=2] {'chan_0','chan_1'}, dimensions={0} | all-to-all | bytes 16384 | tf_op jit(solution)/shard_map/all_to_all | solution.py:38
  226.7 14.5 %all_to_all.82 = bf16[32,2,128]{2,1,0:T(2,128)(2,1)S(1)} all-to-all(bf16[32,2,128]{2,1,0:T(2,128)(2,1)S(1)} %reshape.1488), channel_id=1, replica_groups=mesh['seq_0'=8,'seq_1'=4,'chan_0'=4,'chan_1'=2] {'seq_0','seq_1'}, dimensions={0} | all-to-all | bytes 32768 | tf_op jit(solution)/shard_map/all_to_all | solution.py:18
  241.4 1.2 reshape.1490
  242.5 5.4 %all-to-all-start.10 = ((bf16[8,2,4096]{2,1,0:T(2,128)(2,1)}), bf16[8,2,4096]{2,1,0:T(2,128)(2,1)S(1)}, u32[]{:S(2)}, u32[]{:S(2)}) async-start(bf16[8,2,4096]{2,1,0:T(2,128)(2,1)} %reshape.1490), calls=%async_computation.10 | async-start | bytes 262144 | tf_op jit(solution)/shard_map/all_to_all | solution.py:18
  248.8 4.4 %all-to-all-done.10 = bf16[8,2,4096]{2,1,0:T(2,128)(2,1)S(1)} async-done(((bf16[8,2,4096]{2,1,0:T(2,128)(2,1)}), bf16[8,2,4096]{2,1,0:T(2,128)(2,1)S(1)}, u32[]{:S(2)}, u32[]{:S(2)}) %all-to-all-start.10) | async-done | bytes 131104 | tf_op jit(solution)/shard_map/all_to_all | solution.py:18
  256.0 8.8 %all_to_all.83 = f32[8,8,544]{2,1,0:T(8,128)S(1)} all-to-all(f32[8,8,544]{2,1,0:T(8,128)S(1)} %broadcast_in_dim.227), channel_id=1, replica_groups=mesh['seq_0'=8,'seq_1'=4,'chan_0'=4,'chan_1'=2] {'chan_0','chan_1'}, dimensions={0} | all-to-all | bytes 278528 | tf_op jit(solution)/shard_map/all_to_all | solution.py:18
  264.8 0.9 broadcast_in_dim.228
  265.7 3.9 %all-to-all-start.12 = ((f32[32,8,544]{2,1,0:T(8,128)}), f32[32,8,544]{2,1,0:T(8,128)S(1)}, u32[]{:S(2)}, u32[]{:S(2)}) async-start(f32[32,8,544]{2,1,0:T(8,128)} %broadcast_in_dim.228), calls=%async_computation.12 | async-start | bytes 1310720 | tf_op jit(solution)/shard_map/all_to_all | solution.py:18
  270.9 17.7 %all-to-all-done.12 = f32[32,8,544]{2,1,0:T(8,128)S(1)} async-done(((f32[32,8,544]{2,1,0:T(8,128)}), f32[32,8,544]{2,1,0:T(8,128)S(1)}, u32[]{:S(2)}, u32[]{:S(2)}) %all-to-all-start.12) | async-done | bytes 557088 | tf_op jit(solution)/shard_map/all_to_all | solution.py:18
  289.0 1.5 convolution_bitcast_fusion.1
  291.1 1.1 reshape.1492
  292.3 5.6 %all-to-all-start.13 = ((f32[8,1,8192]{2,1,0:T(1,128)}), f32[8,1,8192]{2,1,0:T(1,128)S(1)}, u32[]{:S(2)}, u32[]{:S(2)}) async-start(f32[8,1,8192]{2,1,0:T(1,128)} %reshape.1492), calls=%async_computation.13 | async-start | bytes 524288 | tf_op jit(solution)/shard_map/all_to_all | solution.py:38
  298.0 6.4 %all-to-all-done.13 = f32[8,1,8192]{2,1,0:T(1,128)S(1)} async-done(((f32[8,1,8192]{2,1,0:T(1,128)}), f32[8,1,8192]{2,1,0:T(1,128)S(1)}, u32[]{:S(2)}, u32[]{:S(2)}) %all-to-all-start.13) | async-done | bytes 262176 | tf_op jit(solution)/shard_map/all_to_all | solution.py:38
  304.3 1.2 reduce.51
  306.8 4.7 %all-to-all-start.14 = ((f32[32,1,256]{2,1,0:T(1,128)}), f32[32,1,256]{2,1,0:T(1,128)S(1)}, u32[]{:S(2)}, u32[]{:S(2)}) async-start(f32[32,1,256]{2,1,0:T(1,128)} %reshape.1494), calls=%async_computation.14 | async-start | bytes 65536 | tf_op jit(solution)/shard_map/all_to_all | solution.py:45
  312.1 8.1 %all-to-all-done.14 = f32[32,1,256]{2,1,0:T(1,128)S(1)} async-done(((f32[32,1,256]{2,1,0:T(1,128)}), f32[32,1,256]{2,1,0:T(1,128)S(1)}, u32[]{:S(2)}, u32[]{:S(2)}) %all-to-all-start.14) | async-done | bytes 32800 | tf_op jit(solution)/shard_map/all_to_all | solution.py:45
  (213 shorter events, 28.3 us)
Async XLA Ops:
  0.6 123.6 %copy-start = (bf16[256,1,1280]{2,0,1:T(8,128)(2,1)S(1)}, bf16[256,1,1280]{2,0,1:T(8,128)(2,1)}, u32[]{:S(2)}) copy-start(bf16[256,1,1280]{2,0,1:T(8,128)(2,1)} %param.33) | copy-start | bytes 1966084
  3.1 2.7 copy-start.2
  5.8 1.0 copy-start.26
  5.8 1.6 copy-start.28
  5.8 2.1 copy-start.32
  5.8 3.3 %copy-start.5 = (bf16[2,64,544]{2,1,0:T(8,128)(2,1)S(1)}, bf16[2,64,544]{2,1,0:T(8,128)(2,1)}, u32[]{:S(2)}) copy-start(bf16[2,64,544]{2,1,0:T(8,128)(2,1)} %param.26) | copy-start | bytes 417796
  6.0 26.5 %copy-start.33 = (f32[2,64]{1,0:T(2,128)S(1)}, f32[2,64]{1,0:T(2,128)}, u32[]{:S(2)}) copy-start(f32[2,64]{1,0:T(2,128)} %param.28) | copy-start | bytes 1540
  6.0 27.0 %copy-start.34 = (f32[2,64]{1,0:T(2,128)S(1)}, f32[2,64]{1,0:T(2,128)}, u32[]{:S(2)}) copy-start(f32[2,64]{1,0:T(2,128)} %param.30) | copy-start | bytes 1540
  6.7 2.5 copy-start.24
  6.7 1.7 copy-start.20
  7.3 1.1 copy-start.9
  8.5 0.6 copy-start.19
  21.4 29.5 %all-to-all-start.1 = ((f32[32,8,544]{2,1,0:T(8,128)}), f32[32,8,544]{2,1,0:T(8,128)S(1)}, u32[]{:S(2)}, u32[]{:S(2)}) async-start(f32[32,8,544]{2,1,0:T(8,128)} %broadcast_in_dim.201), calls=%async_computation.1 | async-start | bytes 1310720 | tf_op jit(solution)/shard_map/all_to_all | solution.py:18
  52.4 2.0 copy-start.15
  53.4 1.0 copy-start.11
  53.4 1.0 copy-start.13
  78.2 13.5 %all-to-all-start.3 = ((f32[32,1,256]{2,1,0:T(1,128)}), f32[32,1,256]{2,1,0:T(1,128)S(1)}, u32[]{:S(2)}, u32[]{:S(2)}) async-start(f32[32,1,256]{2,1,0:T(1,128)} %reshape.1482), calls=%async_computation.3 | async-start | bytes 65536 | tf_op jit(solution)/shard_map/all_to_all | solution.py:45
  102.7 12.5 %all-to-all-start.5 = ((f32[32,1,8]{2,1,0:T(1,128)}), f32[32,1,8]{2,1,0:T(1,128)S(1)}, u32[]{:S(2)}, u32[]{:S(2)}) async-start(f32[32,1,8]{2,1,0:T(1,128)} %broadcast_in_dim.215), calls=%async_computation.5 | async-start | bytes 32768 | tf_op jit(solution)/shard_map/all_to_all | solution.py:18
  124.4 5.9 %copy-start.25 = (s32[8,32]{1,0:T(8,128)S(1)}, s32[8,32]{1,0:T(8,128)}, u32[]{:S(2)}) copy-start(s32[8,32]{1,0:T(8,128)} %param.37) | copy-start | bytes 3076
  124.4 6.3 %copy-start.1 = (s32[8]{0:T(128)S(1)}, s32[8]{0:T(128)}, u32[]{:S(2)}) copy-start(s32[8]{0:T(128)} %param.36) | copy-start | bytes 100
  125.6 37.0 %all-to-all-start.7 = ((f32[32,8,1,1280]{3,1,2,0:T(8,128)}), f32[32,8,1,1280]{3,1,2,0:T(8,128)}, u32[]{:S(2)}, u32[]{:S(2)}) async-start(f32[32,8,1,1280]{3,1,2,0:T(8,128)} %broadcast_in_dim.217), calls=%async_computation.7 | async-start | bytes 2621440 | tf_op jit(solution)/shard_map/all_to_all | solution.py:18
  130.3 7.3 %copy-start.4 = (bf16[1,1024,256]{2,1,0:T(8,128)(2,1)S(1)}, bf16[1,1024,256]{2,1,0:T(8,128)(2,1)}, u32[]{:S(2)}) copy-start(bf16[1,1024,256]{2,1,0:T(8,128)(2,1)} %param.34) | copy-start | bytes 1572868
  164.0 0.6 copy-start.17
  226.0 0.5 copy-start.22
  242.5 10.7 %all-to-all-start.10 = ((bf16[8,2,4096]{2,1,0:T(2,128)(2,1)}), bf16[8,2,4096]{2,1,0:T(2,128)(2,1)S(1)}, u32[]{:S(2)}, u32[]{:S(2)}) async-start(bf16[8,2,4096]{2,1,0:T(2,128)(2,1)} %reshape.1490), calls=%async_computation.10 | async-start | bytes 262144 | tf_op jit(solution)/shard_map/all_to_all | solution.py:18
  254.3 1.4 copy-start.8
  254.3 1.4 copy-start.27
  254.3 1.4 copy-start.31
  254.9 0.9 copy-start.6
  255.0 14.7 %copy-start.10 = (bf16[8,3,64]{2,0,1:T(8,128)(2,1)S(1)}, bf16[8,3,64]{2,0,1:T(8,128)(2,1)}, u32[]{:S(2)}) copy-start(bf16[8,3,64]{2,0,1:T(8,128)(2,1)} %copy-done.9) | copy-start | bytes 9220
  255.0 14.7 %copy-start.21 = (bf16[8,1,64]{2,0,1:T(8,128)(2,1)S(1)}, bf16[8,1,64]{2,0,1:T(8,128)(2,1)}, u32[]{:S(2)}) copy-start(bf16[8,1,64]{2,0,1:T(8,128)(2,1)} %copy-done.20) | copy-start | bytes 3076
  255.0 14.7 %copy-start.18 = (bf16[8,1,2,128]{3,0,2,1:T(8,128)(2,1)S(1)}, bf16[8,1,2,128]{3,0,2,1:T(8,128)(2,1)}, u32[]{:S(2)}) copy-start(bf16[8,1,2,128]{3,0,2,1:T(8,128)(2,1)} %copy-done.17) | copy-start | bytes 12292
  255.6 33.1 %copy-start.7 = (bf16[2,512,64]{1,2,0:T(8,128)(2,1)S(1)}, bf16[2,512,64]{1,2,0:T(8,128)(2,1)}, u32[]{:S(2)}) copy-start(bf16[2,512,64]{1,2,0:T(8,128)(2,1)} %param.27) | copy-start | bytes 393220
  255.6 33.1 %copy-start.30 = (f32[64]{0:T(128)S(1)}, f32[64]{0:T(128)}, u32[]{:S(2)}) copy-start(f32[64]{0:T(128)} %get-tuple-element.230) | copy-start | bytes 772
  255.6 33.2 %copy-start.3 = (f32[2,8,16,64]{3,2,1,0:T(8,128)S(1)}, f32[2,8,16,64]{3,2,1,0:T(8,128)}, u32[]{:S(2)}) copy-start(f32[2,8,16,64]{3,2,1,0:T(8,128)} %param.31) | copy-start | bytes 196612
  255.7 33.3 %copy-start.29 = (f32[64]{0:T(128)S(1)}, f32[64]{0:T(128)}, u32[]{:S(2)}) copy-start(f32[64]{0:T(128)} %get-tuple-element.228) | copy-start | bytes 772
  265.7 22.9 %all-to-all-start.12 = ((f32[32,8,544]{2,1,0:T(8,128)}), f32[32,8,544]{2,1,0:T(8,128)S(1)}, u32[]{:S(2)}, u32[]{:S(2)}) async-start(f32[32,8,544]{2,1,0:T(8,128)} %broadcast_in_dim.228), calls=%async_computation.12 | async-start | bytes 1310720 | tf_op jit(solution)/shard_map/all_to_all | solution.py:18
  290.9 7.0 %copy-start.12 = (f32[8,64]{1,0:T(8,128)S(1)}, f32[8,64]{1,0:T(8,128)}, u32[]{:S(2)}) copy-start(f32[8,64]{1,0:T(8,128)} %copy-done.11) | copy-start | bytes 6148
  290.9 6.9 %copy-start.14 = (f32[8,64]{1,0:T(8,128)S(1)}, f32[8,64]{1,0:T(8,128)}, u32[]{:S(2)}) copy-start(f32[8,64]{1,0:T(8,128)} %copy-done.13) | copy-start | bytes 6148
  290.9 6.9 %copy-start.16 = (f32[8,16]{1,0:T(8,128)S(1)}, f32[8,16]{1,0:T(8,128)}, u32[]{:S(2)}) copy-start(f32[8,16]{1,0:T(8,128)} %copy-done.15) | copy-start | bytes 1540
  292.3 12.1 %all-to-all-start.13 = ((f32[8,1,8192]{2,1,0:T(1,128)}), f32[8,1,8192]{2,1,0:T(1,128)S(1)}, u32[]{:S(2)}, u32[]{:S(2)}) async-start(f32[8,1,8192]{2,1,0:T(1,128)} %reshape.1492), calls=%async_computation.13 | async-start | bytes 524288 | tf_op jit(solution)/shard_map/all_to_all | solution.py:38
  298.0 23.0 %copy-start.23 = (bf16[8,32]{1,0:T(8,128)(2,1)S(1)}, bf16[8,32]{1,0:T(8,128)(2,1)}, u32[]{:S(2)}) copy-start(bf16[8,32]{1,0:T(8,128)(2,1)} %copy-done.22) | copy-start | bytes 1540
  306.8 13.4 %all-to-all-start.14 = ((f32[32,1,256]{2,1,0:T(1,128)}), f32[32,1,256]{2,1,0:T(1,128)S(1)}, u32[]{:S(2)}, u32[]{:S(2)}) async-start(f32[32,1,256]{2,1,0:T(1,128)} %reshape.1494), calls=%async_computation.14 | async-start | bytes 65536 | tf_op jit(solution)/shard_map/all_to_all | solution.py:45
where the time goes:
time: 324 us; the launch traced here: 322 us
  blocking collectives  121 us (37%)
  waiting for transfers between devices  92.6 us (29%)
  starting transfers between devices  43.8 us (14%)
  local copies, waits for them, and re-layouts  37.3 us (12%)
  other arithmetic  16.3 us (5%)
  matrix products  7.84 us (2%)
    all_to_all x5, waiting for transfers between devices, copy_for_each(): return lax.all_to_all(copies, axis, split_axis=0, concat_axis=0, tiled=True)  69.4 us
    all_to_all x5, blocking collectives, copy_for_each(): return lax.all_to_all(copies, axis, split_axis=0, concat_axis=0, tiled=True)  52.7 us
    all_gather x2, blocking collectives, gathered_once(): both, at, found = (lax.all_gather(jnp.concatenate(lines), axis), 0, {})  39.8 us
    all_to_all x2, blocking collectives, sum_at_owner(): lax.all_to_all(blocks, axis, split_axis=0, concat_axis=0, tiled=True)  29 us
    all_to_all x5, starting transfers between devices, copy_for_each(): return lax.all_to_all(copies, axis, split_axis=0, concat_axis=0, tiled=True)  28.9 us
    all_to_all x2, waiting for transfers between devices, sum_in_two_steps(): return jnp.sum(lax.all_to_all(own, far, 0, 0, tiled=True), axis=0)  16.8 us
    unnamed x92, local copies, waits for them, and re-layouts  11.3 us
    all_to_all x2, starting transfers between devices, sum_in_two_steps(): return jnp.sum(lax.all_to_all(own, far, 0, 0, tiled=True), axis=0)  9.38 us
  transfers between devices with their start and end apart: 8, of which 8 were waited for; matrix products, arithmetic and copies ran while one was open for 4% of the time, Pallas kernels for 0%

commit v1 on v0

v1 whole, which is shorter than its diff:
```python
import jax
import jax.numpy as jnp
from jax import lax
from jax.sharding import Mesh
from jax.sharding import PartitionSpec as P

ALL = ("z", "x", "y", "core")
SEQ = ("z", "x")
CHAN = ("y", "core")
PLANE = ("x", "y")
LINE = ("z", "core")
WIRE = jnp.bfloat16

norm_eps = 1e-06
lowest_score = -1e30


def copy_for_each(x, axes):
    copies = jnp.broadcast_to(x, (lax.axis_size(axes), *x.shape))
    return lax.all_to_all(copies, axes, split_axis=0, concat_axis=0, tiled=True)


def of_everyone(x, axes):
    return jnp.sum(copy_for_each(x.astype(WIRE), axes).astype(jnp.float32), axis=0)


def normalize(stream, gain_row):
    widened = stream.astype(jnp.float32)
    inv_rms = lax.rsqrt(jnp.mean(widened * widened, axis=1) + norm_eps)
    return (widened * inv_rms[:, None] * gain_row[None, :]).astype(jnp.bfloat16)


def two_parts(x):
    high = x.astype(WIRE).astype(jnp.float32)
    return high, (x - high).astype(WIRE).astype(jnp.float32)


def mamba_mix(normed, layer, params):
    (
        in_weight,
        conv_weight,
        conv_bias,
        conv_state,
        xproj_weight,
        dt_weight,
        dt_bias,
        a_log,
        skip_gain,
        ssm_state,
    ) = params
    channels = in_weight.shape[3]
    both_proj = jnp.dot(
        normed,
        in_weight[layer].reshape(in_weight.shape[1], 2 * channels),
        preferred_element_type=jnp.float32,
    ).astype(jnp.bfloat16)
    inputs = both_proj[:, :channels]
    gate_half = both_proj[:, channels:]
    window = jnp.concatenate([conv_state[layer], inputs[:, None, :]], axis=1)
    conv_sum = (
        jnp.sum(window.astype(jnp.float32) * conv_weight[layer][None], axis=1)
        + conv_bias[layer][None, :]
    )
    signal = lax.optimization_barrier(jax.nn.silu(conv_sum).astype(jnp.bfloat16))
    x_terms = jnp.dot(signal, xproj_weight[layer], preferred_element_type=jnp.float32)
    mapped_vectors = of_everyone(of_everyone(x_terms, PLANE), LINE)
    low_rank = dt_weight.shape[1]
    state_size = a_log.shape[1]
    dt_low = mapped_vectors[:, :low_rank].astype(jnp.bfloat16)
    b_in = mapped_vectors[:, low_rank : low_rank + state_size]
    c_out = mapped_vectors[:, low_rank + state_size :]
    dt_step = jax.nn.softplus(
        jnp.dot(dt_low, dt_weight[layer], preferred_element_type=jnp.float32)
        + dt_bias[layer][None, :]
    )
    widened = signal.astype(jnp.float32)
    decay_rate = jnp.exp(-dt_step[:, None, :] * jnp.exp(a_log[layer])[None])
    fresh_state = decay_rate * ssm_state[layer] + (dt_step * widened)[:, None, :] * b_in[:, :, None]
    readout = jnp.sum(fresh_state * c_out[:, :, None], axis=1) + skip_gain[layer][None, :] * widened
    gated_out = (readout * jax.nn.silu(gate_half.astype(jnp.float32))).astype(jnp.bfloat16)
    return (gated_out, fresh_state, window[:, 1:, :])


def mix_out(gated_out, out_weight, layer):
    partial = jnp.dot(gated_out, out_weight[layer], preferred_element_type=jnp.float32)
    rows, dim = partial.shape
    parts = lax.axis_size(SEQ)
    blocks = partial.astype(WIRE).reshape(rows, parts, dim // parts).swapaxes(0, 1)
    arrived = lax.all_to_all(blocks, SEQ, split_axis=0, concat_axis=0, tiled=True)
    return of_everyone(jnp.sum(arrived.astype(jnp.float32), axis=0), CHAN)


def local_attention(questions, kv_cache, lengths, page_table, inv_sqrt):
    requests, group_size, width = questions.shape
    pages_dev, block_len = kv_cache.shape[:2]
    slot_ids = lax.axis_index(SEQ) * pages_dev + jnp.arange(pages_dev, dtype=jnp.int32)
    matches = page_table[:, :, None] == slot_ids[None, None, :]
    first_token = jnp.arange(page_table.shape[1], dtype=jnp.int32) * block_len
    left = jnp.clip(lengths[:, None] - first_token[None, :], 0, block_len)
    filled = jnp.sum(jnp.where(matches, left[:, :, None], 0), axis=1)
    visible = (
        jnp.arange(block_len, dtype=jnp.int32)[None, None, :] < filled[:, :, None]
    ).reshape(requests, 1, pages_dev * block_len)
    keys = kv_cache[:, :, 0, 0].reshape(pages_dev * block_len, width)
    values = kv_cache[:, :, 1, 0].reshape(pages_dev * block_len, width)
    scores = (
        jnp.dot(
            questions.reshape(requests * group_size, width),
            keys.T,
            preferred_element_type=jnp.float32,
        )
        * inv_sqrt
    ).reshape(requests, group_size, pages_dev * block_len)
    scores = jnp.where(visible, scores, lowest_score)
    high, low = two_parts(jnp.max(scores, axis=2))
    weight = jnp.where(visible, jnp.exp(scores - (high + low)[..., None]), 0.0)
    total = jnp.sum(weight, axis=2)
    mixed = jnp.dot(
        weight.astype(jnp.bfloat16).reshape(requests * group_size, pages_dev * block_len),
        values,
        preferred_element_type=jnp.float32,
    )
    return high, low, total, mixed


def attend(stream_one, gain_block, asker_lookup_matrix, kv_cache, lengths, page_table, model_dim):
    requests = stream_one.shape[0]
    width = kv_cache.shape[4]
    group_size = asker_lookup_matrix.shape[2] // width - 2
    entries = asker_lookup_matrix.shape[2]
    rows = requests * group_size
    inv_sqrt = width ** (-0.5)
    widened = stream_one.astype(jnp.float32)
    high, low = two_parts(jnp.sum(widened * widened, axis=1))
    scaled = (widened * gain_block[None, :]).astype(jnp.bfloat16)
    terms = jnp.dot(scaled, asker_lookup_matrix[:, 0, :], preferred_element_type=jnp.float32)
    summed = of_everyone(
        jnp.concatenate([terms, high[:, None], low[:, None], jnp.zeros((requests, 126))], axis=1),
        SEQ,
    )
    inv_rms = lax.rsqrt((summed[:, entries] + summed[:, entries + 1]) / model_dim + norm_eps)
    qkv = (summed[:, :entries] * inv_rms[:, None]).astype(jnp.bfloat16)
    questions = qkv[:, : group_size * width].reshape(requests, group_size, width)
    fresh_key = qkv[:, group_size * width : (group_size + 1) * width]
    fresh_value = qkv[:, (group_size + 1) * width :]
    newest_pair = jnp.stack([fresh_key, fresh_value], axis=1)[:, None]
    high, low, total, mixed = local_attention(questions, kv_cache, lengths, page_table, inv_sqrt)
    notes = jnp.stack([high.reshape(rows), low.reshape(rows), total.reshape(rows)])
    notes = jnp.pad(notes, ((0, 5), (0, width - rows)))
    packed = jnp.concatenate([mixed, notes], axis=0).astype(WIRE)
    arrived = copy_for_each(packed, SEQ).astype(jnp.float32)
    tops = (arrived[:, rows, :rows] + arrived[:, rows + 1, :rows]).reshape(
        -1, requests, group_size
    )
    totals = arrived[:, rows + 2, :rows].reshape(-1, requests, group_size)
    mixes = arrived[:, :rows].reshape(-1, requests, group_size, width)
    fresh_score = (
        jnp.sum(
            questions.astype(jnp.float32) * fresh_key[:, None, :].astype(jnp.float32), axis=2
        )
        * inv_sqrt
    )
    final_top = jnp.maximum(jnp.max(tops, axis=0), fresh_score)
    scale = jnp.exp(tops - final_top[None])
    fresh_weight = jnp.exp(fresh_score - final_top)
    denominator = jnp.sum(scale * totals, axis=0) + fresh_weight
    numerator = (
        jnp.sum(scale[..., None] * mixes, axis=0)
        + fresh_weight[..., None] * fresh_value[:, None, :].astype(jnp.float32)
    )
    attended = (numerator / denominator[..., None]).astype(jnp.bfloat16)
    return attended.reshape(requests, group_size * width), newest_pair


def shards(
    hidden,
    norm_gain,
    in_weight,
    conv_weight,
    conv_bias,
    conv_state,
    xproj_weight,
    dt_weight,
    dt_bias,
    a_log,
    skip_gain,
    ssm_state,
    out_weight,
    asker_lookup_matrix,
    o_weight,
    kv_cache,
    lengths,
    page_table,
):
    layer_params = (
        in_weight,
        conv_weight,
        conv_bias,
        conv_state,
        xproj_weight,
        dt_weight,
        dt_bias,
        a_log,
        skip_gain,
        ssm_state,
    )
    requests, model_dim = hidden.shape
    block_cols = model_dim // lax.axis_size(SEQ)
    share_cols = block_cols // lax.axis_size(CHAN)
    first_col = lax.axis_index(SEQ) * block_cols
    normed = normalize(hidden, norm_gain[0])
    gated_first, state_first, conv_first = mamba_mix(normed, 0, layer_params)
    own_block = lax.dynamic_slice_in_dim(hidden, first_col, block_cols, 1)
    gain_block = lax.dynamic_slice_in_dim(norm_gain[1], first_col, block_cols, 0)
    stream_one = (own_block.astype(jnp.float32) + mix_out(gated_first, out_weight, 0)).astype(
        jnp.bfloat16
    )
    attended, newest_pair = attend(
        stream_one, gain_block, asker_lookup_matrix, kv_cache, lengths, page_table, model_dim
    )
    attn_block = of_everyone(
        jnp.dot(attended, o_weight[0], preferred_element_type=jnp.float32), CHAN
    )
    stream_two = (stream_one.astype(jnp.float32) + attn_block).astype(jnp.bfloat16)
    whole_two = copy_for_each(stream_two, SEQ).swapaxes(0, 1).reshape(requests, model_dim)
    normed_two = normalize(whole_two, norm_gain[2])
    gated_two, state_two, conv_two = mamba_mix(normed_two, 1, layer_params)
    out_block = (stream_two.astype(jnp.float32) + mix_out(gated_two, out_weight, 1)).astype(
        jnp.bfloat16
    )
    hidden_out = lax.dynamic_slice_in_dim(
        out_block, lax.axis_index(CHAN) * share_cols, share_cols, 1
    )
    return (
        hidden_out,
        jnp.stack([state_first, state_two]),
        jnp.stack([conv_first, conv_two]),
        newest_pair,
    )


def solution(mesh):
    split = Mesh(mesh.devices.reshape(8, 4, 4, 2), ALL)
    placed = (
        P(),
        P(),
        P(None, None, None, ALL),
        P(None, None, ALL),
        P(None, ALL),
        P(None, None, None, ALL),
        P(None, ALL, None),
        P(None, None, ALL),
        P(None, ALL),
        P(None, None, ALL),
        P(None, ALL),
        P(None, None, None, ALL),
        P(None, ALL, None),
        P(SEQ, CHAN, None),
        P(CHAN, None, SEQ),
        P(SEQ, None, None, CHAN, None),
        P(),
        P(),
    )
    return jax.shard_map(
        shards,
        mesh=split,
        in_specs=placed,
        out_specs=(
            P(None, ALL),
            P(None, None, None, ALL),
            P(None, None, None, ALL),
            P(None, CHAN, None, None),
        ),
        check_vma=False,
    )
```

time: 324 us -> 209 us (0.65)
  blocking collectives: 121 us -> 20.3 us
  local copies, waits for them, and re-layouts: 37.3 us -> 21.1 us
  starting transfers between devices: 43.8 us -> 56.5 us
  other arithmetic: 16.3 us -> 7.72 us
    all_to_all x7 -> x2, blocking collectives: 81.7 us -> 20.3 us  [copy_for_each(): return lax.all_to_all(copies, axes, split_axis=0, concat_axis=0, tiled=True)]
    all_gather x2 -> x0, blocking collectives: 39.8 us -> none  [gathered_once(): both, at, found = (lax.all_gather(jnp.concatenate(lines), axis), 0, {})]
    all_to_all x8 -> x10, starting transfers between devices: 43.8 us -> 56.5 us  [the longest x8 48.8 us: copy_for_each(): return lax.all_to_all(copies, axes, split_axis=0, concat_axis=0, tiled=True)]
    unnamed x92 -> x69, local copies, waits for them, and re-layouts: 11.3 us -> 4.95 us
    another operation x5 -> x1, local copies, waits for them, and re-layouts: 4.37 us -> 0.02 us  [local_attention(): questions.reshape(requests * group_size, width)]
    all_to_all x5 -> x0, other arithmetic: 4.19 us -> none  [the longest x3 2.92 us: sum_at_owner(): lax.all_to_all(blocks, axis, split_axis=0, concat_axis=0, tiled=True)]
    dot_general x6, matrix products: 5.15 us -> 8.64 us  [the longest x2 4.42 us: mix_out(): jnp.dot(gated_out, out_weight[layer], preferred_element_type=jnp.float32)]
    all_to_all x8 -> x10, waiting for transfers between devices: 92.6 us -> 90.1 us  [the longest x8 71.1 us: copy_for_each(): return lax.all_to_all(copies, axes, split_axis=0, concat_axis=0, tiled=True)]
  transfers between devices with their start and end apart: 8 -> 10, of which waited for: 8 -> 10; matrix products, arithmetic and copies ran while one was open for 4% -> 5% of each run, Pallas kernels for 0% -> 0%
where the time goes in v1:
time: 209 us; the launch traced here: 208 us
  waiting for transfers between devices  90.1 us (43%)
  starting transfers between devices  56.5 us (27%)
  local copies, waits for them, and re-layouts  21.1 us (10%)
  blocking collectives  20.3 us (10%)
  matrix products  10.5 us (5%)
  other arithmetic  7.72 us (4%)
    all_to_all x8, waiting for transfers between devices, copy_for_each(): return lax.all_to_all(copies, axes, split_axis=0, concat_axis=0, tiled=True)  71.1 us
    all_to_all x8, starting transfers between devices, copy_for_each(): return lax.all_to_all(copies, axes, split_axis=0, concat_axis=0, tiled=True)  48.8 us
    all_to_all x2, blocking collectives, copy_for_each(): return lax.all_to_all(copies, axes, split_axis=0, concat_axis=0, tiled=True)  20.3 us
    all_to_all x2, waiting for transfers between devices, mix_out(): lax.all_to_all(blocks, SEQ, split_axis=0, concat_axis=0, tiled=True)  19 us
    all_to_all x2, starting transfers between devices, mix_out(): lax.all_to_all(blocks, SEQ, split_axis=0, concat_axis=0, tiled=True)  7.72 us
    broadcast_in_dim x10, local copies, waits for them, and re-layouts, copy_for_each(): copies = jnp.broadcast_to(x, (lax.axis_size(axes), *x.shape))  5.75 us
    unnamed x69, local copies, waits for them, and re-layouts  4.95 us
    dot_general x2, matrix products, mix_out(): jnp.dot(gated_out, out_weight[layer], preferred_element_type=jnp.float32)  4.42 us
  transfers between devices with their start and end apart: 10, of which 10 were waited for; matrix products, arithmetic and copies ran while one was open for 5% of the time, Pallas kernels for 0%

profile of v1, /device:TPU:1, one launch (start us, length us, event | category | flops | bytes accessed | tf_op | source)
XLA Modules:
  0.0 207.6 jit_solution(4144325792044051859)
XLA Ops:
  0.7 2.7 %fusion.102 = (bf16[1,8192,2,64]{1,3,2,0:T(8,128)(2,1)S(1)}, bf16[1,8192,2,64]{1,3,2,0:T(8,128)(2,1)S(1)}) fusion(bf16[2,8192,2,64]{1,3,2,0:T(8,128)(2,1)} %param.20), kind=kLoop, calls=%fused_computation.197 | loop fusion | bytes 8388608 | tf_op jit(solution)/shard_map/slice | solution.py:54
  3.8 0.7 convolution_convert_fusion.8
  5.8 0.7 broadcast_in_dim.109
  6.5 7.6 %all-to-all-start = ((bf16[16,8,544]{2,1,0:T(8,128)(2,1)}), bf16[16,8,544]{2,1,0:T(8,128)(2,1)S(1)}, u32[]{:S(2)}, u32[]{:S(2)}) async-start(bf16[16,8,544]{2,1,0:T(8,128)(2,1)} %broadcast_in_dim.109), calls=%async_computation | async-start | bytes 327680 | tf_op jit(solution)/shard_map/all_to_all | solution.py:20
  14.6 6.5 %all-to-all-done = bf16[16,8,544]{2,1,0:T(8,128)(2,1)S(1)} async-done(((bf16[16,8,544]{2,1,0:T(8,128)(2,1)}), bf16[16,8,544]{2,1,0:T(8,128)(2,1)S(1)}, u32[]{:S(2)}, u32[]{:S(2)}) %all-to-all-start) | async-done | bytes 139296 | tf_op jit(solution)/shard_map/all_to_all | solution.py:20
  21.1 0.7 broadcast_in_dim.110
  21.8 10.4 %all-to-all-start.1 = ((bf16[16,8,544]{2,1,0:T(8,128)(2,1)}), bf16[16,8,544]{2,1,0:T(8,128)(2,1)S(1)}, u32[]{:S(2)}, u32[]{:S(2)}) async-start(bf16[16,8,544]{2,1,0:T(8,128)(2,1)} %broadcast_in_dim.110), calls=%async_computation.1 | async-start | bytes 327680 | tf_op jit(solution)/shard_map/all_to_all | solution.py:20
  32.7 9.0 %all-to-all-done.1 = bf16[16,8,544]{2,1,0:T(8,128)(2,1)S(1)} async-done(((bf16[16,8,544]{2,1,0:T(8,128)(2,1)}), bf16[16,8,544]{2,1,0:T(8,128)(2,1)S(1)}, u32[]{:S(2)}, u32[]{:S(2)}) %all-to-all-start.1) | async-done | bytes 139296 | tf_op jit(solution)/shard_map/all_to_all | solution.py:20
  42.1 2.2 %convolution_convert_fusion.1 = bf16[8,8192]{1,0:T(8,128)(2,1)} fusion(bf16[2,64,8192]{2,1,0:T(8,128)(2,1)} %param.30, f32[8,64]{1,0:T(8,128)S(1)} %fusion.33, bf16[8,64]{1,0:T(8,128)(2,1)S(1)} %multiply_convert_fusion.1, bf16[8,128]{1,0:T(8,128)(2,1)S(1)} %convolution_convert_fusion.8, f32[64]{0:T(128)S(1)} %get-tuple-element.56), kind=kOutput, calls=%fused_computation.1 | convolution fusion | flops 8459264 | bytes 1185024 | tf_op jit(solution)/shard_map/dot_general | solution.py:85
  44.4 3.9 %all-to-all-start.2 = ((bf16[32,8,256]{2,1,0:T(8,128)(2,1)}), bf16[32,8,256]{2,1,0:T(8,128)(2,1)S(1)}, u32[]{:S(2)}, u32[]{:S(2)}) async-start(bf16[32,8,256]{2,1,0:T(8,128)(2,1)} %bitcast.14), calls=%async_computation.2 | async-start | bytes 262144 | tf_op jit(solution)/shard_map/all_to_all | solution.py:89
  48.2 9.8 %all-to-all-done.2 = bf16[32,8,256]{2,1,0:T(8,128)(2,1)S(1)} async-done(((bf16[32,8,256]{2,1,0:T(8,128)(2,1)}), bf16[32,8,256]{2,1,0:T(8,128)(2,1)S(1)}, u32[]{:S(2)}, u32[]{:S(2)}) %all-to-all-start.2) | async-done | bytes 131104 | tf_op jit(solution)/shard_map/all_to_all | solution.py:89
  58.1 0.6 broadcast_in_dim.111
  58.7 4.9 %all-to-all-start.3 = ((bf16[8,8,256]{2,1,0:T(8,128)(2,1)}), bf16[8,8,256]{2,1,0:T(8,128)(2,1)S(1)}, u32[]{:S(2)}, u32[]{:S(2)}) async-start(bf16[8,8,256]{2,1,0:T(8,128)(2,1)} %broadcast_in_dim.111), calls=%async_computation.3 | async-start | bytes 65536 | tf_op jit(solution)/shard_map/all_to_all | solution.py:20
  63.6 4.7 %all-to-all-done.3 = bf16[8,8,256]{2,1,0:T(8,128)(2,1)S(1)} async-done(((bf16[8,8,256]{2,1,0:T(8,128)(2,1)}), bf16[8,8,256]{2,1,0:T(8,128)(2,1)S(1)}, u32[]{:S(2)}, u32[]{:S(2)}) %all-to-all-start.3) | async-done | bytes 32800 | tf_op jit(solution)/shard_map/all_to_all | solution.py:20
  69.2 0.9 broadcast_in_dim.117
  70.1 3.9 %all-to-all-start.4 = ((bf16[32,8,1408]{2,1,0:T(8,128)(2,1)}), bf16[32,8,1408]{2,1,0:T(8,128)(2,1)S(1)}, u32[]{:S(2)}, u32[]{:S(2)}) async-start(bf16[32,8,1408]{2,1,0:T(8,128)(2,1)} %broadcast_in_dim.117), calls=%async_computation.4 | async-start | bytes 1441792 | tf_op jit(solution)/shard_map/all_to_all | solution.py:20
  74.1 4.2 %fusion.103 = (bf16[8,256,1,1,128]{4,2,3,1,0:T(2,128)(2,1)}, bf16[8,256,1,1,128]{4,2,3,1,0:T(2,128)(2,1)S(1)}) fusion(bf16[8,256,2,1,128]{4,2,3,1,0:T(2,128)(2,1)} %param.33), kind=kLoop, calls=%fused_computation.198 | loop fusion | bytes 2097152 | tf_op jit(solution)/shard_map/slice | solution.py:105
  78.3 0.9 copy.81
  79.6 2.1 %copy.82 = bf16[8,256,1,1,128]{4,1,0,3,2:T(8,128)(2,1)} copy(bf16[8,256,1,1,128]{4,2,3,1,0:T(2,128)(2,1)} %get-tuple-element.30) | data formatting | bytes 1048576
  81.8 12.3 %all-to-all-done.4 = bf16[32,8,1408]{2,1,0:T(8,128)(2,1)S(1)} async-done(((bf16[32,8,1408]{2,1,0:T(8,128)(2,1)}), bf16[32,8,1408]{2,1,0:T(8,128)(2,1)S(1)}, u32[]{:S(2)}, u32[]{:S(2)}) %all-to-all-start.4) | async-done | bytes 720928 | tf_op jit(solution)/shard_map/all_to_all | solution.py:20
  94.5 1.4 fusion.108
  96.3 1.4 convolution_convert_fusion.3
  97.7 0.9 broadcast_in_dim.120
  98.6 5.6 %all-to-all-start.5 = ((bf16[32,72,128]{2,1,0:T(8,128)(2,1)}), bf16[32,72,128]{2,1,0:T(8,128)(2,1)S(1)}, u32[]{:S(2)}, u32[]{:S(2)}) async-start(bf16[32,72,128]{2,1,0:T(8,128)(2,1)} %broadcast_in_dim.120), calls=%async_computation.5 | async-start | bytes 1179648 | tf_op jit(solution)/shard_map/all_to_all | solution.py:20
  104.5 16.3 %all-to-all-done.5 = bf16[32,72,128]{2,1,0:T(8,128)(2,1)S(1)} async-done(((bf16[32,72,128]{2,1,0:T(8,128)(2,1)}), bf16[32,72,128]{2,1,0:T(8,128)(2,1)S(1)}, u32[]{:S(2)}, u32[]{:S(2)}) %all-to-all-start.5) | async-done | bytes 589856 | tf_op jit(solution)/shard_map/all_to_all | solution.py:20
  120.9 1.0 copy-done.1
  122.0 0.8 fusion.43
  122.8 0.7 fusion.44
  124.0 1.6 fusion.1
  125.7 1.2 convolution_convert_fusion.6
  126.9 10.6 %all_to_all.60 = bf16[8,8,256]{2,1,0:T(8,128)(2,1)S(1)} all-to-all(bf16[8,8,256]{2,1,0:T(8,128)(2,1)S(1)} %broadcast_in_dim.121), channel_id=1, replica_groups=mesh['z'=8,'x'=4,'y'=4,'core'=2] {'y','core'}, dimensions={0} | all-to-all | bytes 65536 | tf_op jit(solution)/shard_map/all_to_all | solution.py:20
  137.6 0.7 broadcast_in_dim.122
  138.2 4.6 %all-to-all-start.7 = ((bf16[32,8,256]{2,1,0:T(8,128)(2,1)}), bf16[32,8,256]{2,1,0:T(8,128)(2,1)S(1)}, u32[]{:S(2)}, u32[]{:S(2)}) async-start(bf16[32,8,256]{2,1,0:T(8,128)(2,1)} %broadcast_in_dim.122), calls=%async_computation.7 | async-start | bytes 262144 | tf_op jit(solution)/shard_map/all_to_all | solution.py:20
  142.9 9.3 %all-to-all-done.7 = bf16[32,8,256]{2,1,0:T(8,128)(2,1)S(1)} async-done(((bf16[32,8,256]{2,1,0:T(8,128)(2,1)}), bf16[32,8,256]{2,1,0:T(8,128)(2,1)S(1)}, u32[]{:S(2)}, u32[]{:S(2)}) %all-to-all-start.7) | async-done | bytes 131104 | tf_op jit(solution)/shard_map/all_to_all | solution.py:20
  152.5 0.6 convolution_convert_fusion.7
  153.4 9.7 %all_to_all.61 = bf16[16,8,544]{2,1,0:T(8,128)(2,1)S(1)} all-to-all(bf16[16,8,544]{2,1,0:T(8,128)(2,1)S(1)} %broadcast_in_dim.124), channel_id=1, replica_groups=mesh['z'=8,'x'=4,'y'=4,'core'=2] {'x','y'}, dimensions={0} | all-to-all | bytes 278528 | tf_op jit(solution)/shard_map/all_to_all | solution.py:20
  163.1 0.7 broadcast_in_dim.125
  163.7 6.9 %all-to-all-start.9 = ((bf16[16,8,544]{2,1,0:T(8,128)(2,1)}), bf16[16,8,544]{2,1,0:T(8,128)(2,1)S(1)}, u32[]{:S(2)}, u32[]{:S(2)}) async-start(bf16[16,8,544]{2,1,0:T(8,128)(2,1)} %broadcast_in_dim.125), calls=%async_computation.9 | async-start | bytes 327680 | tf_op jit(solution)/shard_map/all_to_all | solution.py:20
  171.3 9.0 %all-to-all-done.9 = bf16[16,8,544]{2,1,0:T(8,128)(2,1)S(1)} async-done(((bf16[16,8,544]{2,1,0:T(8,128)(2,1)}), bf16[16,8,544]{2,1,0:T(8,128)(2,1)S(1)}, u32[]{:S(2)}, u32[]{:S(2)}) %all-to-all-start.9) | async-done | bytes 139296 | tf_op jit(solution)/shard_map/all_to_all | solution.py:20
  180.7 2.2 %convolution_convert_fusion = bf16[8,8192]{1,0:T(8,128)(2,1)} fusion(bf16[2,64,8192]{2,1,0:T(8,128)(2,1)} %param.30, f32[8,64]{1,0:T(8,128)S(1)} %fusion.29, bf16[8,64]{1,0:T(8,128)(2,1)S(1)} %multiply_convert_fusion, bf16[8,128]{1,0:T(8,128)(2,1)S(1)} %convolution_convert_fusion.7, f32[64]{0:T(128)S(1)} %copy-done.26), kind=kOutput, calls=%fused_computation | convolution fusion | flops 8459264 | bytes 1185024 | tf_op jit(solution)/shard_map/dot_general | solution.py:85
  182.9 3.9 %all-to-all-start.10 = ((bf16[32,8,256]{2,1,0:T(8,128)(2,1)}), bf16[32,8,256]{2,1,0:T(8,128)(2,1)S(1)}, u32[]{:S(2)}, u32[]{:S(2)}) async-start(bf16[32,8,256]{2,1,0:T(8,128)(2,1)} %bitcast.43), calls=%async_computation.10 | async-start | bytes 262144 | tf_op jit(solution)/shard_map/all_to_all | solution.py:89
  186.8 0.6 pad_maximum_fusion.2
  187.5 9.2 %all-to-all-done.10 = bf16[32,8,256]{2,1,0:T(8,128)(2,1)S(1)} async-done(((bf16[32,8,256]{2,1,0:T(8,128)(2,1)}), bf16[32,8,256]{2,1,0:T(8,128)(2,1)S(1)}, u32[]{:S(2)}, u32[]{:S(2)}) %all-to-all-start.10) | async-done | bytes 131104 | tf_op jit(solution)/shard_map/all_to_all | solution.py:89
  196.7 0.6 broadcast_in_dim.126
  197.3 4.9 %all-to-all-start.11 = ((bf16[8,8,256]{2,1,0:T(8,128)(2,1)}), bf16[8,8,256]{2,1,0:T(8,128)(2,1)S(1)}, u32[]{:S(2)}, u32[]{:S(2)}) async-start(bf16[8,8,256]{2,1,0:T(8,128)(2,1)} %broadcast_in_dim.126), calls=%async_computation.11 | async-start | bytes 65536 | tf_op jit(solution)/shard_map/all_to_all | solution.py:20
  202.2 0.7 pad_maximum_fusion
  202.8 4.1 %all-to-all-done.11 = bf16[8,8,256]{2,1,0:T(8,128)(2,1)S(1)} async-done(((bf16[8,8,256]{2,1,0:T(8,128)(2,1)}), bf16[8,8,256]{2,1,0:T(8,128)(2,1)S(1)}, u32[]{:S(2)}, u32[]{:S(2)}) %all-to-all-start.11) | async-done | bytes 32800 | tf_op jit(solution)/shard_map/all_to_all | solution.py:20
  206.9 0.7 fusion.67
  (152 shorter events, 8.0 us)
Async XLA Ops:
  0.6 68.1 %copy-start = (bf16[256,1,1280]{2,0,1:T(8,128)(2,1)S(1)}, bf16[256,1,1280]{2,0,1:T(8,128)(2,1)}, u32[]{:S(2)}) copy-start(bf16[256,1,1280]{2,0,1:T(8,128)(2,1)} %param.31) | copy-start | bytes 1966084
  0.6 2.7 %copy-start.9 = (f32[3,8192]{1,0:T(4,128)S(1)}, f32[3,8192]{1,0:T(4,128)}, u32[]{:S(2)}) copy-start(f32[3,8192]{1,0:T(4,128)} %param.19) | copy-start | bytes 294916
  0.7 2.9 %copy-start.2 = (bf16[8,8192]{1,0:T(8,128)(2,1)S(1)}, bf16[8,8192]{1,0:T(8,128)(2,1)}, u32[]{:S(2)}) copy-start(bf16[8,8192]{1,0:T(8,128)(2,1)} %param.18) | copy-start | bytes 393220
  3.3 1.1 copy-start.21
  3.4 1.2 copy-start.24
  3.4 1.7 copy-start.28
  3.4 2.3 %copy-start.5 = (bf16[2,64,544]{2,1,0:T(8,128)(2,1)S(1)}, bf16[2,64,544]{2,1,0:T(8,128)(2,1)}, u32[]{:S(2)}) copy-start(bf16[2,64,544]{2,1,0:T(8,128)(2,1)} %param.24) | copy-start | bytes 417796
  3.4 38.5 %copy-start.7 = (bf16[2,512,64]{1,2,0:T(8,128)(2,1)S(1)}, bf16[2,512,64]{1,2,0:T(8,128)(2,1)}, u32[]{:S(2)}) copy-start(bf16[2,512,64]{1,2,0:T(8,128)(2,1)} %param.25) | copy-start | bytes 393220
  3.4 38.6 %copy-start.3 = (f32[2,8,16,64]{3,2,1,0:T(8,128)S(1)}, f32[2,8,16,64]{3,2,1,0:T(8,128)}, u32[]{:S(2)}) copy-start(f32[2,8,16,64]{3,2,1,0:T(8,128)} %param.29) | copy-start | bytes 196612
  3.6 10.6 %copy-start.29 = (f32[2,64]{1,0:T(2,128)S(1)}, f32[2,64]{1,0:T(2,128)}, u32[]{:S(2)}) copy-start(f32[2,64]{1,0:T(2,128)} %param.26) | copy-start | bytes 1540
  3.6 28.7 %copy-start.30 = (f32[2,64]{1,0:T(2,128)S(1)}, f32[2,64]{1,0:T(2,128)}, u32[]{:S(2)}) copy-start(f32[2,64]{1,0:T(2,128)} %param.28) | copy-start | bytes 1540
  3.6 29.2 %copy-start.20 = (f32[2,16,64]{2,1,0:T(8,128)S(1)}, f32[2,16,64]{2,1,0:T(8,128)}, u32[]{:S(2)}) copy-start(f32[2,16,64]{2,1,0:T(8,128)} %param.27) | copy-start | bytes 24580
  4.5 1.2 copy-start.18
  6.5 14.6 %all-to-all-start = ((bf16[16,8,544]{2,1,0:T(8,128)(2,1)}), bf16[16,8,544]{2,1,0:T(8,128)(2,1)S(1)}, u32[]{:S(2)}, u32[]{:S(2)}) async-start(bf16[16,8,544]{2,1,0:T(8,128)(2,1)} %broadcast_in_dim.109), calls=%async_computation | async-start | bytes 327680 | tf_op jit(solution)/shard_map/all_to_all | solution.py:20
  21.8 19.9 %all-to-all-start.1 = ((bf16[16,8,544]{2,1,0:T(8,128)(2,1)}), bf16[16,8,544]{2,1,0:T(8,128)(2,1)S(1)}, u32[]{:S(2)}, u32[]{:S(2)}) async-start(bf16[16,8,544]{2,1,0:T(8,128)(2,1)} %broadcast_in_dim.110), calls=%async_computation.1 | async-start | bytes 327680 | tf_op jit(solution)/shard_map/all_to_all | solution.py:20
  41.9 28.3 %copy-start.14 = (f32[8,16]{1,0:T(8,128)}, f32[8,16]{1,0:T(8,128)S(1)}, u32[]{:S(2)}) copy-start(f32[8,16]{1,0:T(8,128)S(1)} %get-tuple-element.43) | copy-start | bytes 1540
  42.0 28.1 %copy-start.10 = (f32[8,64]{1,0:T(8,128)}, f32[8,64]{1,0:T(8,128)S(1)}, u32[]{:S(2)}) copy-start(f32[8,64]{1,0:T(8,128)S(1)} %get-tuple-element.53) | copy-start | bytes 6148
  42.0 28.1 %copy-start.12 = (f32[8,64]{1,0:T(8,128)}, f32[8,64]{1,0:T(8,128)S(1)}, u32[]{:S(2)}) copy-start(f32[8,64]{1,0:T(8,128)S(1)} %get-tuple-element.54) | copy-start | bytes 6148
  44.4 13.7 %all-to-all-start.2 = ((bf16[32,8,256]{2,1,0:T(8,128)(2,1)}), bf16[32,8,256]{2,1,0:T(8,128)(2,1)S(1)}, u32[]{:S(2)}, u32[]{:S(2)}) async-start(bf16[32,8,256]{2,1,0:T(8,128)(2,1)} %bitcast.14), calls=%async_computation.2 | async-start | bytes 262144 | tf_op jit(solution)/shard_map/all_to_all | solution.py:89
  58.7 9.6 %all-to-all-start.3 = ((bf16[8,8,256]{2,1,0:T(8,128)(2,1)}), bf16[8,8,256]{2,1,0:T(8,128)(2,1)S(1)}, u32[]{:S(2)}, u32[]{:S(2)}) async-start(bf16[8,8,256]{2,1,0:T(8,128)(2,1)} %broadcast_in_dim.111), calls=%async_computation.3 | async-start | bytes 65536 | tf_op jit(solution)/shard_map/all_to_all | solution.py:20
  68.5 0.6 copy-start.16
  70.1 24.0 %all-to-all-start.4 = ((bf16[32,8,1408]{2,1,0:T(8,128)(2,1)}), bf16[32,8,1408]{2,1,0:T(8,128)(2,1)S(1)}, u32[]{:S(2)}, u32[]{:S(2)}) async-start(bf16[32,8,1408]{2,1,0:T(8,128)(2,1)} %broadcast_in_dim.117), calls=%async_computation.4 | async-start | bytes 1441792 | tf_op jit(solution)/shard_map/all_to_all | solution.py:20
  74.1 5.1 %copy-start.31 = (s32[8]{0:T(128)S(1)}, s32[8]{0:T(128)}, u32[]{:S(2)}) copy-start(s32[8]{0:T(128)} %param.34) | copy-start | bytes 100
  74.1 5.2 %copy-start.23 = (s32[8,32]{1,0:T(8,128)S(1)}, s32[8,32]{1,0:T(8,128)}, u32[]{:S(2)}) copy-start(s32[8,32]{1,0:T(8,128)} %param.35) | copy-start | bytes 3076
  98.6 22.2 %all-to-all-start.5 = ((bf16[32,72,128]{2,1,0:T(8,128)(2,1)}), bf16[32,72,128]{2,1,0:T(8,128)(2,1)S(1)}, u32[]{:S(2)}, u32[]{:S(2)}) async-start(bf16[32,72,128]{2,1,0:T(8,128)(2,1)} %broadcast_in_dim.120), calls=%async_computation.5 | async-start | bytes 1179648 | tf_op jit(solution)/shard_map/all_to_all | solution.py:20
  104.2 33.3 %copy-start.17 = (bf16[8,256]{1,0:T(8,128)(2,1)S(1)}, bf16[8,256]{1,0:T(8,128)(2,1)}, u32[]{:S(2)}) copy-start(bf16[8,256]{1,0:T(8,128)(2,1)} %copy-done.16) | copy-start | bytes 12292
  120.9 1.0 copy-start.1
  125.6 27.6 %copy-start.22 = (f32[4,64]{1,0:T(4,128)S(1)}, f32[4,64]{1,0:T(4,128)}, u32[]{:S(2)}) copy-start(f32[4,64]{1,0:T(4,128)} %get-tuple-element.51) | copy-start | bytes 3076
  125.6 27.6 %copy-start.27 = (f32[64]{0:T(128)S(1)}, f32[64]{0:T(128)}, u32[]{:S(2)}) copy-start(f32[64]{0:T(128)} %get-tuple-element.59) | copy-start | bytes 772
  125.6 27.6 %copy-start.6 = (bf16[2,64,544]{2,1,0:T(8,128)(2,1)S(1)}, bf16[2,64,544]{2,1,0:T(8,128)(2,1)}, u32[]{:S(2)}) copy-start(bf16[2,64,544]{2,1,0:T(8,128)(2,1)} %param.24) | copy-start | bytes 417796
  138.2 32.5 %copy-start.19 = (bf16[8,1,64]{2,0,1:T(8,128)(2,1)S(1)}, bf16[8,1,64]{2,0,1:T(8,128)(2,1)}, u32[]{:S(2)}) copy-start(bf16[8,1,64]{2,0,1:T(8,128)(2,1)} %copy-done.18) | copy-start | bytes 3076
  138.2 13.9 %all-to-all-start.7 = ((bf16[32,8,256]{2,1,0:T(8,128)(2,1)}), bf16[32,8,256]{2,1,0:T(8,128)(2,1)S(1)}, u32[]{:S(2)}, u32[]{:S(2)}) async-start(bf16[32,8,256]{2,1,0:T(8,128)(2,1)} %broadcast_in_dim.122), calls=%async_computation.7 | async-start | bytes 262144 | tf_op jit(solution)/shard_map/all_to_all | solution.py:20
  142.8 37.6 %copy-start.8 = (bf16[2,512,64]{1,2,0:T(8,128)(2,1)S(1)}, bf16[2,512,64]{1,2,0:T(8,128)(2,1)}, u32[]{:S(2)}) copy-start(bf16[2,512,64]{1,2,0:T(8,128)(2,1)} %param.25) | copy-start | bytes 393220
  142.8 37.6 %copy-start.25 = (f32[64]{0:T(128)S(1)}, f32[64]{0:T(128)}, u32[]{:S(2)}) copy-start(f32[64]{0:T(128)} %get-tuple-element.57) | copy-start | bytes 772
  152.4 28.2 %copy-start.4 = (f32[2,8,16,64]{3,2,1,0:T(8,128)S(1)}, f32[2,8,16,64]{3,2,1,0:T(8,128)}, u32[]{:S(2)}) copy-start(f32[2,8,16,64]{3,2,1,0:T(8,128)} %param.29) | copy-start | bytes 196612
  152.4 28.3 %copy-start.26 = (f32[64]{0:T(128)S(1)}, f32[64]{0:T(128)}, u32[]{:S(2)}) copy-start(f32[64]{0:T(128)} %get-tuple-element.55) | copy-start | bytes 772
  153.1 34.3 %copy-start.11 = (f32[8,64]{1,0:T(8,128)S(1)}, f32[8,64]{1,0:T(8,128)}, u32[]{:S(2)}) copy-start(f32[8,64]{1,0:T(8,128)} %copy-done.10) | copy-start | bytes 6148
  153.1 34.3 %copy-start.13 = (f32[8,64]{1,0:T(8,128)S(1)}, f32[8,64]{1,0:T(8,128)}, u32[]{:S(2)}) copy-start(f32[8,64]{1,0:T(8,128)} %copy-done.12) | copy-start | bytes 6148
  153.1 34.3 %copy-start.15 = (f32[8,16]{1,0:T(8,128)S(1)}, f32[8,16]{1,0:T(8,128)}, u32[]{:S(2)}) copy-start(f32[8,16]{1,0:T(8,128)} %copy-done.14) | copy-start | bytes 1540
  163.7 16.6 %all-to-all-start.9 = ((bf16[16,8,544]{2,1,0:T(8,128)(2,1)}), bf16[16,8,544]{2,1,0:T(8,128)(2,1)S(1)}, u32[]{:S(2)}, u32[]{:S(2)}) async-start(bf16[16,8,544]{2,1,0:T(8,128)(2,1)} %broadcast_in_dim.125), calls=%async_computation.9 | async-start | bytes 327680 | tf_op jit(solution)/shard_map/all_to_all | solution.py:20
  182.9 13.8 %all-to-all-start.10 = ((bf16[32,8,256]{2,1,0:T(8,128)(2,1)}), bf16[32,8,256]{2,1,0:T(8,128)(2,1)S(1)}, u32[]{:S(2)}, u32[]{:S(2)}) async-start(bf16[32,8,256]{2,1,0:T(8,128)(2,1)} %bitcast.43), calls=%async_computation.10 | async-start | bytes 262144 | tf_op jit(solution)/shard_map/all_to_all | solution.py:89
  197.3 9.6 %all-to-all-start.11 = ((bf16[8,8,256]{2,1,0:T(8,128)(2,1)}), bf16[8,8,256]{2,1,0:T(8,128)(2,1)S(1)}, u32[]{:S(2)}, u32[]{:S(2)}) async-start(bf16[8,8,256]{2,1,0:T(8,128)(2,1)} %broadcast_in_dim.126), calls=%async_computation.11 | async-start | bytes 65536 | tf_op jit(solution)/shard_map/all_to_all | solution.py:20

commit v2 on v1

v2 whole, which is shorter than its diff:
```python
import jax
import jax.numpy as jnp
from jax import lax
from jax.sharding import Mesh
from jax.sharding import PartitionSpec as P

ALL = ("z", "x", "y", "core")
SEQ = ("z", "x")
CHAN = ("y", "core")
PLANE = ("x", "y")
LINE = ("z", "core")
WIRE = jnp.bfloat16

norm_eps = 1e-06
lowest_score = -1e30


def copy_for_each(x, axes):
    copies = jnp.broadcast_to(x, (lax.axis_size(axes), *x.shape))
    return lax.all_to_all(copies, axes, split_axis=0, concat_axis=0, tiled=True)


def of_everyone(x, axes):
    return jnp.sum(copy_for_each(x.astype(WIRE), axes).astype(jnp.float32), axis=0)


def normalize(stream, gain_row):
    widened = stream.astype(jnp.float32)
    inv_rms = lax.rsqrt(jnp.mean(widened * widened, axis=1) + norm_eps)
    return (widened * inv_rms[:, None] * gain_row[None, :]).astype(jnp.bfloat16)


def two_parts(x):
    high = x.astype(WIRE).astype(jnp.float32)
    return high, (x - high).astype(WIRE).astype(jnp.float32)


def layer_values(layer, conv_weight, conv_bias, conv_state, dt_bias, a_log, skip_gain, ssm_state):
    return (
        conv_weight[layer],
        conv_bias[layer],
        conv_state[layer],
        dt_bias[layer],
        jnp.exp(a_log[layer]),
        skip_gain[layer],
        ssm_state[layer],
    )


def rows_in_use(pages_dev, block_len, lengths, page_table):
    slot_ids = lax.axis_index(SEQ) * pages_dev + jnp.arange(pages_dev, dtype=jnp.int32)
    matches = page_table[:, :, None] == slot_ids[None, None, :]
    first_token = jnp.arange(page_table.shape[1], dtype=jnp.int32) * block_len
    left = jnp.clip(lengths[:, None] - first_token[None, :], 0, block_len)
    filled = jnp.sum(jnp.where(matches, left[:, :, None], 0), axis=1)
    place = jnp.arange(2 * block_len, dtype=jnp.int32)
    limit = jnp.where(place % 2 == 0, place // 2, block_len)
    return (limit[None, None, :] < filled[:, :, None]).reshape(lengths.shape[0], -1)


def mamba_in(normed, layer, in_weight, xproj_weight, values):
    conv_weight, conv_bias, conv_state = values[:3]
    channels = in_weight.shape[3]
    both_proj = jnp.dot(
        normed,
        in_weight[layer].reshape(in_weight.shape[1], 2 * channels),
        preferred_element_type=jnp.float32,
    ).astype(jnp.bfloat16)
    inputs = both_proj[:, :channels]
    gate = jax.nn.silu(both_proj[:, channels:].astype(jnp.float32))
    window = jnp.concatenate([conv_state, inputs[:, None, :]], axis=1)
    conv_sum = (
        jnp.sum(window.astype(jnp.float32) * conv_weight[None], axis=1) + conv_bias[None, :]
    )
    signal = lax.optimization_barrier(jax.nn.silu(conv_sum).astype(jnp.bfloat16))
    x_terms = jnp.dot(signal, xproj_weight[layer], preferred_element_type=jnp.float32)
    return x_terms, signal, gate, window[:, 1:, :]


def mamba_out(mapped_vectors, signal, gate, layer, dt_weight, out_weight, values):
    dt_bias, decay, skip_gain, ssm_state = values[3:]
    low_rank = dt_weight.shape[1]
    state_size = decay.shape[0]
    dt_low = mapped_vectors[:, :low_rank].astype(jnp.bfloat16)
    b_in = mapped_vectors[:, low_rank : low_rank + state_size]
    c_out = mapped_vectors[:, low_rank + state_size :]
    dt_step = jax.nn.softplus(
        jnp.dot(dt_low, dt_weight[layer], preferred_element_type=jnp.float32) + dt_bias[None, :]
    )
    widened = signal.astype(jnp.float32)
    decay_rate = jnp.exp(-dt_step[:, None, :] * decay[None])
    fresh_state = decay_rate * ssm_state + (dt_step * widened)[:, None, :] * b_in[:, :, None]
    readout = jnp.sum(fresh_state * c_out[:, :, None], axis=1) + skip_gain[None, :] * widened
    gated_out = (readout * gate).astype(jnp.bfloat16)
    partial = jnp.dot(gated_out, out_weight[layer], preferred_element_type=jnp.float32)
    rows, dim = partial.shape
    parts = lax.axis_size(SEQ)
    blocks = partial.astype(WIRE).reshape(rows, parts, dim // parts).swapaxes(0, 1)
    return blocks, fresh_state


def block_sums(blocks):
    arrived = lax.all_to_all(blocks, SEQ, split_axis=0, concat_axis=0, tiled=True)
    return of_everyone(jnp.sum(arrived.astype(jnp.float32), axis=0), CHAN)


def local_attention(questions, kv_rows, in_use, inv_sqrt):
    requests, group_size, width = questions.shape
    tokens = kv_rows.shape[0]
    visible = in_use[:, None, :]
    scores = (
        jnp.dot(
            questions.reshape(requests * group_size, width),
            kv_rows.T,
            preferred_element_type=jnp.float32,
        )
        * inv_sqrt
    ).reshape(requests, group_size, tokens)
    scores = jnp.where(visible, scores, lowest_score)
    high, low = two_parts(jnp.max(scores, axis=2))
    weight = jnp.where(visible, jnp.exp(scores - (high + low)[..., None]), 0.0)
    total = jnp.sum(weight, axis=2)
    moved = jnp.roll(
        weight.astype(jnp.bfloat16).reshape(requests * group_size, tokens), 1, axis=1
    )
    mixed = jnp.dot(moved, kv_rows, preferred_element_type=jnp.float32)
    return high, low, total, mixed


def project_questions(stream_one, gain_block, asker_lookup_matrix, model_dim):
    requests = stream_one.shape[0]
    entries = asker_lookup_matrix.shape[2]
    widened = stream_one.astype(jnp.float32)
    high, low = two_parts(jnp.sum(widened * widened, axis=1))
    scaled = (widened * gain_block[None, :]).astype(jnp.bfloat16)
    terms = jnp.dot(scaled, asker_lookup_matrix[:, 0, :], preferred_element_type=jnp.float32)
    summed = of_everyone(
        jnp.concatenate([terms, high[:, None], low[:, None], jnp.zeros((requests, 126))], axis=1),
        SEQ,
    )
    inv_rms = lax.rsqrt((summed[:, entries] + summed[:, entries + 1]) / model_dim + norm_eps)
    return (summed[:, :entries] * inv_rms[:, None]).astype(jnp.bfloat16)


def attend(qkv, kv_rows, in_use, width):
    requests, entries = qkv.shape
    group_size = entries // width - 2
    rows = requests * group_size
    inv_sqrt = width ** (-0.5)
    questions = qkv[:, : group_size * width].reshape(requests, group_size, width)
    fresh_key = qkv[:, group_size * width : (group_size + 1) * width]
    fresh_value = qkv[:, (group_size + 1) * width :]
    fresh_score = (
        jnp.sum(
            questions.astype(jnp.float32) * fresh_key[:, None, :].astype(jnp.float32), axis=2
        )
        * inv_sqrt
    )
    high, low, total, mixed = local_attention(questions, kv_rows, in_use, inv_sqrt)
    notes = jnp.stack([high.reshape(rows), low.reshape(rows), total.reshape(rows)])
    notes = jnp.pad(notes, ((0, 5), (0, width - rows)))
    packed = jnp.concatenate([mixed, notes], axis=0).astype(WIRE)
    packed, fresh_score, fresh_value = lax.optimization_barrier(
        (packed, fresh_score, fresh_value.astype(jnp.float32))
    )
    arrived = copy_for_each(packed, SEQ).astype(jnp.float32)
    tops = (arrived[:, rows, :rows] + arrived[:, rows + 1, :rows]).reshape(
        -1, requests, group_size
    )
    totals = arrived[:, rows + 2, :rows].reshape(-1, requests, group_size)
    mixes = arrived[:, :rows].reshape(-1, requests, group_size, width)
    final_top = jnp.maximum(jnp.max(tops, axis=0), fresh_score)
    scale = jnp.exp(tops - final_top[None])
    fresh_weight = jnp.exp(fresh_score - final_top)
    denominator = jnp.sum(scale * totals, axis=0) + fresh_weight
    numerator = (
        jnp.sum(scale[..., None] * mixes, axis=0)
        + fresh_weight[..., None] * fresh_value[:, None, :]
    )
    attended = (numerator / denominator[..., None]).astype(jnp.bfloat16)
    return attended.reshape(requests, group_size * width)


def shards(
    hidden,
    norm_gain,
    in_weight,
    conv_weight,
    conv_bias,
    conv_state,
    xproj_weight,
    dt_weight,
    dt_bias,
    a_log,
    skip_gain,
    ssm_state,
    out_weight,
    asker_lookup_matrix,
    o_weight,
    kv_cache,
    lengths,
    page_table,
):
    requests, model_dim = hidden.shape
    block_cols = model_dim // lax.axis_size(SEQ)
    share_cols = block_cols // lax.axis_size(CHAN)
    small = (conv_weight, conv_bias, conv_state, dt_bias, a_log, skip_gain, ssm_state)
    pages_dev, block_len, pair, _, width = kv_cache.shape
    kv_rows = kv_cache.reshape(pages_dev * block_len * pair, width)
    first_col = lax.axis_index(SEQ) * block_cols
    values_first = layer_values(0, *small)
    terms, signal, gate, conv_first = mamba_in(
        normalize(hidden, norm_gain[0]), 0, in_weight, xproj_weight, values_first
    )
    side = (
        values_first,
        layer_values(1, *small),
        lax.dynamic_slice_in_dim(hidden, first_col, block_cols, 1),
        lax.dynamic_slice_in_dim(norm_gain[1], first_col, block_cols, 0),
        norm_gain[2].reshape(-1, 1, block_cols),
        rows_in_use(pages_dev, block_len, lengths, page_table),
        lax.axis_index(CHAN) * share_cols,
        signal,
        gate,
        conv_first,
    )
    copies = copy_for_each(terms.astype(WIRE), PLANE)
    copies, side = lax.optimization_barrier((copies, side))
    (
        values_first,
        values_second,
        own_block,
        gain_block,
        gain_second,
        in_use,
        first_share,
        signal,
        gate,
        conv_first,
    ) = side
    mapped_vectors = of_everyone(jnp.sum(copies.astype(jnp.float32), axis=0), LINE)
    blocks, state_first = mamba_out(
        mapped_vectors, signal, gate, 0, dt_weight, out_weight, values_first
    )
    blocks, state_first = lax.optimization_barrier((blocks, state_first))
    stream_one = (own_block.astype(jnp.float32) + block_sums(blocks)).astype(jnp.bfloat16)
    qkv = project_questions(stream_one, gain_block, asker_lookup_matrix, model_dim)
    attended = attend(qkv, kv_rows, in_use, width)
    attn_block = of_everyone(
        jnp.dot(attended, o_weight[0], preferred_element_type=jnp.float32), CHAN
    )
    stream_two = (stream_one.astype(jnp.float32) + attn_block).astype(jnp.bfloat16)
    whole_two = copy_for_each(stream_two, SEQ).astype(jnp.float32)
    inv_rms = lax.rsqrt(jnp.sum(whole_two * whole_two, axis=(0, 2)) / model_dim + norm_eps)
    normed = (whole_two * inv_rms[:, None] * gain_second).astype(jnp.bfloat16)
    terms, signal, gate, conv_second = mamba_in(
        normed.swapaxes(0, 1).reshape(requests, model_dim), 1, in_weight, xproj_weight, values_second
    )
    terms, gate, new_conv = lax.optimization_barrier(
        (terms, gate, jnp.stack([conv_first, conv_second]))
    )
    mapped_vectors = of_everyone(of_everyone(terms, PLANE), LINE)
    blocks, state_second = mamba_out(
        mapped_vectors, signal, gate, 1, dt_weight, out_weight, values_second
    )
    blocks, new_ssm = lax.optimization_barrier((blocks, jnp.stack([state_first, state_second])))
    added, qkv, first_share = lax.optimization_barrier((block_sums(blocks), qkv, first_share))
    newest_pair = qkv[:, -2 * width :].reshape(requests, 1, 2, width)
    out_block = (stream_two.astype(jnp.float32) + added).astype(jnp.bfloat16)
    hidden_out = lax.dynamic_slice_in_dim(out_block, first_share, share_cols, 1)
    return hidden_out, new_ssm, new_conv, newest_pair


def solution(mesh):
    split = Mesh(mesh.devices.reshape(8, 4, 4, 2), ALL)
    placed = (
        P(),
        P(),
        P(None, None, None, ALL),
        P(None, None, ALL),
        P(None, ALL),
        P(None, None, None, ALL),
        P(None, ALL, None),
        P(None, None, ALL),
        P(None, ALL),
        P(None, None, ALL),
        P(None, ALL),
        P(None, None, None, ALL),
        P(None, ALL, None),
        P(SEQ, CHAN, None),
        P(CHAN, None, SEQ),
        P(SEQ, None, None, CHAN, None),
        P(),
        P(),
    )
    return jax.shard_map(
        shards,
        mesh=split,
        in_specs=placed,
        out_specs=(
            P(None, ALL),
            P(None, None, None, ALL),
            P(None, None, None, ALL),
            P(None, CHAN, None, None),
        ),
        check_vma=False,
    )
```

time: 209 us -> 212 us (1.014)
  blocking collectives: 20.3 us -> 161 us
  waiting for transfers between devices: 90.1 us -> 0.01 us
  starting transfers between devices: 56.5 us -> 7.57 us
  other arithmetic: 7.72 us -> 14.9 us
  local copies, waits for them, and re-layouts: 21.1 us -> 16.9 us
    all_to_all x2 -> x9, blocking collectives: 20.3 us -> 133 us  [copy_for_each(): return lax.all_to_all(copies, axes, split_axis=0, concat_axis=0, tiled=True)]
    all_to_all x8 -> x1, waiting for transfers between devices: 71.1 us -> 0.01 us  [copy_for_each(): return lax.all_to_all(copies, axes, split_axis=0, concat_axis=0, tiled=True)]
    all_to_all x8 -> x1, starting transfers between devices: 48.8 us -> 7.57 us  [copy_for_each(): return lax.all_to_all(copies, axes, split_axis=0, concat_axis=0, tiled=True)]
    all_to_all x0 -> x2, blocking collectives: none -> 27.1 us  [block_sums(): lax.all_to_all(blocks, SEQ, split_axis=0, concat_axis=0, tiled=True)]
    all_to_all x2 -> x0, waiting for transfers between devices: 19 us -> none  [mix_out(): lax.all_to_all(blocks, SEQ, split_axis=0, concat_axis=0, tiled=True)]
    all_to_all x2 -> x0, starting transfers between devices: 7.72 us -> none  [mix_out(): lax.all_to_all(blocks, SEQ, split_axis=0, concat_axis=0, tiled=True)]
    broadcast_in_dim x10, local copies, waits for them, and re-layouts: 5.75 us -> 0.88 us  [copy_for_each(): copies = jnp.broadcast_to(x, (lax.axis_size(axes), *x.shape))]
    squeeze x1 -> x5, local copies, waits for them, and re-layouts: 0.01 us -> 3.31 us  [the longest x1 1.3 us: layer_values(): skip_gain[layer]]
  transfers between devices with their start and end apart: 10 -> 1, of which waited for: 10 -> 0; matrix products, arithmetic and copies ran while one was open for 5% -> 4% of each run, Pallas kernels for 0% -> 0%
where the time goes in v2:
time: 212 us; the launch traced here: 211 us
  blocking collectives  161 us (76%)
  local copies, waits for them, and re-layouts  16.9 us (8%)
  other arithmetic  14.9 us (7%)
  matrix products  9.93 us (5%)
  starting transfers between devices  7.57 us (4%)
    all_to_all x9, blocking collectives, copy_for_each(): return lax.all_to_all(copies, axes, split_axis=0, concat_axis=0, tiled=True)  133 us
    all_to_all x2, blocking collectives, block_sums(): lax.all_to_all(blocks, SEQ, split_axis=0, concat_axis=0, tiled=True)  27.1 us
    all_to_all x1, starting transfers between devices, copy_for_each(): return lax.all_to_all(copies, axes, split_axis=0, concat_axis=0, tiled=True)  7.57 us
  transfers between devices with their start and end apart: 1, of which 0 were waited for; matrix products, arithmetic and copies ran while one was open for 4% of the time, Pallas kernels for 0%

profile of v2, /device:TPU:1, one launch (start us, length us, event | category | flops | bytes accessed | tf_op | source)
XLA Modules:
  0.0 211.0 jit_solution(968642609316036911)
XLA Ops:
  0.6 1.8 slice_reduce_fusion
  2.5 2.7 %fusion.97 = (bf16[1,8192,2,64]{1,3,2,0:T(8,128)(2,1)S(1)}, bf16[1,8192,2,64]{1,3,2,0:T(8,128)(2,1)S(1)}) fusion(bf16[2,8192,2,64]{1,3,2,0:T(8,128)(2,1)} %param.20), kind=kLoop, calls=%fused_computation.198 | loop fusion | bytes 8388608 | tf_op jit(solution)/shard_map/slice | solution.py:66
  5.4 0.7 convolution_convert_fusion.7
  7.5 0.7 broadcast_in_dim.63
  8.2 7.6 %all-to-all-start = ((bf16[16,8,544]{2,1,0:T(8,128)(2,1)}), bf16[16,8,544]{2,1,0:T(8,128)(2,1)S(1)}, u32[]{:S(2)}, u32[]{:S(2)}) async-start(bf16[16,8,544]{2,1,0:T(8,128)(2,1)} %broadcast_in_dim.63), calls=%async_computation | async-start | bytes 327680 | tf_op jit(solution)/shard_map/all_to_all | solution.py:20
  15.8 0.7 convert_multiply_fusion.12
  16.4 0.6 constant_dynamic-slice_fusion.1
  17.5 0.9 slice_bitcast_fusion
  18.4 1.3 exponential_bitcast_fusion
  19.8 1.3 slice_bitcast_fusion.9
  21.1 1.2 constant_dynamic-slice_fusion
  22.3 0.6 reshape_squeeze.11
  22.9 1.3 fusion.46
  24.3 18.8 %all_to_all.60 = bf16[16,8,544]{2,1,0:T(8,128)(2,1)S(1)} all-to-all(bf16[16,8,544]{2,1,0:T(8,128)(2,1)S(1)} %broadcast_in_dim.116), channel_id=1, replica_groups=mesh['z'=8,'x'=4,'y'=4,'core'=2] {'z','core'}, dimensions={0} | all-to-all | bytes 278528 | tf_op jit(solution)/shard_map/all_to_all | solution.py:20
  43.1 1.0 fusion.101
  44.1 0.8 multiply_reduce_fusion.1
  44.9 1.5 convolution_convert_fusion.1
  46.4 14.7 %all_to_all.61 = bf16[32,8,256]{2,1,0:T(8,128)(2,1)S(1)} all-to-all(bf16[32,8,256]{2,1,0:T(8,128)(2,1)S(1)} %bitcast.149), channel_id=1, replica_groups=mesh['z'=8,'x'=4,'y'=4,'core'=2] {'z','x'}, dimensions={0} | all-to-all | bytes 262144 | tf_op jit(solution)/shard_map/all_to_all | solution.py:103
  61.1 10.8 %all_to_all.62 = bf16[8,8,256]{2,1,0:T(8,128)(2,1)S(1)} all-to-all(bf16[8,8,256]{2,1,0:T(8,128)(2,1)S(1)} %broadcast_in_dim.117), channel_id=1, replica_groups=mesh['z'=8,'x'=4,'y'=4,'core'=2] {'y','core'}, dimensions={0} | all-to-all | bytes 65536 | tf_op jit(solution)/shard_map/all_to_all | solution.py:20
  72.3 1.3 convolution_convert_fusion.2
  73.8 23.0 %all_to_all.63 = bf16[32,8,1408]{2,1,0:T(8,128)(2,1)S(1)} all-to-all(bf16[32,8,1408]{2,1,0:T(8,128)(2,1)S(1)} %broadcast_in_dim.121), channel_id=1, replica_groups=mesh['z'=8,'x'=4,'y'=4,'core'=2] {'z','x'}, dimensions={0} | all-to-all | bytes 1441792 | tf_op jit(solution)/shard_map/all_to_all | solution.py:20
  97.2 0.6 slice_convert_fusion.8
  97.8 0.6 fusion.102
  99.5 21.9 %all_to_all.64 = bf16[32,72,128]{2,1,0:T(8,128)(2,1)S(1)} all-to-all(bf16[32,72,128]{2,1,0:T(8,128)(2,1)S(1)} %broadcast_in_dim.124), channel_id=1, replica_groups=mesh['z'=8,'x'=4,'y'=4,'core'=2] {'z','x'}, dimensions={0} | all-to-all | bytes 1179648 | tf_op jit(solution)/shard_map/all_to_all | solution.py:20
  121.5 1.0 copy-done.1
  122.9 0.8 fusion.39
  123.6 1.3 fusion.38
  125.0 1.6 fusion.1
  126.6 0.8 reduce_sum.232
  127.5 0.6 fusion.96
  128.1 0.8 copy.67
  128.9 0.8 fusion.40
  129.7 1.2 convolution_convert_fusion.5
  130.9 10.7 %all_to_all.65 = bf16[8,8,256]{2,1,0:T(8,128)(2,1)S(1)} all-to-all(bf16[8,8,256]{2,1,0:T(8,128)(2,1)S(1)} %broadcast_in_dim.125), channel_id=1, replica_groups=mesh['z'=8,'x'=4,'y'=4,'core'=2] {'y','core'}, dimensions={0} | all-to-all | bytes 65536 | tf_op jit(solution)/shard_map/all_to_all | solution.py:20
  141.7 13.4 %all_to_all.66 = bf16[32,8,256]{2,1,0:T(8,128)(2,1)S(1)} all-to-all(bf16[32,8,256]{2,1,0:T(8,128)(2,1)S(1)} %broadcast_in_dim.126), channel_id=1, replica_groups=mesh['z'=8,'x'=4,'y'=4,'core'=2] {'z','x'}, dimensions={0} | all-to-all | bytes 262144 | tf_op jit(solution)/shard_map/all_to_all | solution.py:20
  155.4 0.6 convolution_convert_fusion.6
  156.2 0.7 multiply_reduce_fusion.2
  156.9 0.6 multiply_convert_fusion
  157.7 1.3 pad_maximum_fusion.2
  159.0 9.7 %all_to_all.67 = bf16[16,8,544]{2,1,0:T(8,128)(2,1)S(1)} all-to-all(bf16[16,8,544]{2,1,0:T(8,128)(2,1)S(1)} %broadcast_in_dim.128), channel_id=1, replica_groups=mesh['z'=8,'x'=4,'y'=4,'core'=2] {'x','y'}, dimensions={0} | all-to-all | bytes 278528 | tf_op jit(solution)/shard_map/all_to_all | solution.py:20
  168.7 15.7 %all_to_all.68 = bf16[16,8,544]{2,1,0:T(8,128)(2,1)S(1)} all-to-all(bf16[16,8,544]{2,1,0:T(8,128)(2,1)S(1)} %broadcast_in_dim.129), channel_id=1, replica_groups=mesh['z'=8,'x'=4,'y'=4,'core'=2] {'z','core'}, dimensions={0} | all-to-all | bytes 278528 | tf_op jit(solution)/shard_map/all_to_all | solution.py:20
  184.5 1.0 fusion.100
  185.6 0.7 pad_maximum_fusion
  186.3 1.5 convolution_convert_fusion
  187.7 12.5 %all_to_all.69 = bf16[32,8,256]{2,1,0:T(8,128)(2,1)S(1)} all-to-all(bf16[32,8,256]{2,1,0:T(8,128)(2,1)S(1)} %bitcast.151), channel_id=1, replica_groups=mesh['z'=8,'x'=4,'y'=4,'core'=2] {'z','x'}, dimensions={0} | all-to-all | bytes 262144 | tf_op jit(solution)/shard_map/all_to_all | solution.py:103
  200.2 9.4 %all_to_all.70 = bf16[8,8,256]{2,1,0:T(8,128)(2,1)S(1)} all-to-all(bf16[8,8,256]{2,1,0:T(8,128)(2,1)S(1)} %broadcast_in_dim.130), channel_id=1, replica_groups=mesh['z'=8,'x'=4,'y'=4,'core'=2] {'y','core'}, dimensions={0} | all-to-all | bytes 65536 | tf_op jit(solution)/shard_map/all_to_all | solution.py:20
  209.7 0.6 copy.70
  210.3 0.7 fusion.60
  (116 shorter events, 5.8 us)
Async XLA Ops:
  0.6 97.2 %copy-start = (bf16[8,256,2,1,128]{4,2,3,1,0:T(2,128)(2,1)S(1)}, bf16[8,256,2,1,128]{4,2,3,1,0:T(2,128)(2,1)}, u32[]{:S(2)}) copy-start(bf16[8,256,2,1,128]{4,2,3,1,0:T(2,128)(2,1)} %param.33) | copy-start | bytes 3145732
  2.5 2.7 %copy-start.2 = (bf16[8,8192]{1,0:T(8,128)(2,1)S(1)}, bf16[8,8192]{1,0:T(8,128)(2,1)}, u32[]{:S(2)}) copy-start(bf16[8,8192]{1,0:T(8,128)(2,1)} %param.18) | copy-start | bytes 393220
  5.2 1.0 copy-start.10
  5.2 1.0 copy-start.13
  5.2 1.6 copy-start.16
  5.2 2.1 %copy-start.3 = (bf16[2,64,544]{2,1,0:T(8,128)(2,1)S(1)}, bf16[2,64,544]{2,1,0:T(8,128)(2,1)}, u32[]{:S(2)}) copy-start(bf16[2,64,544]{2,1,0:T(8,128)(2,1)} %param.24) | copy-start | bytes 417796
  5.2 11.8 %copy-start.17 = (s32[8]{0:T(128)S(1)}, s32[8]{0:T(128)}, u32[]{:S(2)}) copy-start(s32[8]{0:T(128)} %param.34) | copy-start | bytes 100
  5.2 11.9 %copy-start.12 = (s32[8,32]{1,0:T(8,128)S(1)}, s32[8,32]{1,0:T(8,128)}, u32[]{:S(2)}) copy-start(s32[8,32]{1,0:T(8,128)} %param.35) | copy-start | bytes 3076
  6.1 1.2 copy-start.8
  7.3 10.1 %copy-start.6 = (bf16[8,64]{1,0:T(8,128)(2,1)}, bf16[8,64]{1,0:T(8,128)(2,1)S(1)}, u32[]{:S(2)}) copy-start(bf16[8,64]{1,0:T(8,128)(2,1)S(1)} %multiply_convert_fusion.1) | copy-start | bytes 3076
  8.2 16.1 %all-to-all-start = ((bf16[16,8,544]{2,1,0:T(8,128)(2,1)}), bf16[16,8,544]{2,1,0:T(8,128)(2,1)S(1)}, u32[]{:S(2)}, u32[]{:S(2)}) async-start(bf16[16,8,544]{2,1,0:T(8,128)(2,1)} %broadcast_in_dim.63), calls=%async_computation | async-start | bytes 327680 | tf_op jit(solution)/shard_map/all_to_all | solution.py:20
  24.2 47.8 %copy-start.9 = (bf16[8,256]{1,0:T(8,128)(2,1)S(1)}, bf16[8,256]{1,0:T(8,128)(2,1)}, u32[]{:S(2)}) copy-start(bf16[8,256]{1,0:T(8,128)(2,1)} %constant_dynamic-slice_fusion.1) | copy-start | bytes 12292
  24.2 48.1 %copy-start.11 = (f32[1,256]{1,0:T(1,128)S(1)}, f32[1,256]{1,0:T(1,128)}, u32[]{:S(2)}) copy-start(f32[1,256]{1,0:T(1,128)} %constant_dynamic-slice_fusion) | copy-start | bytes 3076
  121.4 33.9 %copy-start.5 = (f32[32,1,256]{2,0,1:T(8,128)S(1)}, f32[32,1,256]{2,0,1:T(8,128)}, u32[]{:S(2)}) copy-start(f32[32,1,256]{2,0,1:T(8,128)} %reshape_squeeze.11) | copy-start | bytes 98308
  121.5 1.0 copy-start.1
  126.6 30.9 %copy-start.4 = (bf16[2,64,544]{2,1,0:T(8,128)(2,1)S(1)}, bf16[2,64,544]{2,1,0:T(8,128)(2,1)}, u32[]{:S(2)}) copy-start(bf16[2,64,544]{2,1,0:T(8,128)(2,1)} %param.24) | copy-start | bytes 417796
  155.1 29.4 %copy-start.15 = (f32[64]{0:T(128)S(1)}, f32[64]{0:T(128)}, u32[]{:S(2)}) copy-start(f32[64]{0:T(128)} %get-tuple-element.57) | copy-start | bytes 772
  155.3 30.2 %copy-start.7 = (f32[16,64]{1,0:T(8,128)S(1)}, f32[16,64]{1,0:T(8,128)}, u32[]{:S(2)}) copy-start(f32[16,64]{1,0:T(8,128)} %get-tuple-element.58) | copy-start | bytes 12292
  155.4 30.8 %copy-start.14 = (f32[64]{0:T(128)S(1)}, f32[64]{0:T(128)}, u32[]{:S(2)}) copy-start(f32[64]{0:T(128)} %get-tuple-element.60) | copy-start | bytes 772

commit v3 on v1

v3 whole, which is shorter than its diff:
```python
import functools

import jax
import jax.numpy as jnp
from jax import lax
from jax.experimental import pallas as pl
from jax.experimental.pallas import tpu as pltpu
from jax.sharding import Mesh
from jax.sharding import PartitionSpec as P

ALL = ("z", "x", "y", "core")
SEQ = ("z", "x")
SEQ_SUM = ("x", "z")
CHAN = ("y", "core")
CHAN_SUM = ("core", "y")
PLANE = ("x", "y")
LINE = ("core", "z")
WIRE = jnp.bfloat16
F32 = jnp.float32

norm_eps = 1e-06
lowest_score = -1e30


def exchange(copies, axes):
    return lax.all_to_all(copies, axes, split_axis=0, concat_axis=0, tiled=True)


def copied(x, axes):
    return jnp.broadcast_to(x, (lax.axis_size(axes), *x.shape))


def whole(shape):
    return pl.BlockSpec(shape, lambda _: (0,) * len(shape))


def layer_of(shape, layer):
    return pl.BlockSpec((1, *shape[1:]), lambda _: (layer,) + (0,) * (len(shape) - 1))


def local_call(body, inputs, outputs, scratch=(), aliases={}):
    def spec(shape, layer):
        if layer in ("far", "scalar"):
            return pl.BlockSpec(memory_space=pltpu.HBM if layer == "far" else pltpu.SMEM)
        return whole(shape) if layer is None else layer_of(shape, layer)

    return pl.pallas_call(
        body,
        grid=(1,),
        in_specs=[spec(x.shape, layer) for x, layer in inputs],
        out_specs=[spec(shape, layer) for shape, _, layer in outputs],
        out_shape=[jax.ShapeDtypeStruct(shape, dtype) for shape, dtype, _ in outputs],
        scratch_shapes=list(scratch),
        input_output_aliases=aliases,
        compiler_params=pltpu.CompilerParams(vmem_limit_bytes=12 * 1024 * 1024),
    )(*[x for x, _ in inputs])


def silu(x):
    return x * lax.logistic(x)


def added_up(ref):
    total = ref[0].astype(F32)
    for k in range(1, ref.shape[0]):
        total = total + ref[k].astype(F32)
    return total


def store_copies(ref, x):
    for k in range(ref.shape[0]):
        ref[k] = x


def against_rows(a, b):
    return lax.dot_general(a, b, (((1,), (1,)), ((), ())), preferred_element_type=F32)


def mamba_in_body(layer, *refs):
    refs = list(refs)
    stream_ref, gain_ref, in_ref, taps_ref, bias_ref, past_ref, xproj_ref = refs[:7]
    terms_ref, signal_ref, gate_ref, conv_ref, normed_ref, held_ref, done = refs[-7:]
    dim = normed_ref.shape[1]
    pieces = done.shape[0]
    piece = dim // pieces
    copies = [
        pltpu.make_async_copy(
            in_ref.at[layer, :, :, pl.ds(k * piece, piece)],
            held_ref.at[:, :, pl.ds(k * piece, piece)],
            done.at[k],
        )
        for k in range(pieces)
    ]
    for copy in copies:
        copy.start()
    gain_row = (0, None, 2)[2 * layer]
    if len(stream_ref.shape) == 2:
        x = stream_ref[...].astype(F32)
        inv_rms = lax.rsqrt(jnp.sum(x * x, axis=1, keepdims=True) / dim + norm_eps)
        normed_ref[...] = (x * inv_rms * gain_ref[gain_row : gain_row + 1, :]).astype(jnp.bfloat16)
    else:
        blocks, _, width = stream_ref.shape
        squares = jnp.zeros(stream_ref.shape[1:], F32)
        for k in range(blocks):
            x = stream_ref[k].astype(F32)
            squares = squares + x * x
        inv_rms = lax.rsqrt(jnp.sum(squares, axis=1, keepdims=True) / dim + norm_eps)
        for k in range(blocks):
            cols = slice(k * width, (k + 1) * width)
            normed_ref[:, cols] = (
                stream_ref[k].astype(F32) * inv_rms * gain_ref[gain_row : gain_row + 1, cols]
            ).astype(jnp.bfloat16)
    inputs = jnp.zeros(signal_ref.shape, F32)
    gates = jnp.zeros(signal_ref.shape, F32)
    for k, copy in enumerate(copies):
        copy.wait()
        cols = slice(k * piece, (k + 1) * piece)
        normed = normed_ref[:, cols]
        inputs = inputs + against_rows(normed, held_ref[0, :, cols])
        gates = gates + against_rows(normed, held_ref[1, :, cols])
    inputs = inputs.astype(jnp.bfloat16)
    gates = gates.astype(jnp.bfloat16)
    taps = taps_ref[0]
    conv_sum = inputs.astype(F32) * taps[3:4]
    for k in range(3):
        conv_sum = conv_sum + past_ref[0, k].astype(F32) * taps[k : k + 1]
    signal = silu(conv_sum + bias_ref[layer : layer + 1, :]).astype(jnp.bfloat16)
    terms = jnp.dot(signal, xproj_ref[0], preferred_element_type=F32)
    store_copies(terms_ref, terms.astype(WIRE))
    signal_ref[...] = signal.astype(F32)
    gate_ref[...] = silu(gates.astype(F32))
    conv_ref[0, 0] = past_ref[0, 1]
    conv_ref[0, 1] = past_ref[0, 2]
    conv_ref[0, 2] = inputs


def mamba_in(stream, layer, norm_gain, in_rows, conv_weight, conv_bias, past, xproj_weight, conv_so_far):
    requests = past.shape[2]
    channels = past.shape[3]
    inputs = [
        (stream, None),
        (norm_gain, None),
        (in_rows, "far"),
        (conv_weight, layer),
        (conv_bias, None),
        (past, layer),
        (xproj_weight, layer),
    ]
    aliases = {}
    if conv_so_far is not None:
        aliases = {len(inputs): 3}
        inputs.append((conv_so_far, "far"))
    terms, signal, gate, conv = local_call(
        functools.partial(mamba_in_body, layer),
        inputs,
        [
            ((lax.axis_size(PLANE), requests, xproj_weight.shape[2]), WIRE, None),
            ((requests, channels), F32, None),
            ((requests, channels), F32, None),
            (past.shape, jnp.bfloat16, layer),
        ],
        [
            pltpu.VMEM((requests, in_rows.shape[3]), jnp.bfloat16),
            pltpu.VMEM(in_rows.shape[1:], jnp.bfloat16),
            pltpu.SemaphoreType.DMA((4,)),
        ],
        aliases,
    )
    return terms, signal, gate, conv


def mamba_out_body(layer, order, *refs):
    arrived_ref, signal_ref, gate_ref, dt_ref, bias_ref, decay_ref, skip_ref, state_ref, out_ref = (
        refs[:9]
    )
    blocks_ref, fresh_ref = refs[-2:]
    mapped = added_up(arrived_ref)
    low_rank = dt_ref.shape[2]
    states = decay_ref.shape[1]
    low = mapped[:, :low_rank].astype(jnp.bfloat16)
    raw = against_rows(low, dt_ref[0]) + bias_ref[layer : layer + 1, :]
    step = jnp.maximum(raw, 0.0) + jnp.log1p(jnp.exp(-jnp.abs(raw)))
    signal = signal_ref[...]
    pushed = step * signal
    rates = jnp.exp(decay_ref[0])
    rest = mapped[:, low_rank:]
    eye = lax.broadcasted_iota(jnp.int32, (states, states), 0) == lax.broadcasted_iota(
        jnp.int32, (states, states), 1
    )

    def column(row):
        return jnp.sum(jnp.where(eye, row, 0.0), axis=1, keepdims=True)

    readouts = []
    for b in range(mapped.shape[0]):
        b_in = column(rest[b : b + 1, :states])
        c_out = column(rest[b : b + 1, states : 2 * states])
        fresh = (
            jnp.exp(-step[b : b + 1] * rates) * state_ref[0, b] + pushed[b : b + 1] * b_in
        )
        fresh_ref[0, b] = fresh
        readouts.append(jnp.sum(fresh * c_out, axis=0, keepdims=True))
    readout = jnp.concatenate(readouts, axis=0) + skip_ref[layer : layer + 1, :] * signal
    gated = (readout * gate_ref[...]).astype(jnp.bfloat16)
    width = blocks_ref.shape[2]
    for place, block in enumerate(order):
        blocks_ref[place] = jnp.dot(
            gated,
            out_ref[0, :, block * width : (block + 1) * width],
            preferred_element_type=F32,
        ).astype(WIRE)


def mamba_out(arrived, signal, gate, layer, dt_rows, dt_bias, a_log, skip_gain, ssm_state, out_weight, so_far):
    far, near = (lax.axis_size(axis) for axis in SEQ_SUM)
    order = [k * far + j for j in range(far) for k in range(near)]
    inputs = [
        (arrived, None),
        (signal, None),
        (gate, None),
        (dt_rows, layer),
        (dt_bias, None),
        (a_log, layer),
        (skip_gain, None),
        (ssm_state, layer),
        (out_weight, layer),
    ]
    aliases = {}
    if so_far is not None:
        aliases = {len(inputs): 1}
        inputs.append((so_far, "far"))
    blocks, fresh = local_call(
        functools.partial(mamba_out_body, layer, order),
        inputs,
        [
            ((far * near, signal.shape[0], out_weight.shape[2] // (far * near)), WIRE, None),
            (ssm_state.shape, F32, layer),
        ],
        (),
        aliases,
    )
    arrived = exchange(blocks, SEQ_SUM)
    own = jnp.sum(arrived.astype(F32), axis=0).astype(WIRE)
    return exchange(copied(own, CHAN_SUM), CHAN_SUM), fresh


def two_parts(x):
    high = x.astype(WIRE).astype(F32)
    return high, x - high


def questions_body(arrived_ref, hidden_ref, gain_ref, matrix_ref, stream_ref, terms_ref):
    width = stream_ref.shape[1]
    first = pl.multiple_of(seq_index() * width, width)
    stream = (hidden_ref[:, pl.ds(first, width)].astype(F32) + added_up(arrived_ref)).astype(
        jnp.bfloat16
    )
    stream_ref[...] = stream
    wide = stream.astype(F32)
    high, low = two_parts(jnp.sum(wide * wide, axis=1, keepdims=True))
    scaled = (wide * gain_ref[1:2, pl.ds(first, width)]).astype(jnp.bfloat16)
    terms = jnp.dot(scaled, matrix_ref[...], preferred_element_type=F32)
    lane = lax.broadcasted_iota(jnp.int32, (stream.shape[0], 128), 1)
    notes = jnp.where(lane == 0, high, jnp.where(lane == 1, low, 0.0))
    entries = terms.shape[1]
    for k in range(terms_ref.shape[0]):
        terms_ref[k, :, :entries] = terms.astype(WIRE)
        terms_ref[k, :, entries:] = notes.astype(WIRE)


def seq_index():
    return lax.axis_index("z") * lax.axis_size("x") + lax.axis_index("x")


def flip(x):
    n = max(x.shape)
    eye = lax.broadcasted_iota(jnp.int32, (n, n), 0) == lax.broadcasted_iota(jnp.int32, (n, n), 1)
    return jnp.sum(jnp.where(eye, x, 0.0), axis=x.shape.index(n), keepdims=True)


def store_part(out_ref, top, total, mixed):
    rows, width = mixed.shape
    high, low = two_parts(top)
    pad = jnp.zeros((1, width - rows), F32)
    notes = [jnp.concatenate([v, pad], axis=1) for v in (high, low, total)]
    notes = jnp.concatenate([*notes, jnp.zeros((out_ref.shape[1] - rows - 3, width), F32)], axis=0)
    for k in range(out_ref.shape[0]):
        out_ref[k, :rows, :] = mixed.astype(WIRE)
        out_ref[k, rows:, :] = notes.astype(WIRE)


def merged(arrived_ref):
    parts, stored, _ = arrived_ref.shape
    rows = stored - 8
    notes = [arrived_ref[k, rows:, :].astype(F32) for k in range(parts)]
    tops = [v[0:1, :rows] + v[1:2, :rows] for v in notes]
    top = tops[0]
    for v in tops[1:]:
        top = jnp.maximum(top, v)
    total = jnp.zeros_like(top)
    mixed = jnp.zeros((rows, arrived_ref.shape[2]), F32)
    for k in range(parts):
        scale = jnp.exp(tops[k] - top)
        total = total + scale * notes[k][2:3, :rows]
        mixed = mixed + flip(scale) * arrived_ref[k, :rows, :].astype(F32)
    return top, total, mixed


def attention_body(
    arrived_ref, kv_ref, lengths_ref, table_ref, part_ref, pair_ref, questions_ref, scores_ref, *, block_len, dim
):
    summed = added_up(arrived_ref)
    requests = summed.shape[0]
    width = kv_ref.shape[1]
    entries = summed.shape[1] - 128
    group_size = entries // width - 2
    rows = requests * group_size
    tokens = kv_ref.shape[0]
    chunk = 2 * block_len
    inv_rms = lax.rsqrt((summed[:, entries : entries + 1] + summed[:, entries + 1 : entries + 2]) / dim + norm_eps)
    qkv = (summed[:, :entries] * inv_rms).astype(jnp.bfloat16)
    fresh = qkv[:, group_size * width :]
    fresh = fresh.astype(F32)
    pair_ref[...] = fresh
    fresh_scores = []
    for g in range(group_size):
        one = qkv[:, g * width : (g + 1) * width]
        questions_ref[g * requests : (g + 1) * requests, :] = one.astype(F32)
        fresh_scores.append(jnp.sum(one.astype(F32) * fresh[:, :width], axis=1, keepdims=True))
    questions = questions_ref[...].astype(jnp.bfloat16)
    inv_sqrt = width ** (-0.5)
    is_first = seq_index() == 0
    fresh_score = jnp.where(is_first, jnp.concatenate(fresh_scores, axis=0) * inv_sqrt, lowest_score)
    first_slot = seq_index() * (tokens // chunk)
    table = table_ref[...]
    row = lax.broadcasted_iota(jnp.int32, table.shape, 0)
    lengths = jnp.zeros(table.shape, jnp.int32)
    for b in range(requests):
        lengths = jnp.where(row == b, lengths_ref[b], lengths)
    left = jnp.clip(
        lengths - lax.broadcasted_iota(jnp.int32, table.shape, 1) * block_len, 0, block_len
    )
    place = lax.broadcasted_iota(jnp.int32, (requests, chunk), 1)
    limit = jnp.where(place % 2 == 0, place // 2, block_len)
    top = fresh_score
    hidden_from = []
    for k in range(tokens // chunk):
        filled = jnp.sum(jnp.where(table == first_slot + k, left, 0), axis=1, keepdims=True)
        visible = jnp.concatenate([(limit < filled).astype(F32)] * group_size, axis=0) > 0.5
        hidden_from.append(visible)
        scores = against_rows(questions, kv_ref[k * chunk : (k + 1) * chunk, :]) * inv_sqrt
        scores = jnp.where(visible, scores, lowest_score)
        scores_ref[:, k * chunk : (k + 1) * chunk] = scores
        top = jnp.maximum(top, jnp.max(scores, axis=1, keepdims=True))
    high, low = two_parts(top)
    top = high + low.astype(WIRE).astype(F32)
    weight = jnp.where(is_first, jnp.exp(fresh_score - top), 0.0)
    total = weight
    values = jnp.concatenate([fresh[:, width:]] * group_size, axis=0)
    mixed = weight * values
    for k in range(tokens // chunk):
        weight = jnp.where(
            hidden_from[k], jnp.exp(scores_ref[:, k * chunk : (k + 1) * chunk] - top), 0.0
        )
        total = total + jnp.sum(weight, axis=1, keepdims=True)
        moved = pltpu.roll(weight, 1, 1).astype(jnp.bfloat16)
        mixed = mixed + jnp.dot(moved, kv_ref[k * chunk : (k + 1) * chunk, :], preferred_element_type=F32)
    store_part(part_ref, flip(top), flip(total), mixed)


def merge_body(arrived_ref, part_ref):
    top, total, mixed = merged(arrived_ref)
    store_part(part_ref, top, total, mixed)


def attention_out_body(arrived_ref, weight_ref, sums_ref):
    _, total, mixed = merged(arrived_ref)
    attended = (mixed / flip(total)).astype(jnp.bfloat16)
    requests = sums_ref.shape[1]
    width = attended.shape[1]
    result = jnp.zeros(sums_ref.shape[1:], F32)
    for g in range(attended.shape[0] // requests):
        result = result + jnp.dot(
            attended[g * requests : (g + 1) * requests],
            weight_ref[g * width : (g + 1) * width, :],
            preferred_element_type=F32,
        )
    store_copies(sums_ref, result.astype(WIRE))


def last_body(arrived_ref, stream_ref, fresh_ref, out_ref, pair_ref):
    head = pair_ref.shape[3]
    for b in range(pair_ref.shape[0]):
        pair_ref[b, 0] = jnp.concatenate(
            [fresh_ref[b : b + 1, :head], fresh_ref[b : b + 1, head:]], axis=0
        ).astype(jnp.bfloat16)
    result = (stream_ref[...].astype(F32) + added_up(arrived_ref)).astype(jnp.bfloat16)
    place = lax.axis_index("y") * lax.axis_size("core") + lax.axis_index("core")
    width = out_ref.shape[1]
    result = result.astype(F32)
    own = result[:, :width]
    for k in range(1, result.shape[1] // width):
        own = jnp.where(place == k, result[:, k * width : (k + 1) * width], own)
    out_ref[...] = own.astype(jnp.bfloat16)


def shards(
    hidden,
    norm_gain,
    in_weight,
    conv_weight,
    conv_bias,
    conv_state,
    xproj_weight,
    dt_weight,
    dt_bias,
    a_log,
    skip_gain,
    ssm_state,
    out_weight,
    asker_lookup_matrix,
    o_weight,
    kv_cache,
    lengths,
    page_table,
):
    requests, model_dim = hidden.shape
    block_cols = model_dim // lax.axis_size(SEQ)
    share_cols = block_cols // lax.axis_size(CHAN)
    pages_dev, block_len, pair, _, width = kv_cache.shape
    entries = asker_lookup_matrix.shape[2]
    rows = requests * (entries // width - 2)
    in_rows = pltpu.with_memory_space_constraint(in_weight.transpose(0, 2, 3, 1), pltpu.HBM)
    dt_rows = dt_weight.transpose(0, 2, 1)
    past = conv_state.transpose(0, 2, 1, 3)
    kv_rows = kv_cache.reshape(pages_dev * block_len * pair, width)
    conv_args = (conv_weight, conv_bias, past, xproj_weight)
    state_args = (dt_rows, dt_bias, a_log, skip_gain, ssm_state, out_weight)

    def sums_of_proj(terms):
        own = jnp.sum(exchange(terms, PLANE).astype(F32), axis=0).astype(WIRE)
        return exchange(copied(own, LINE), LINE)

    terms, signal, gate, new_conv = mamba_in(hidden, 0, norm_gain, in_rows, *conv_args, None)
    arrived, new_ssm = mamba_out(sums_of_proj(terms), signal, gate, 0, *state_args, None)
    stream_one, terms = local_call(
        questions_body,
        [
            (arrived, None),
            (hidden, None),
            (norm_gain, None),
            (asker_lookup_matrix.reshape(block_cols, entries), None),
        ],
        [
            ((requests, block_cols), jnp.bfloat16, None),
            ((lax.axis_size("x"), requests, entries + 128), WIRE, None),
        ],
    )
    own = jnp.sum(exchange(terms, "x").astype(F32), axis=0).astype(WIRE)
    part, fresh = local_call(
        functools.partial(attention_body, block_len=block_len, dim=model_dim),
        [
            (exchange(copied(own, "z"), "z"), None),
            (kv_rows, None),
            (lengths, "scalar"),
            (page_table, None),
        ],
        [
            ((lax.axis_size("x"), rows + 8, width), WIRE, None),
            ((requests, 2 * width), F32, None),
        ],
        [pltpu.VMEM((rows, width), F32), pltpu.VMEM((rows, kv_rows.shape[0]), F32)],
    )
    (part,) = local_call(
        merge_body,
        [(exchange(part, "x"), None)],
        [((lax.axis_size("z"), rows + 8, width), WIRE, None)],
    )
    (sums,) = local_call(
        attention_out_body,
        [(exchange(part, "z"), None), (o_weight[0], None)],
        [((lax.axis_size(CHAN), requests, block_cols), WIRE, None)],
    )
    added = jnp.sum(exchange(sums, CHAN_SUM).astype(F32), axis=0)
    stream_two = (stream_one.astype(F32) + added).astype(jnp.bfloat16)
    terms, signal, gate, new_conv = mamba_in(
        exchange(copied(stream_two, SEQ), SEQ), 1, norm_gain, in_rows, *conv_args, new_conv
    )
    arrived, new_ssm = mamba_out(sums_of_proj(terms), signal, gate, 1, *state_args, new_ssm)
    hidden_out, newest_pair = local_call(
        last_body,
        [(arrived, None), (stream_two, None), (fresh, None)],
        [
            ((requests, share_cols), jnp.bfloat16, None),
            ((requests, 1, 2, width), jnp.bfloat16, None),
        ],
    )
    return hidden_out, new_ssm, new_conv.transpose(0, 2, 1, 3), newest_pair


def solution(mesh):
    split = Mesh(mesh.devices.reshape(8, 4, 4, 2), ALL)
    placed = (
        P(),
        P(),
        P(None, None, None, ALL),
        P(None, None, ALL),
        P(None, ALL),
        P(None, None, None, ALL),
        P(None, ALL, None),
        P(None, None, ALL),
        P(None, ALL),
        P(None, None, ALL),
        P(None, ALL),
        P(None, None, None, ALL),
        P(None, ALL, None),
        P(SEQ, CHAN, None),
        P(CHAN, None, SEQ),
        P(SEQ, None, None, CHAN, None),
        P(),
        P(),
    )
    return jax.shard_map(
        shards,
        mesh=split,
        in_specs=placed,
        out_specs=(
            P(None, ALL),
            P(None, None, None, ALL),
            P(None, None, None, ALL),
            P(None, CHAN, None, None),
        ),
        check_vma=False,
    )
```

time: 209 us -> 188 us (0.90)
  blocking collectives: 20.3 us -> 164 us
  waiting for transfers between devices: 90.1 us -> 0 us
  starting transfers between devices: 56.5 us -> 0 us
  local copies, waits for them, and re-layouts: 21.1 us -> 9.91 us
  Pallas kernels: 0 us -> 10.6 us
  matrix products: 10.5 us -> 0 us
  other arithmetic: 7.72 us -> 1.97 us
    all_to_all x2 -> x14, blocking collectives: 20.3 us -> 164 us  [exchange(): return lax.all_to_all(copies, axes, split_axis=0, concat_axis=0, tiled=True)]
    all_to_all x10 -> x0, waiting for transfers between devices: 90.1 us -> none  [the longest x8 71.1 us: copy_for_each(): return lax.all_to_all(copies, axes, split_axis=0, concat_axis=0, tiled=True)]
    all_to_all x10 -> x0, starting transfers between devices: 56.5 us -> none  [the longest x8 48.8 us: copy_for_each(): return lax.all_to_all(copies, axes, split_axis=0, concat_axis=0, tiled=True)]
    pallas_call x0 -> x9, Pallas kernels: none -> 10.6 us  [local_call(): pl.pallas_call(body, grid=(1,), in_specs=[spec(x.shape, layer) for x, lay...]
    dot_general x12 -> x0, matrix products: 10.5 us -> none  [the longest x2 4.42 us: mix_out(): jnp.dot(gated_out, out_weight[layer], preferred_element_type=jnp.float32)]
    slice x6 -> x0, local copies, waits for them, and re-layouts: 7.11 us -> none  [the longest x1 4.18 us: local_attention(): values = kv_cache[:, :, 1, 0].reshape(pages_dev * block_len, width)]
    broadcast_in_dim x13 -> x6, local copies, waits for them, and re-layouts: 5.76 us -> 0.07 us  [copied(): return jnp.broadcast_to(x, (lax.axis_size(axes), *x.shape))]
    unnamed x69 -> x50, local copies, waits for them, and re-layouts: 4.95 us -> 9.84 us
  transfers between devices with their start and end apart: 10 -> 0, of which waited for: 10 -> 0; matrix products, arithmetic and copies ran while one was open for 5% -> 0% of each run, Pallas kernels for 0% -> 0%
where the time goes in v3:
time: 188 us; the launch traced here: 187 us
  blocking collectives  164 us (87%)
  Pallas kernels  10.6 us (6%)
  local copies, waits for them, and re-layouts  9.91 us (5%)
  other arithmetic  1.97 us (1%)
    all_to_all x14, blocking collectives, exchange(): return lax.all_to_all(copies, axes, split_axis=0, concat_axis=0, tiled=True)  164 us
    pallas_call x9, Pallas kernels, local_call(): pl.pallas_call(body, grid=(1,), in_specs=[spec(x.shape, layer) for x, lay...  10.6 us
    unnamed x50, local copies, waits for them, and re-layouts  9.84 us

profile of v3, /device:TPU:1, one launch (start us, length us, event | category | flops | bytes accessed | tf_op | source)
XLA Modules:
  0.0 186.8 jit_solution(17736946630051373047)
XLA Ops:
  0.6 0.0 copy-start
  0.7 1.0 copy-done.1
  1.7 0.9 copy-done.4
  2.6 0.9 copy-done.12
  3.5 0.7 copy-done.15
  4.2 0.7 copy-done.17
  4.9 0.7 copy-done.20
  5.6 2.7 %shard_map.201 = (bf16[16,8,544]{2,1,0:T(8,128)(2,1)S(1)}, f32[8,64]{1,0:T(8,128)S(1)}, f32[8,64]{1,0:T(8,128)S(1)}, bf16[2,3,8,64]{3,2,1,0:T(8,128)(2,1)}) custom-call(bf16[8,8192]{1,0:T(8,128)(2,1)S(1)} %copy-done.12, f32[3,8192]{1,0:T(4,128)S(1)} %copy-done.1, bf16[2,2,64,8192]{3,2,1,0:T(8,128)(2,1)} %bitcast.14, f32[2,4,64]{2,1,0:T(4,128)S(1)} %copy-done.17, ...), custom_call_target="tpu_custom_call" | custom-call | tf_op jit(solution)/shard_map/pallas_call | solution.py:47
  8.3 14.4 %all_to_all.70 = bf16[16,8,544]{2,1,0:T(8,128)(2,1)S(1)} all-to-all(bf16[16,8,544]{2,1,0:T(8,128)(2,1)S(1)} %get-tuple-element.22), channel_id=1, replica_groups=mesh['z'=8,'x'=4,'y'=4,'core'=2] {'x','y'}, dimensions={0} | all-to-all | bytes 278528 | tf_op jit(solution)/shard_map/all_to_all | solution.py:26
  22.8 0.0 copy-start.5
  22.8 0.0 copy-start.16
  22.8 0.0 copy-start.18
  22.8 0.0 copy-start.21
  22.8 18.2 %all_to_all.71.refs_0_ = bf16[16,8,544]{2,1,0:T(8,128)(2,1)S(1)} all-to-all(bf16[16,8,544]{2,1,0:T(8,128)(2,1)S(1)} %broadcast_in_dim.18), channel_id=1, replica_groups=mesh['z'=8,'x'=4,'y'=4,'core'=2] {'core','z'}, dimensions={0} | all-to-all | bytes 278528 | tf_op jit(solution)/shard_map/all_to_all | solution.py:26
  41.0 0.0 copy-start.7
  41.0 0.9 copy-done.7
  41.9 0.9 copy-done.9
  42.8 0.8 shard_map.202
  43.7 13.8 %all_to_all.72 = bf16[32,8,256]{2,1,0:T(8,128)(2,1)} all-to-all(bf16[32,8,256]{2,1,0:T(8,128)(2,1)S(1)} %get-tuple-element.25), channel_id=1, replica_groups=mesh['z'=8,'x'=4,'y'=4,'core'=2] {'x','z'}, dimensions={0} | all-to-all | bytes 262144 | tf_op jit(solution)/shard_map/all_to_all | solution.py:26
  57.4 0.9 reduce_sum.70
  58.4 9.6 %all_to_all.73.arrived_ref = bf16[8,8,256]{2,1,0:T(8,128)(2,1)S(1)} all-to-all(bf16[8,8,256]{2,1,0:T(8,128)(2,1)S(1)} %broadcast_in_dim.19), channel_id=1, replica_groups=mesh['z'=8,'x'=4,'y'=4,'core'=2] {'core','y'}, dimensions={0} | all-to-all | bytes 65536 | tf_op jit(solution)/shard_map/all_to_all | solution.py:26
  68.0 0.0 copy-done.2
  68.0 1.1 copy-done.6
  69.1 0.9 copy-done.13
  70.0 0.2 shard_map.203
  70.2 7.7 %all_to_all.74 = bf16[4,8,1408]{2,1,0:T(8,128)(2,1)} all-to-all(bf16[4,8,1408]{2,1,0:T(8,128)(2,1)S(1)} %get-tuple-element.27), channel_id=1, replica_groups=mesh['z'=8,'x'=4,'y'=4,'core'=2] {'x'}, dimensions={0} | all-to-all | bytes 180224 | tf_op jit(solution)/shard_map/all_to_all | solution.py:26
  77.9 0.9 reduce_sum.71
  78.8 10.9 %all_to_all.75.arrived_ref = bf16[8,8,1408]{2,1,0:T(8,128)(2,1)S(1)} all-to-all(bf16[8,8,1408]{2,1,0:T(8,128)(2,1)S(1)} %broadcast_in_dim.20), channel_id=1, replica_groups=mesh['z'=8,'x'=4,'y'=4,'core'=2] {'z'}, dimensions={0} | all-to-all | bytes 360448 | tf_op jit(solution)/shard_map/all_to_all | solution.py:26
  89.7 0.0 copy-done.3
  89.7 1.8 shard_map.204
  91.5 0.0 copy-start.8
  91.5 0.0 copy-start.10
  91.5 7.0 %all_to_all.76.arrived_ref = bf16[4,72,128]{2,1,0:T(8,128)(2,1)S(1)} all-to-all(bf16[4,72,128]{2,1,0:T(8,128)(2,1)S(1)} %get-tuple-element.28), channel_id=1, replica_groups=mesh['z'=8,'x'=4,'y'=4,'core'=2] {'x'}, dimensions={0} | all-to-all | bytes 147456 | tf_op jit(solution)/shard_map/all_to_all | solution.py:26
  98.6 0.1 shard_map.205
  98.7 10.5 %all_to_all.77.arrived_ref = bf16[8,72,128]{2,1,0:T(8,128)(2,1)S(1)} all-to-all(bf16[8,72,128]{2,1,0:T(8,128)(2,1)S(1)} %shard_map.205), channel_id=1, replica_groups=mesh['z'=8,'x'=4,'y'=4,'core'=2] {'z'}, dimensions={0} | all-to-all | bytes 294912 | tf_op jit(solution)/shard_map/all_to_all | solution.py:26
  109.2 1.0 copy-done.11
  110.2 0.3 shard_map.206
  110.5 12.3 %all_to_all.78 = bf16[8,8,256]{2,1,0:T(8,128)(2,1)S(1)} all-to-all(bf16[8,8,256]{2,1,0:T(8,128)(2,1)S(1)} %shard_map.206), channel_id=1, replica_groups=mesh['z'=8,'x'=4,'y'=4,'core'=2] {'core','y'}, dimensions={0} | all-to-all | bytes 65536 | tf_op jit(solution)/shard_map/all_to_all | solution.py:26
  122.9 12.7 %all_to_all.79.refs_0_ = bf16[32,8,256]{2,1,0:T(8,128)(2,1)S(1)} all-to-all(bf16[32,8,256]{2,1,0:T(8,128)(2,1)S(1)} %broadcast_in_dim.21), channel_id=1, replica_groups=mesh['z'=8,'x'=4,'y'=4,'core'=2] {'z','x'}, dimensions={0} | all-to-all | bytes 262144 | tf_op jit(solution)/shard_map/all_to_all | solution.py:26
  135.7 0.0 copy-done.21
  135.7 2.5 %shard_map.207 = (bf16[16,8,544]{2,1,0:T(8,128)(2,1)S(1)}, f32[8,64]{1,0:T(8,128)S(1)}, f32[8,64]{1,0:T(8,128)S(1)}, bf16[2,3,8,64]{3,2,1,0:T(8,128)(2,1)}) custom-call(bf16[32,8,256]{2,1,0:T(8,128)(2,1)S(1)} %all_to_all.79.refs_0_, f32[3,8192]{1,0:T(4,128)S(1)} %copy-done.2, bf16[2,2,64,8192]{3,2,1,0:T(8,128)(2,1)} %bitcast.15, ...), custom_call_target="tpu_custom_call", output_to_operand_aliasing={{3}: (7, {})} | custom-call | tf_op jit(solution)/shard_map/pallas_call | solution.py:47
  138.2 9.7 %all_to_all.80 = bf16[16,8,544]{2,1,0:T(8,128)(2,1)S(1)} all-to-all(bf16[16,8,544]{2,1,0:T(8,128)(2,1)S(1)} %get-tuple-element.30), channel_id=1, replica_groups=mesh['z'=8,'x'=4,'y'=4,'core'=2] {'x','y'}, dimensions={0} | all-to-all | bytes 278528 | tf_op jit(solution)/shard_map/all_to_all | solution.py:26
  148.0 13.3 %all_to_all.81.refs_0_ = bf16[16,8,544]{2,1,0:T(8,128)(2,1)S(1)} all-to-all(bf16[16,8,544]{2,1,0:T(8,128)(2,1)S(1)} %broadcast_in_dim.22), channel_id=1, replica_groups=mesh['z'=8,'x'=4,'y'=4,'core'=2] {'core','z'}, dimensions={0} | all-to-all | bytes 278528 | tf_op jit(solution)/shard_map/all_to_all | solution.py:26
  161.3 0.0 copy-done.8
  161.3 1.0 shard_map.208
  162.2 13.8 %all_to_all.82 = bf16[32,8,256]{2,1,0:T(8,128)(2,1)S(1)} all-to-all(bf16[32,8,256]{2,1,0:T(8,128)(2,1)S(1)} %get-tuple-element.34), channel_id=1, replica_groups=mesh['z'=8,'x'=4,'y'=4,'core'=2] {'x','z'}, dimensions={0} | all-to-all | bytes 262144 | tf_op jit(solution)/shard_map/all_to_all | solution.py:26
  176.1 9.6 %all_to_all.83.arrived_ref = bf16[8,8,256]{2,1,0:T(8,128)(2,1)S(1)} all-to-all(bf16[8,8,256]{2,1,0:T(8,128)(2,1)S(1)} %broadcast_in_dim.23), channel_id=1, replica_groups=mesh['z'=8,'x'=4,'y'=4,'core'=2] {'core','y'}, dimensions={0} | all-to-all | bytes 65536 | tf_op jit(solution)/shard_map/all_to_all | solution.py:26
  185.7 1.1 shard_map.209
  (38 shorter events, 0.2 us)
Async XLA Ops:
  0.6 40.4 %copy-start = (bf16[2,64,8192]{2,1,0:T(8,128)(2,1)S(1)}, bf16[2,64,8192]{2,1,0:T(8,128)(2,1)}, u32[]{:S(2)}) copy-start(bf16[2,64,8192]{2,1,0:T(8,128)(2,1)} %refs_8_.3) | copy-start | bytes 6291460
  0.6 1.1 copy-start.1
  1.7 0.9 copy-start.4
  2.6 0.9 copy-start.12
  3.5 0.7 copy-start.15
  4.2 0.7 copy-start.17
  4.9 0.7 copy-start.20
  5.6 35.4 %copy-start.14 = (f32[2,16,64]{2,1,0:T(8,128)S(1)}, f32[2,16,64]{2,1,0:T(8,128)}, u32[]{:S(2)}) copy-start(f32[2,16,64]{2,1,0:T(8,128)} %refs_5_.3) | copy-start | bytes 24580
  5.6 35.4 %copy-start.22 = (f32[2,64]{1,0:T(2,128)S(1)}, f32[2,64]{1,0:T(2,128)}, u32[]{:S(2)}) copy-start(f32[2,64]{1,0:T(2,128)} %refs_4_.7) | copy-start | bytes 1540
  5.6 35.4 %copy-start.23 = (f32[2,64]{1,0:T(2,128)S(1)}, f32[2,64]{1,0:T(2,128)}, u32[]{:S(2)}) copy-start(f32[2,64]{1,0:T(2,128)} %refs_6_.7) | copy-start | bytes 1540
  5.6 62.4 %copy-start.2 = (f32[3,8192]{1,0:T(4,128)S(1)}, f32[3,8192]{1,0:T(4,128)}, u32[]{:S(2)}) copy-start(f32[3,8192]{1,0:T(4,128)} %refs_1_.3) | copy-start | bytes 294916
  5.6 84.1 %copy-start.3 = (bf16[8,256,2,1,128]{4,2,3,1,0:T(2,128)(2,1)S(1)}, bf16[8,256,2,1,128]{4,2,3,1,0:T(2,128)(2,1)}, u32[]{:S(2)}) copy-start(bf16[8,256,2,1,128]{4,2,3,1,0:T(2,128)(2,1)} %param.33) | copy-start | bytes 3145732
  5.6 84.1 %copy-start.19 = (s32[8,32]{1,0:T(8,128)S(1)}, s32[8,32]{1,0:T(8,128)}, u32[]{:S(2)}) copy-start(s32[8,32]{1,0:T(8,128)} %table_ref.1) | copy-start | bytes 3076
  5.6 84.1 %copy-start.24 = (s32[8]{0:T(128)S(1)}, s32[8]{0:T(128)}, u32[]{:S(2)}) copy-start(s32[8]{0:T(128)} %lengths_ref.1) | copy-start | bytes 100
  22.8 112.9 %copy-start.5 = (bf16[2,64,544]{2,1,0:T(8,128)(2,1)S(1)}, bf16[2,64,544]{2,1,0:T(8,128)(2,1)}, u32[]{:S(2)}) copy-start(bf16[2,64,544]{2,1,0:T(8,128)(2,1)} %refs_6_.6) | copy-start | bytes 417796
  22.8 112.9 %copy-start.16 = (bf16[2,8,3,64]{3,1,2,0:T(8,128)(2,1)S(1)}, bf16[2,8,3,64]{3,1,2,0:T(8,128)(2,1)}, u32[]{:S(2)}) copy-start(bf16[2,8,3,64]{3,1,2,0:T(8,128)(2,1)} %param.23) | copy-start | bytes 18436
  22.8 112.9 %copy-start.18 = (f32[2,4,64]{2,1,0:T(4,128)S(1)}, f32[2,4,64]{2,1,0:T(4,128)}, u32[]{:S(2)}) copy-start(f32[2,4,64]{2,1,0:T(4,128)} %refs_3_.3) | copy-start | bytes 6148
  22.8 112.9 %copy-start.21 = (f32[2,64]{1,0:T(2,128)S(1)}, f32[2,64]{1,0:T(2,128)}, u32[]{:S(2)}) copy-start(f32[2,64]{1,0:T(2,128)} %refs_4_.6) | copy-start | bytes 1540
  41.0 0.9 copy-start.7
  41.9 0.9 copy-start.9
  68.0 1.1 copy-start.6
  69.1 0.9 copy-start.13
  91.5 69.8 %copy-start.8 = (bf16[2,512,64]{1,2,0:T(8,128)(2,1)S(1)}, bf16[2,512,64]{1,2,0:T(8,128)(2,1)}, u32[]{:S(2)}) copy-start(bf16[2,512,64]{1,2,0:T(8,128)(2,1)} %param.25) | copy-start | bytes 393220
  91.5 69.8 %copy-start.10 = (f32[2,8,16,64]{3,2,1,0:T(8,128)S(1)}, f32[2,8,16,64]{3,2,1,0:T(8,128)}, u32[]{:S(2)}) copy-start(f32[2,8,16,64]{3,2,1,0:T(8,128)} %refs_7_.3) | copy-start | bytes 196612
  109.2 1.0 copy-start.11

commit v4 on v3

--- a/solution.py
+++ b/solution.py
@@ -36,6 +36,10 @@
 
 def layer_of(shape, layer):
     return pl.BlockSpec((1, *shape[1:]), lambda _: (layer,) + (0,) * (len(shape) - 1))
+
+
+def far(x):
+    return pltpu.with_memory_space_constraint(x, pltpu.HBM)
 
 
 def local_call(body, inputs, outputs, scratch=(), aliases={}):
@@ -77,9 +81,9 @@
 
 
 def mamba_in_body(layer, *refs):
-    refs = list(refs)
     stream_ref, gain_ref, in_ref, taps_ref, bias_ref, past_ref, xproj_ref = refs[:7]
-    terms_ref, signal_ref, gate_ref, conv_ref, normed_ref, held_ref, done = refs[-7:]
+    normed_ref, held_ref, done = refs[-3:]
+    terms_ref, signal_ref, gate_ref, conv_ref = refs[7:11] if layer == 0 else refs[8:12]
     dim = normed_ref.shape[1]
     pieces = done.shape[0]
     piece = dim // pieces
@@ -93,6 +97,12 @@
     ]
     for copy in copies:
         copy.start()
+    if layer == 0:
+        own_ref, own_gain_ref = refs[11:13]
+        width = own_ref.shape[1]
+        first = pl.multiple_of(seq_index() * width, width)
+        own_ref[...] = stream_ref[:, pl.ds(first, width)]
+        own_gain_ref[...] = gain_ref[1:2, pl.ds(first, width)]
     gain_row = (0, None, 2)[2 * layer]
     if len(stream_ref.shape) == 2:
         x = stream_ref[...].astype(F32)
@@ -134,7 +144,9 @@
     conv_ref[0, 2] = inputs
 
 
-def mamba_in(stream, layer, norm_gain, in_rows, conv_weight, conv_bias, past, xproj_weight, conv_so_far):
+def mamba_in(
+    stream, layer, norm_gain, in_rows, conv_weight, conv_bias, past, xproj_weight, conv_so_far
+):
     requests = past.shape[2]
     channels = past.shape[3]
     inputs = [
@@ -150,7 +162,11 @@
     if conv_so_far is not None:
         aliases = {len(inputs): 3}
         inputs.append((conv_so_far, "far"))
-    terms, signal, gate, conv = local_call(
+    extra = []
+    if layer == 0:
+        width = stream.shape[1] // lax.axis_size(SEQ)
+        extra = [((requests, width), jnp.bfloat16, None), ((1, width), F32, None)]
+    return local_call(
         functools.partial(mamba_in_body, layer),
         inputs,
         [
@@ -158,6 +174,7 @@
             ((requests, channels), F32, None),
             ((requests, channels), F32, None),
             (past.shape, jnp.bfloat16, layer),
+            *extra,
         ],
         [
             pltpu.VMEM((requests, in_rows.shape[3]), jnp.bfloat16),
@@ -166,14 +183,25 @@
         ],
         aliases,
     )
-    return terms, signal, gate, conv
 
 
 def mamba_out_body(layer, order, *refs):
     arrived_ref, signal_ref, gate_ref, dt_ref, bias_ref, decay_ref, skip_ref, state_ref, out_ref = (
         refs[:9]
     )
-    blocks_ref, fresh_ref = refs[-2:]
+    blocks_ref, fresh_ref, held_ref, done = refs[-4:]
+    pieces = done.shape[0]
+    piece = held_ref.shape[1] // pieces
+    copies = [
+        pltpu.make_async_copy(
+            out_ref.at[layer, :, pl.ds(k * piece, piece)],
+            held_ref.at[:, pl.ds(k * piece, piece)],
+            done.at[k],
+        )
+        for k in range(pieces)
+    ]
+    for copy in copies:
+        copy.start()
     mapped = added_up(arrived_ref)
     low_rank = dt_ref.shape[2]
     states = decay_ref.shape[1]
@@ -203,27 +231,31 @@
     readout = jnp.concatenate(readouts, axis=0) + skip_ref[layer : layer + 1, :] * signal
     gated = (readout * gate_ref[...]).astype(jnp.bfloat16)
     width = blocks_ref.shape[2]
-    for place, block in enumerate(order):
+    for place, block in sorted(enumerate(order), key=lambda pair: pair[1]):
+        if block * width % piece == 0:
+            copies[block * width // piece].wait()
         blocks_ref[place] = jnp.dot(
             gated,
-            out_ref[0, :, block * width : (block + 1) * width],
+            held_ref[:, block * width : (block + 1) * width],
             preferred_element_type=F32,
         ).astype(WIRE)
 
 
-def mamba_out(arrived, signal, gate, layer, dt_rows, dt_bias, a_log, skip_gain, ssm_state, out_weight, so_far):
-    far, near = (lax.axis_size(axis) for axis in SEQ_SUM)
-    order = [k * far + j for j in range(far) for k in range(near)]
+def mamba_out(
+    arrived, signal, gate, layer, dt_rows, ssm_state, dt_bias, a_log, skip_gain, out_weight, so_far
+):
+    wide, deep = (lax.axis_size(axis) for axis in SEQ_SUM)
+    order = [k * wide + j for j in range(wide) for k in range(deep)]
     inputs = [
         (arrived, None),
         (signal, None),
         (gate, None),
-        (dt_rows, layer),
+        (dt_rows, min(layer, dt_rows.shape[0] - 1)),
         (dt_bias, None),
         (a_log, layer),
         (skip_gain, None),
-        (ssm_state, layer),
-        (out_weight, layer),
+        (ssm_state, min(layer, ssm_state.shape[0] - 1)),
+        (far(out_weight), "far"),
     ]
     aliases = {}
     if so_far is not None:
@@ -233,10 +265,10 @@
         functools.partial(mamba_out_body, layer, order),
         inputs,
         [
-            ((far * near, signal.shape[0], out_weight.shape[2] // (far * near)), WIRE, None),
-            (ssm_state.shape, F32, layer),
-        ],
-        (),
+            ((wide * deep, signal.shape[0], out_weight.shape[2] // (wide * deep)), WIRE, None),
+            ((a_log.shape[0], *ssm_state.shape[1:]), F32, layer),
+        ],
+        [pltpu.VMEM(out_weight.shape[1:], jnp.bfloat16), pltpu.SemaphoreType.DMA((2,))],
         aliases,
     )
     arrived = exchange(blocks, SEQ_SUM)
@@ -250,15 +282,11 @@
 
 
 def questions_body(arrived_ref, hidden_ref, gain_ref, matrix_ref, stream_ref, terms_ref):
-    width = stream_ref.shape[1]
-    first = pl.multiple_of(seq_index() * width, width)
-    stream = (hidden_ref[:, pl.ds(first, width)].astype(F32) + added_up(arrived_ref)).astype(
-        jnp.bfloat16
-    )
+    stream = (hidden_ref[...].astype(F32) + added_up(arrived_ref)).astype(jnp.bfloat16)
     stream_ref[...] = stream
     wide = stream.astype(F32)
     high, low = two_parts(jnp.sum(wide * wide, axis=1, keepdims=True))
-    scaled = (wide * gain_ref[1:2, pl.ds(first, width)]).astype(jnp.bfloat16)
+    scaled = (wide * gain_ref[...]).astype(jnp.bfloat16)
     terms = jnp.dot(scaled, matrix_ref[...], preferred_element_type=F32)
     lane = lax.broadcasted_iota(jnp.int32, (stream.shape[0], 128), 1)
     notes = jnp.where(lane == 0, high, jnp.where(lane == 1, low, 0.0))
@@ -430,26 +458,31 @@
     pages_dev, block_len, pair, _, width = kv_cache.shape
     entries = asker_lookup_matrix.shape[2]
     rows = requests * (entries // width - 2)
-    in_rows = pltpu.with_memory_space_constraint(in_weight.transpose(0, 2, 3, 1), pltpu.HBM)
+    in_rows = far(in_weight.transpose(0, 2, 3, 1))
     dt_rows = dt_weight.transpose(0, 2, 1)
     past = conv_state.transpose(0, 2, 1, 3)
     kv_rows = kv_cache.reshape(pages_dev * block_len * pair, width)
     conv_args = (conv_weight, conv_bias, past, xproj_weight)
-    state_args = (dt_rows, dt_bias, a_log, skip_gain, ssm_state, out_weight)
+    state_args = (dt_bias, a_log, skip_gain, out_weight)
+    matrix = asker_lookup_matrix.reshape(block_cols, entries)
 
     def sums_of_proj(terms):
         own = jnp.sum(exchange(terms, PLANE).astype(F32), axis=0).astype(WIRE)
         return exchange(copied(own, LINE), LINE)
 
-    terms, signal, gate, new_conv = mamba_in(hidden, 0, norm_gain, in_rows, *conv_args, None)
-    arrived, new_ssm = mamba_out(sums_of_proj(terms), signal, gate, 0, *state_args, None)
+    terms, signal, gate, new_conv, own_block, own_gain = mamba_in(
+        far(hidden), 0, far(norm_gain), in_rows, *[far(x) for x in conv_args], None
+    )
+    arrived, new_ssm = mamba_out(
+        sums_of_proj(terms), signal, gate, 0, dt_rows, ssm_state, *state_args, None
+    )
     stream_one, terms = local_call(
         questions_body,
         [
             (arrived, None),
-            (hidden, None),
-            (norm_gain, None),
-            (asker_lookup_matrix.reshape(block_cols, entries), None),
+            (own_block, None),
+            (own_gain, None),
+            (matrix, None),
         ],
         [
             ((requests, block_cols), jnp.bfloat16, None),
@@ -486,7 +519,9 @@
     terms, signal, gate, new_conv = mamba_in(
         exchange(copied(stream_two, SEQ), SEQ), 1, norm_gain, in_rows, *conv_args, new_conv
     )
-    arrived, new_ssm = mamba_out(sums_of_proj(terms), signal, gate, 1, *state_args, new_ssm)
+    arrived, new_ssm = mamba_out(
+        sums_of_proj(terms), signal, gate, 1, dt_rows, ssm_state, *state_args, new_ssm
+    )
     hidden_out, newest_pair = local_call(
         last_body,
         [(arrived, None), (stream_two, None), (fresh, None)],

time: 188 us -> 178 us (0.947)
  local copies, waits for them, and re-layouts: 9.91 us -> 0.13 us
  Pallas kernels: 10.6 us -> 13.6 us
    unnamed x50 -> x30, local copies, waits for them, and re-layouts: 9.84 us -> 0.07 us
    pallas_call x9, Pallas kernels: 10.6 us -> 13.6 us  [local_call(): pl.pallas_call(body, grid=(1,), in_specs=[spec(x.shape, layer) for x, lay...]
where the time goes in v4:
time: 178 us
  blocking collectives  163 us (92%)
  Pallas kernels  13.6 us (8%)
    all_to_all x14, blocking collectives, exchange(): return lax.all_to_all(copies, axes, split_axis=0, concat_axis=0, tiled=True)  163 us
    pallas_call x9, Pallas kernels, local_call(): pl.pallas_call(body, grid=(1,), in_specs=[spec(x.shape, layer) for x, lay...  13.6 us

profile of v4, /device:TPU:1, one launch (start us, length us, event | category | flops | bytes accessed | tf_op | source)
XLA Modules:
  0.0 177.6 jit_solution(15699443626002267442)
XLA Ops:
  0.6 0.0 copy-start.5
  0.6 0.0 copy-start.13
  0.7 0.0 copy-start.7
  0.7 0.0 copy-start.12
  0.7 0.0 copy-start.4
  0.7 0.0 copy-start.2
  0.7 0.0 copy-start
  0.7 0.0 copy-start.10
  0.7 0.0 copy-start.14
  0.7 3.7 %shard_map.201 = (bf16[16,8,544]{2,1,0:T(8,128)(2,1)S(1)}, f32[8,64]{1,0:T(8,128)S(1)}, f32[8,64]{1,0:T(8,128)S(1)}, bf16[2,3,8,64]{3,2,1,0:T(8,128)(2,1)}, bf16...) custom-call(bf16[8,8192]{1,0:T(8,128)(2,1)} %refs_0_.1, f32[3,8192]{1,0:T(4,128)} %refs_1_.3, ...), custom_call_target="tpu_custom_call" | custom-call | tf_op jit(solution)/shard_map/pallas_call | solution.py:51
  4.4 0.0 copy-start.6
  4.4 14.5 %all_to_all.70 = bf16[16,8,544]{2,1,0:T(8,128)(2,1)S(1)} all-to-all(bf16[16,8,544]{2,1,0:T(8,128)(2,1)S(1)} %get-tuple-element.24), channel_id=1, replica_groups=mesh['z'=8,'x'=4,'y'=4,'core'=2] {'x','y'}, dimensions={0} | all-to-all | bytes 278528 | tf_op jit(solution)/shard_map/all_to_all | solution.py:26
  18.9 0.0 copy-start.11
  19.0 18.2 %all_to_all.71.refs_0_ = bf16[16,8,544]{2,1,0:T(8,128)(2,1)S(1)} all-to-all(bf16[16,8,544]{2,1,0:T(8,128)(2,1)S(1)} %broadcast_in_dim.18), channel_id=1, replica_groups=mesh['z'=8,'x'=4,'y'=4,'core'=2] {'core','z'}, dimensions={0} | all-to-all | bytes 278528 | tf_op jit(solution)/shard_map/all_to_all | solution.py:26
  37.2 0.0 copy-done.5
  37.2 0.0 copy-done.13
  37.2 0.0 copy-done.7
  37.2 0.0 copy-done.12
  37.2 0.0 copy-done.4
  37.2 1.9 %shard_map.202 = (bf16[32,8,256]{2,1,0:T(8,128)(2,1)S(1)}, f32[2,8,16,64]{3,2,1,0:T(8,128)}) custom-call(bf16[16,8,544]{2,1,0:T(8,128)(2,1)S(1)} %all_to_all.71.refs_0_, f32[8,64]{1,0:T(8,128)S(1)} %get-tuple-element.25.refs_1_, f32[8,64]{1,0:T(8,128)S(1)} %get-tuple-element.26.refs_2_, bf16[2,64,512]{2,1,0:T(8,128)(2,1)S(1)} %bitcast.9, ...), custom_call_target="tpu_custom_call" | custom-call | tf_op jit(solution)/shard_map/pallas_call | solution.py:51
  39.2 13.7 %all_to_all.72 = bf16[32,8,256]{2,1,0:T(8,128)(2,1)S(1)} all-to-all(bf16[32,8,256]{2,1,0:T(8,128)(2,1)S(1)} %get-tuple-element.27), channel_id=1, replica_groups=mesh['z'=8,'x'=4,'y'=4,'core'=2] {'x','z'}, dimensions={0} | all-to-all | bytes 262144 | tf_op jit(solution)/shard_map/all_to_all | solution.py:26
  52.9 9.6 %all_to_all.73.arrived_ref = bf16[8,8,256]{2,1,0:T(8,128)(2,1)S(1)} all-to-all(bf16[8,8,256]{2,1,0:T(8,128)(2,1)S(1)} %broadcast_in_dim.19), channel_id=1, replica_groups=mesh['z'=8,'x'=4,'y'=4,'core'=2] {'core','y'}, dimensions={0} | all-to-all | bytes 65536 | tf_op jit(solution)/shard_map/all_to_all | solution.py:26
  62.5 0.0 copy-done.2
  62.5 0.2 shard_map.203
  62.7 7.0 %all_to_all.74 = bf16[4,8,1408]{2,1,0:T(8,128)(2,1)S(1)} all-to-all(bf16[4,8,1408]{2,1,0:T(8,128)(2,1)S(1)} %get-tuple-element.31), channel_id=1, replica_groups=mesh['z'=8,'x'=4,'y'=4,'core'=2] {'x'}, dimensions={0} | all-to-all | bytes 180224 | tf_op jit(solution)/shard_map/all_to_all | solution.py:26
  69.8 10.9 %all_to_all.75.arrived_ref = bf16[8,8,1408]{2,1,0:T(8,128)(2,1)S(1)} all-to-all(bf16[8,8,1408]{2,1,0:T(8,128)(2,1)S(1)} %broadcast_in_dim.20), channel_id=1, replica_groups=mesh['z'=8,'x'=4,'y'=4,'core'=2] {'z'}, dimensions={0} | all-to-all | bytes 360448 | tf_op jit(solution)/shard_map/all_to_all | solution.py:26
  80.7 0.0 copy-done
  80.7 0.0 copy-done.10
  80.7 0.0 copy-done.14
  80.7 1.8 shard_map.204
  82.5 6.9 %all_to_all.76.arrived_ref = bf16[4,72,128]{2,1,0:T(8,128)(2,1)S(1)} all-to-all(bf16[4,72,128]{2,1,0:T(8,128)(2,1)S(1)} %get-tuple-element.32), channel_id=1, replica_groups=mesh['z'=8,'x'=4,'y'=4,'core'=2] {'x'}, dimensions={0} | all-to-all | bytes 147456 | tf_op jit(solution)/shard_map/all_to_all | solution.py:26
  89.4 0.1 shard_map.205
  89.5 10.5 %all_to_all.77.arrived_ref = bf16[8,72,128]{2,1,0:T(8,128)(2,1)S(1)} all-to-all(bf16[8,72,128]{2,1,0:T(8,128)(2,1)S(1)} %shard_map.205), channel_id=1, replica_groups=mesh['z'=8,'x'=4,'y'=4,'core'=2] {'z'}, dimensions={0} | all-to-all | bytes 294912 | tf_op jit(solution)/shard_map/all_to_all | solution.py:26
  100.0 0.0 copy-done.6
  100.0 0.3 shard_map.206
  100.3 12.3 %all_to_all.78 = bf16[8,8,256]{2,1,0:T(8,128)(2,1)S(1)} all-to-all(bf16[8,8,256]{2,1,0:T(8,128)(2,1)S(1)} %shard_map.206), channel_id=1, replica_groups=mesh['z'=8,'x'=4,'y'=4,'core'=2] {'core','y'}, dimensions={0} | all-to-all | bytes 65536 | tf_op jit(solution)/shard_map/all_to_all | solution.py:26
  112.7 12.7 %all_to_all.79.refs_0_ = bf16[32,8,256]{2,1,0:T(8,128)(2,1)S(1)} all-to-all(bf16[32,8,256]{2,1,0:T(8,128)(2,1)S(1)} %broadcast_in_dim.21), channel_id=1, replica_groups=mesh['z'=8,'x'=4,'y'=4,'core'=2] {'z','x'}, dimensions={0} | all-to-all | bytes 262144 | tf_op jit(solution)/shard_map/all_to_all | solution.py:26
  125.4 0.0 copy-done.1
  125.4 0.0 copy-done.8
  125.4 0.0 copy-done.9
  125.4 0.0 copy-done.11
  125.5 2.5 %shard_map.207 = (bf16[16,8,544]{2,1,0:T(8,128)(2,1)S(1)}, f32[8,64]{1,0:T(8,128)S(1)}, f32[8,64]{1,0:T(8,128)S(1)}, bf16[2,3,8,64]{3,2,1,0:T(8,128)(2,1)}) custom-call(bf16[32,8,256]{2,1,0:T(8,128)(2,1)S(1)} %all_to_all.79.refs_0_, f32[3,8192]{1,0:T(4,128)S(1)} %copy-done.3, bf16[2,2,64,8192]{3,2,1,0:T(8,128)(2,1)} %bitcast.15, ...), custom_call_target="tpu_custom_call", output_to_operand_aliasing={{3}: (7, {})} | custom-call | tf_op jit(solution)/shard_map/pallas_call | solution.py:51
  128.0 9.7 %all_to_all.80 = bf16[16,8,544]{2,1,0:T(8,128)(2,1)S(1)} all-to-all(bf16[16,8,544]{2,1,0:T(8,128)(2,1)S(1)} %get-tuple-element.34), channel_id=1, replica_groups=mesh['z'=8,'x'=4,'y'=4,'core'=2] {'x','y'}, dimensions={0} | all-to-all | bytes 278528 | tf_op jit(solution)/shard_map/all_to_all | solution.py:26
  137.8 13.3 %all_to_all.81.refs_0_ = bf16[16,8,544]{2,1,0:T(8,128)(2,1)S(1)} all-to-all(bf16[16,8,544]{2,1,0:T(8,128)(2,1)S(1)} %broadcast_in_dim.22), channel_id=1, replica_groups=mesh['z'=8,'x'=4,'y'=4,'core'=2] {'core','z'}, dimensions={0} | all-to-all | bytes 278528 | tf_op jit(solution)/shard_map/all_to_all | solution.py:26
  151.1 1.9 %shard_map.208 = (bf16[32,8,256]{2,1,0:T(8,128)(2,1)S(1)}, f32[2,8,16,64]{3,2,1,0:T(8,128)}) custom-call(bf16[16,8,544]{2,1,0:T(8,128)(2,1)S(1)} %all_to_all.81.refs_0_, f32[8,64]{1,0:T(8,128)S(1)} %get-tuple-element.35.refs_1_, f32[8,64]{1,0:T(8,128)S(1)} %get-tuple-element.36.refs_2_, ...), custom_call_target="tpu_custom_call", output_to_operand_aliasing={{1}: (9, {})} | custom-call | tf_op jit(solution)/shard_map/pallas_call | solution.py:51
  153.0 13.8 %all_to_all.82 = bf16[32,8,256]{2,1,0:T(8,128)(2,1)S(1)} all-to-all(bf16[32,8,256]{2,1,0:T(8,128)(2,1)S(1)} %get-tuple-element.38), channel_id=1, replica_groups=mesh['z'=8,'x'=4,'y'=4,'core'=2] {'x','z'}, dimensions={0} | all-to-all | bytes 262144 | tf_op jit(solution)/shard_map/all_to_all | solution.py:26
  166.8 9.6 %all_to_all.83.arrived_ref = bf16[8,8,256]{2,1,0:T(8,128)(2,1)S(1)} all-to-all(bf16[8,8,256]{2,1,0:T(8,128)(2,1)S(1)} %broadcast_in_dim.23), channel_id=1, replica_groups=mesh['z'=8,'x'=4,'y'=4,'core'=2] {'core','y'}, dimensions={0} | all-to-all | bytes 65536 | tf_op jit(solution)/shard_map/all_to_all | solution.py:26
  176.5 1.1 shard_map.209
  (18 shorter events, 0.3 us)
Async XLA Ops:
  0.6 36.6 %copy-start.5 = (f32[2,8,16,64]{3,2,1,0:T(8,128)S(1)}, f32[2,8,16,64]{3,2,1,0:T(8,128)}, u32[]{:S(2)}) copy-start(f32[2,8,16,64]{3,2,1,0:T(8,128)} %refs_7_.3) | copy-start | bytes 196612
  0.6 36.6 %copy-start.13 = (f32[2,64]{1,0:T(2,128)S(1)}, f32[2,64]{1,0:T(2,128)}, u32[]{:S(2)}) copy-start(f32[2,64]{1,0:T(2,128)} %refs_6_.7) | copy-start | bytes 1540
  0.7 36.6 %copy-start.7 = (f32[2,16,64]{2,1,0:T(8,128)S(1)}, f32[2,16,64]{2,1,0:T(8,128)}, u32[]{:S(2)}) copy-start(f32[2,16,64]{2,1,0:T(8,128)} %refs_5_.3) | copy-start | bytes 24580
  0.7 36.6 %copy-start.12 = (f32[2,64]{1,0:T(2,128)S(1)}, f32[2,64]{1,0:T(2,128)}, u32[]{:S(2)}) copy-start(f32[2,64]{1,0:T(2,128)} %refs_4_.7) | copy-start | bytes 1540
  0.7 36.6 %copy-start.4 = (bf16[2,512,64]{1,2,0:T(8,128)(2,1)S(1)}, bf16[2,512,64]{1,2,0:T(8,128)(2,1)}, u32[]{:S(2)}) copy-start(bf16[2,512,64]{1,2,0:T(8,128)(2,1)} %param.25) | copy-start | bytes 393220
  0.7 61.8 %copy-start.2 = (bf16[256,1,1280]{2,0,1:T(8,128)(2,1)S(1)}, bf16[256,1,1280]{2,0,1:T(8,128)(2,1)}, u32[]{:S(2)}) copy-start(bf16[256,1,1280]{2,0,1:T(8,128)(2,1)} %param.31) | copy-start | bytes 1966084
  0.7 80.0 %copy-start = (bf16[8,256,2,1,128]{4,2,3,1,0:T(2,128)(2,1)S(1)}, bf16[8,256,2,1,128]{4,2,3,1,0:T(2,128)(2,1)}, u32[]{:S(2)}) copy-start(bf16[8,256,2,1,128]{4,2,3,1,0:T(2,128)(2,1)} %param.33) | copy-start | bytes 3145732
  0.7 80.0 %copy-start.10 = (s32[8,32]{1,0:T(8,128)S(1)}, s32[8,32]{1,0:T(8,128)}, u32[]{:S(2)}) copy-start(s32[8,32]{1,0:T(8,128)} %table_ref.1) | copy-start | bytes 3076
  0.7 80.0 %copy-start.14 = (s32[8]{0:T(128)S(1)}, s32[8]{0:T(128)}, u32[]{:S(2)}) copy-start(s32[8]{0:T(128)} %lengths_ref.1) | copy-start | bytes 100
  4.4 95.6 %copy-start.6 = (bf16[1,1024,256]{2,1,0:T(8,128)(2,1)S(1)}, bf16[1,1024,256]{2,1,0:T(8,128)(2,1)}, u32[]{:S(2)}) copy-start(bf16[1,1024,256]{2,1,0:T(8,128)(2,1)} %param.32) | copy-start | bytes 1572868
  18.9 106.5 %copy-start.1 = (bf16[2,64,544]{2,1,0:T(8,128)(2,1)S(1)}, bf16[2,64,544]{2,1,0:T(8,128)(2,1)}, u32[]{:S(2)}) copy-start(bf16[2,64,544]{2,1,0:T(8,128)(2,1)} %refs_6_.6) | copy-start | bytes 417796
  18.9 106.5 %copy-start.3 = (f32[3,8192]{1,0:T(4,128)S(1)}, f32[3,8192]{1,0:T(4,128)}, u32[]{:S(2)}) copy-start(f32[3,8192]{1,0:T(4,128)} %refs_1_.3) | copy-start | bytes 294916
  18.9 106.5 %copy-start.8 = (bf16[2,8,3,64]{3,1,2,0:T(8,128)(2,1)S(1)}, bf16[2,8,3,64]{3,1,2,0:T(8,128)(2,1)}, u32[]{:S(2)}) copy-start(bf16[2,8,3,64]{3,1,2,0:T(8,128)(2,1)} %param.23) | copy-start | bytes 18436
  18.9 106.5 %copy-start.9 = (f32[2,4,64]{2,1,0:T(4,128)S(1)}, f32[2,4,64]{2,1,0:T(4,128)}, u32[]{:S(2)}) copy-start(f32[2,4,64]{2,1,0:T(4,128)} %refs_3_.3) | copy-start | bytes 6148
  18.9 106.5 %copy-start.11 = (f32[2,64]{1,0:T(2,128)S(1)}, f32[2,64]{1,0:T(2,128)}, u32[]{:S(2)}) copy-start(f32[2,64]{1,0:T(2,128)} %refs_4_.6) | copy-start | bytes 1540

commit v5 on v4

--- a/solution.py
+++ b/solution.py
@@ -15,6 +15,7 @@
 CHAN_SUM = ("core", "y")
 PLANE = ("x", "y")
 LINE = ("core", "z")
+CORE_FIRST = ("core", "z", "x", "y")
 WIRE = jnp.bfloat16
 F32 = jnp.float32
 
@@ -185,6 +186,28 @@
     )
 
 
+def store_shares(shares_ref, block, x):
+    row = lax.broadcasted_iota(jnp.int32, (8, 128), 0)
+    group = lax.broadcasted_iota(jnp.int32, (8, 128), 1) // 32
+    own = row // 2 == group
+    packed = []
+    for half in range(2):
+        tile = x[:, half * 128 : (half + 1) * 128]
+        turned = [tile] + [pltpu.roll(tile, 32 * k, 1) for k in range(1, 4)]
+        for q in range(4):
+            z = turned[-q % 4]
+            for g in range(1, 4):
+                z = jnp.where(group == g, turned[(g - q) % 4], z)
+            z = jnp.where(own, z, 0.0)
+            z = z + pltpu.roll(z, 4, 0)
+            packed.append(z + pltpu.roll(z, 2, 0))
+    for core in range(2):
+        lines = packed[core]
+        for k in range(1, 4):
+            lines = jnp.where(row // 2 == k, packed[2 * k + core], lines)
+        shares_ref[core, block * 8 : block * 8 + 8, :] = lines.astype(WIRE)
+
+
 def mamba_out_body(layer, order, *refs):
     arrived_ref, signal_ref, gate_ref, dt_ref, bias_ref, decay_ref, skip_ref, state_ref, out_ref = (
         refs[:9]
@@ -230,15 +253,19 @@
         readouts.append(jnp.sum(fresh * c_out, axis=0, keepdims=True))
     readout = jnp.concatenate(readouts, axis=0) + skip_ref[layer : layer + 1, :] * signal
     gated = (readout * gate_ref[...]).astype(jnp.bfloat16)
-    width = blocks_ref.shape[2]
-    for place, block in sorted(enumerate(order), key=lambda pair: pair[1]):
+    width = held_ref.shape[1] // len(order)
+    for block in range(len(order)):
         if block * width % piece == 0:
             copies[block * width // piece].wait()
-        blocks_ref[place] = jnp.dot(
+        result = jnp.dot(
             gated,
             held_ref[:, block * width : (block + 1) * width],
             preferred_element_type=F32,
-        ).astype(WIRE)
+        )
+        if layer == 0:
+            blocks_ref[order.index(block)] = result.astype(WIRE)
+        else:
+            store_shares(blocks_ref, block, result)
 
 
 def mamba_out(
@@ -265,12 +292,21 @@
         functools.partial(mamba_out_body, layer, order),
         inputs,
         [
-            ((wide * deep, signal.shape[0], out_weight.shape[2] // (wide * deep)), WIRE, None),
+            (
+                (wide * deep, signal.shape[0], out_weight.shape[2] // (wide * deep))
+                if layer == 0
+                else (2, lax.axis_size(ALL), 128),
+                WIRE,
+                None,
+            ),
             ((a_log.shape[0], *ssm_state.shape[1:]), F32, layer),
         ],
-        [pltpu.VMEM(out_weight.shape[1:], jnp.bfloat16), pltpu.SemaphoreType.DMA((2,))],
+        [pltpu.VMEM(out_weight.shape[1:], jnp.bfloat16), pltpu.SemaphoreType.DMA((4,))],
         aliases,
     )
+    if layer:
+        shares = exchange(blocks.reshape(-1, 2, 128), CORE_FIRST)
+        return shares.reshape(-1, 128), fresh
     arrived = exchange(blocks, SEQ_SUM)
     own = jnp.sum(arrived.astype(F32), axis=0).astype(WIRE)
     return exchange(copied(own, CHAN_SUM), CHAN_SUM), fresh
@@ -422,14 +458,22 @@
         pair_ref[b, 0] = jnp.concatenate(
             [fresh_ref[b : b + 1, :head], fresh_ref[b : b + 1, head:]], axis=0
         ).astype(jnp.bfloat16)
-    result = (stream_ref[...].astype(F32) + added_up(arrived_ref)).astype(jnp.bfloat16)
+    total = jnp.zeros((8, 128), F32)
+    for k in range(arrived_ref.shape[0] // 8):
+        total = total + arrived_ref[k * 8 : (k + 1) * 8, :].astype(F32)
+    total = total + pltpu.roll(total, 4, 0)
+    total = total + pltpu.roll(total, 2, 0)
+    row = lax.broadcasted_iota(jnp.int32, (8, 128), 0)
+    added = total
+    for k in range(1, 4):
+        added = jnp.where(row // 2 == k, pltpu.roll(total, 128 - 32 * k, 1), added)
     place = lax.axis_index("y") * lax.axis_size("core") + lax.axis_index("core")
     width = out_ref.shape[1]
-    result = result.astype(F32)
-    own = result[:, :width]
-    for k in range(1, result.shape[1] // width):
-        own = jnp.where(place == k, result[:, k * width : (k + 1) * width], own)
-    out_ref[...] = own.astype(jnp.bfloat16)
+    stream = stream_ref[...].astype(F32)
+    own = stream[:, :width]
+    for k in range(1, stream.shape[1] // width):
+        own = jnp.where(place == k, stream[:, k * width : (k + 1) * width], own)
+    out_ref[...] = (own + added[:, :width]).astype(jnp.bfloat16)
 
 
 def shards(

time: 178 us -> 176 us (0.989)
  blocking collectives: 163 us -> 159 us
    all_to_all x14 -> x13, blocking collectives: 163 us -> 159 us  [exchange(): return lax.all_to_all(copies, axes, split_axis=0, concat_axis=0, tiled=True)]
where the time goes in v5:
time: 176 us; the launch traced here: 175 us
  blocking collectives  159 us (90%)
  Pallas kernels  14.5 us (8%)
    all_to_all x13, blocking collectives, exchange(): return lax.all_to_all(copies, axes, split_axis=0, concat_axis=0, tiled=True)  159 us
    pallas_call x9, Pallas kernels, local_call(): pl.pallas_call(body, grid=(1,), in_specs=[spec(x.shape, layer) for x, lay...  14.5 us

profile of v5, /device:TPU:1, one launch (start us, length us, event | category | flops | bytes accessed | tf_op | source)
XLA Modules:
  0.0 175.0 jit_solution(5872215497250323081)
XLA Ops:
  0.6 0.0 copy-start.5
  0.6 0.0 copy-start.13
  0.7 0.0 copy-start.7
  0.7 0.0 copy-start.12
  0.7 0.0 copy-start.4
  0.7 0.0 copy-start.2
  0.7 0.0 copy-start
  0.7 0.0 copy-start.10
  0.7 0.0 copy-start.14
  0.7 3.7 %shard_map.201 = (bf16[16,8,544]{2,1,0:T(8,128)(2,1)S(1)}, f32[8,64]{1,0:T(8,128)S(1)}, f32[8,64]{1,0:T(8,128)S(1)}, bf16[2,3,8,64]{3,2,1,0:T(8,128)(2,1)}, bf16...) custom-call(bf16[8,8192]{1,0:T(8,128)(2,1)} %refs_0_.1, f32[3,8192]{1,0:T(4,128)} %refs_1_.3, ...), custom_call_target="tpu_custom_call" | custom-call | tf_op jit(solution)/shard_map/pallas_call | solution.py:52
  4.4 0.0 copy-start.6
  4.4 14.5 %all_to_all.65 = bf16[16,8,544]{2,1,0:T(8,128)(2,1)S(1)} all-to-all(bf16[16,8,544]{2,1,0:T(8,128)(2,1)S(1)} %get-tuple-element.24), channel_id=1, replica_groups=mesh['z'=8,'x'=4,'y'=4,'core'=2] {'x','y'}, dimensions={0} | all-to-all | bytes 278528 | tf_op jit(solution)/shard_map/all_to_all | solution.py:27
  18.9 0.0 copy-start.11
  19.0 18.2 %all_to_all.66.refs_0_ = bf16[16,8,544]{2,1,0:T(8,128)(2,1)S(1)} all-to-all(bf16[16,8,544]{2,1,0:T(8,128)(2,1)S(1)} %broadcast_in_dim.15), channel_id=1, replica_groups=mesh['z'=8,'x'=4,'y'=4,'core'=2] {'core','z'}, dimensions={0} | all-to-all | bytes 278528 | tf_op jit(solution)/shard_map/all_to_all | solution.py:27
  37.2 0.0 copy-done.5
  37.2 0.0 copy-done.13
  37.2 0.0 copy-done.7
  37.2 0.0 copy-done.12
  37.2 0.0 copy-done.4
  37.2 2.1 %shard_map.202 = (bf16[32,8,256]{2,1,0:T(8,128)(2,1)S(1)}, f32[2,8,16,64]{3,2,1,0:T(8,128)}) custom-call(bf16[16,8,544]{2,1,0:T(8,128)(2,1)S(1)} %all_to_all.66.refs_0_, f32[8,64]{1,0:T(8,128)S(1)} %get-tuple-element.25.refs_1_, f32[8,64]{1,0:T(8,128)S(1)} %get-tuple-element.26.refs_2_, bf16[2,64,512]{2,1,0:T(8,128)(2,1)S(1)} %bitcast.11, ...), custom_call_target="tpu_custom_call" | custom-call | tf_op jit(solution)/shard_map/pallas_call | solution.py:52
  39.4 13.7 %all_to_all.67 = bf16[32,8,256]{2,1,0:T(8,128)(2,1)S(1)} all-to-all(bf16[32,8,256]{2,1,0:T(8,128)(2,1)S(1)} %get-tuple-element.27), channel_id=1, replica_groups=mesh['z'=8,'x'=4,'y'=4,'core'=2] {'x','z'}, dimensions={0} | all-to-all | bytes 262144 | tf_op jit(solution)/shard_map/all_to_all | solution.py:27
  53.1 9.6 %all_to_all.68.arrived_ref = bf16[8,8,256]{2,1,0:T(8,128)(2,1)S(1)} all-to-all(bf16[8,8,256]{2,1,0:T(8,128)(2,1)S(1)} %broadcast_in_dim.16), channel_id=1, replica_groups=mesh['z'=8,'x'=4,'y'=4,'core'=2] {'core','y'}, dimensions={0} | all-to-all | bytes 65536 | tf_op jit(solution)/shard_map/all_to_all | solution.py:27
  62.7 0.0 copy-done.2
  62.7 0.2 shard_map.203
  63.0 7.0 %all_to_all.69 = bf16[4,8,1408]{2,1,0:T(8,128)(2,1)S(1)} all-to-all(bf16[4,8,1408]{2,1,0:T(8,128)(2,1)S(1)} %get-tuple-element.31), channel_id=1, replica_groups=mesh['z'=8,'x'=4,'y'=4,'core'=2] {'x'}, dimensions={0} | all-to-all | bytes 180224 | tf_op jit(solution)/shard_map/all_to_all | solution.py:27
  70.0 10.9 %all_to_all.70.arrived_ref = bf16[8,8,1408]{2,1,0:T(8,128)(2,1)S(1)} all-to-all(bf16[8,8,1408]{2,1,0:T(8,128)(2,1)S(1)} %broadcast_in_dim.17), channel_id=1, replica_groups=mesh['z'=8,'x'=4,'y'=4,'core'=2] {'z'}, dimensions={0} | all-to-all | bytes 360448 | tf_op jit(solution)/shard_map/all_to_all | solution.py:27
  80.9 0.0 copy-done
  80.9 0.0 copy-done.10
  80.9 0.0 copy-done.14
  80.9 1.8 %shard_map.204 = (bf16[4,72,128]{2,1,0:T(8,128)(2,1)S(1)}, f32[8,256]{1,0:T(8,128)S(1)}) custom-call(bf16[8,8,1408]{2,1,0:T(8,128)(2,1)S(1)} %all_to_all.70.arrived_ref, bf16[4096,128]{1,0:T(8,128)(2,1)S(1)} %bitcast.9, s32[8]{0:T(128)S(1)} %copy-done.14, s32[8,32]{1,0:T(8,128)S(1)} %copy-done.10), custom_call_target="tpu_custom_call" | custom-call | tf_op jit(solution)/shard_map/pallas_call | solution.py:52
  82.7 6.9 %all_to_all.71.arrived_ref = bf16[4,72,128]{2,1,0:T(8,128)(2,1)S(1)} all-to-all(bf16[4,72,128]{2,1,0:T(8,128)(2,1)S(1)} %get-tuple-element.32), channel_id=1, replica_groups=mesh['z'=8,'x'=4,'y'=4,'core'=2] {'x'}, dimensions={0} | all-to-all | bytes 147456 | tf_op jit(solution)/shard_map/all_to_all | solution.py:27
  89.6 0.1 shard_map.205
  89.7 10.5 %all_to_all.72.arrived_ref = bf16[8,72,128]{2,1,0:T(8,128)(2,1)S(1)} all-to-all(bf16[8,72,128]{2,1,0:T(8,128)(2,1)S(1)} %shard_map.205), channel_id=1, replica_groups=mesh['z'=8,'x'=4,'y'=4,'core'=2] {'z'}, dimensions={0} | all-to-all | bytes 294912 | tf_op jit(solution)/shard_map/all_to_all | solution.py:27
  100.2 0.0 copy-done.6
  100.2 0.3 shard_map.206
  100.5 12.3 %all_to_all.73 = bf16[8,8,256]{2,1,0:T(8,128)(2,1)S(1)} all-to-all(bf16[8,8,256]{2,1,0:T(8,128)(2,1)S(1)} %shard_map.206), channel_id=1, replica_groups=mesh['z'=8,'x'=4,'y'=4,'core'=2] {'core','y'}, dimensions={0} | all-to-all | bytes 65536 | tf_op jit(solution)/shard_map/all_to_all | solution.py:27
  112.9 12.7 %all_to_all.74.refs_0_ = bf16[32,8,256]{2,1,0:T(8,128)(2,1)S(1)} all-to-all(bf16[32,8,256]{2,1,0:T(8,128)(2,1)S(1)} %broadcast_in_dim.18), channel_id=1, replica_groups=mesh['z'=8,'x'=4,'y'=4,'core'=2] {'z','x'}, dimensions={0} | all-to-all | bytes 262144 | tf_op jit(solution)/shard_map/all_to_all | solution.py:27
  125.6 0.0 copy-done.1
  125.6 0.0 copy-done.3
  125.6 0.0 copy-done.8
  125.6 0.0 copy-done.9
  125.7 0.0 copy-done.11
  125.7 2.5 %shard_map.207 = (bf16[16,8,544]{2,1,0:T(8,128)(2,1)S(1)}, f32[8,64]{1,0:T(8,128)S(1)}, f32[8,64]{1,0:T(8,128)S(1)}, bf16[2,3,8,64]{3,2,1,0:T(8,128)(2,1)}) custom-call(bf16[32,8,256]{2,1,0:T(8,128)(2,1)S(1)} %all_to_all.74.refs_0_, f32[3,8192]{1,0:T(4,128)S(1)} %copy-done.3, bf16[2,2,64,8192]{3,2,1,0:T(8,128)(2,1)} %bitcast.19, ...), custom_call_target="tpu_custom_call", output_to_operand_aliasing={{3}: (7, {})} | custom-call | tf_op jit(solution)/shard_map/pallas_call | solution.py:52
  128.2 9.7 %all_to_all.75 = bf16[16,8,544]{2,1,0:T(8,128)(2,1)S(1)} all-to-all(bf16[16,8,544]{2,1,0:T(8,128)(2,1)S(1)} %get-tuple-element.34), channel_id=1, replica_groups=mesh['z'=8,'x'=4,'y'=4,'core'=2] {'x','y'}, dimensions={0} | all-to-all | bytes 278528 | tf_op jit(solution)/shard_map/all_to_all | solution.py:27
  138.0 13.3 %all_to_all.76.refs_0_ = bf16[16,8,544]{2,1,0:T(8,128)(2,1)S(1)} all-to-all(bf16[16,8,544]{2,1,0:T(8,128)(2,1)S(1)} %broadcast_in_dim.19), channel_id=1, replica_groups=mesh['z'=8,'x'=4,'y'=4,'core'=2] {'core','z'}, dimensions={0} | all-to-all | bytes 278528 | tf_op jit(solution)/shard_map/all_to_all | solution.py:27
  151.3 2.6 %shard_map.208 = (bf16[2,256,128]{2,1,0:T(8,128)(2,1)S(1)}, f32[2,8,16,64]{3,2,1,0:T(8,128)}) custom-call(bf16[16,8,544]{2,1,0:T(8,128)(2,1)S(1)} %all_to_all.76.refs_0_, f32[8,64]{1,0:T(8,128)S(1)} %get-tuple-element.35.refs_1_, f32[8,64]{1,0:T(8,128)S(1)} %get-tuple-element.36.refs_2_, ...), custom_call_target="tpu_custom_call", output_to_operand_aliasing={{1}: (9, {})} | custom-call | tf_op jit(solution)/shard_map/pallas_call | solution.py:52
  153.9 19.9 %all_to_all.77 = bf16[256,2,128]{2,1,0:T(2,128)(2,1)S(1)} all-to-all(bf16[256,2,128]{2,1,0:T(2,128)(2,1)S(1)} %bitcast.15), channel_id=1, replica_groups=mesh['z'=8,'x'=4,'y'=4,'core'=2] {'core','z','x','y'}, dimensions={0} | all-to-all | bytes 262144 | tf_op jit(solution)/shard_map/all_to_all | solution.py:27
  173.9 1.1 shard_map.209
  (15 shorter events, 0.2 us)
Async XLA Ops:
  0.6 36.6 %copy-start.5 = (f32[2,8,16,64]{3,2,1,0:T(8,128)S(1)}, f32[2,8,16,64]{3,2,1,0:T(8,128)}, u32[]{:S(2)}) copy-start(f32[2,8,16,64]{3,2,1,0:T(8,128)} %refs_7_.3) | copy-start | bytes 196612
  0.6 36.6 %copy-start.13 = (f32[2,64]{1,0:T(2,128)S(1)}, f32[2,64]{1,0:T(2,128)}, u32[]{:S(2)}) copy-start(f32[2,64]{1,0:T(2,128)} %refs_6_.7) | copy-start | bytes 1540
  0.7 36.6 %copy-start.7 = (f32[2,16,64]{2,1,0:T(8,128)S(1)}, f32[2,16,64]{2,1,0:T(8,128)}, u32[]{:S(2)}) copy-start(f32[2,16,64]{2,1,0:T(8,128)} %refs_5_.3) | copy-start | bytes 24580
  0.7 36.6 %copy-start.12 = (f32[2,64]{1,0:T(2,128)S(1)}, f32[2,64]{1,0:T(2,128)}, u32[]{:S(2)}) copy-start(f32[2,64]{1,0:T(2,128)} %refs_4_.7) | copy-start | bytes 1540
  0.7 36.6 %copy-start.4 = (bf16[2,512,64]{1,2,0:T(8,128)(2,1)S(1)}, bf16[2,512,64]{1,2,0:T(8,128)(2,1)}, u32[]{:S(2)}) copy-start(bf16[2,512,64]{1,2,0:T(8,128)(2,1)} %param.25) | copy-start | bytes 393220
  0.7 62.1 %copy-start.2 = (bf16[256,1,1280]{2,0,1:T(8,128)(2,1)S(1)}, bf16[256,1,1280]{2,0,1:T(8,128)(2,1)}, u32[]{:S(2)}) copy-start(bf16[256,1,1280]{2,0,1:T(8,128)(2,1)} %param.31) | copy-start | bytes 1966084
  0.7 80.2 %copy-start = (bf16[8,256,2,1,128]{4,2,3,1,0:T(2,128)(2,1)S(1)}, bf16[8,256,2,1,128]{4,2,3,1,0:T(2,128)(2,1)}, u32[]{:S(2)}) copy-start(bf16[8,256,2,1,128]{4,2,3,1,0:T(2,128)(2,1)} %param.33) | copy-start | bytes 3145732
  0.7 80.2 %copy-start.10 = (s32[8,32]{1,0:T(8,128)S(1)}, s32[8,32]{1,0:T(8,128)}, u32[]{:S(2)}) copy-start(s32[8,32]{1,0:T(8,128)} %table_ref.1) | copy-start | bytes 3076
  0.7 80.2 %copy-start.14 = (s32[8]{0:T(128)S(1)}, s32[8]{0:T(128)}, u32[]{:S(2)}) copy-start(s32[8]{0:T(128)} %lengths_ref.1) | copy-start | bytes 100
  4.4 95.8 %copy-start.6 = (bf16[1,1024,256]{2,1,0:T(8,128)(2,1)S(1)}, bf16[1,1024,256]{2,1,0:T(8,128)(2,1)}, u32[]{:S(2)}) copy-start(bf16[1,1024,256]{2,1,0:T(8,128)(2,1)} %param.32) | copy-start | bytes 1572868
  18.9 106.7 %copy-start.1 = (bf16[2,64,544]{2,1,0:T(8,128)(2,1)S(1)}, bf16[2,64,544]{2,1,0:T(8,128)(2,1)}, u32[]{:S(2)}) copy-start(bf16[2,64,544]{2,1,0:T(8,128)(2,1)} %refs_6_.6) | copy-start | bytes 417796
  18.9 106.7 %copy-start.3 = (f32[3,8192]{1,0:T(4,128)S(1)}, f32[3,8192]{1,0:T(4,128)}, u32[]{:S(2)}) copy-start(f32[3,8192]{1,0:T(4,128)} %refs_1_.3) | copy-start | bytes 294916
  18.9 106.7 %copy-start.8 = (bf16[2,8,3,64]{3,1,2,0:T(8,128)(2,1)S(1)}, bf16[2,8,3,64]{3,1,2,0:T(8,128)(2,1)}, u32[]{:S(2)}) copy-start(bf16[2,8,3,64]{3,1,2,0:T(8,128)(2,1)} %param.23) | copy-start | bytes 18436
  18.9 106.7 %copy-start.9 = (f32[2,4,64]{2,1,0:T(4,128)S(1)}, f32[2,4,64]{2,1,0:T(4,128)}, u32[]{:S(2)}) copy-start(f32[2,4,64]{2,1,0:T(4,128)} %refs_3_.3) | copy-start | bytes 6148
  18.9 106.7 %copy-start.11 = (f32[2,64]{1,0:T(2,128)S(1)}, f32[2,64]{1,0:T(2,128)}, u32[]{:S(2)}) copy-start(f32[2,64]{1,0:T(2,128)} %refs_4_.6) | copy-start | bytes 1540

commit v6 on v5

--- a/solution.py
+++ b/solution.py
@@ -116,8 +116,10 @@
             x = stream_ref[k].astype(F32)
             squares = squares + x * x
         inv_rms = lax.rsqrt(jnp.sum(squares, axis=1, keepdims=True) / dim + norm_eps)
+        wide, deep = (lax.axis_size(axis) for axis in SEQ_SUM)
         for k in range(blocks):
-            cols = slice(k * width, (k + 1) * width)
+            block = k % deep * wide + k // deep
+            cols = slice(block * width, (block + 1) * width)
             normed_ref[:, cols] = (
                 stream_ref[k].astype(F32) * inv_rms * gain_ref[gain_row : gain_row + 1, cols]
             ).astype(jnp.bfloat16)
@@ -212,9 +214,13 @@
     arrived_ref, signal_ref, gate_ref, dt_ref, bias_ref, decay_ref, skip_ref, state_ref, out_ref = (
         refs[:9]
     )
-    blocks_ref, fresh_ref, held_ref, done = refs[-4:]
-    pieces = done.shape[0]
-    piece = held_ref.shape[1] // pieces
+    blocks_ref, fresh_ref = refs[9:11] if layer == 0 else refs[10:12]
+    if layer == 0:
+        held_ref, done = refs[11:]
+    else:
+        held_ref = out_ref.at[0]
+    pieces = 2 if layer == 0 else 0
+    piece = out_ref.shape[2] // max(pieces, 1)
     copies = [
         pltpu.make_async_copy(
             out_ref.at[layer, :, pl.ds(k * piece, piece)],
@@ -253,9 +259,9 @@
         readouts.append(jnp.sum(fresh * c_out, axis=0, keepdims=True))
     readout = jnp.concatenate(readouts, axis=0) + skip_ref[layer : layer + 1, :] * signal
     gated = (readout * gate_ref[...]).astype(jnp.bfloat16)
-    width = held_ref.shape[1] // len(order)
+    width = out_ref.shape[2] // len(order)
     for block in range(len(order)):
-        if block * width % piece == 0:
+        if layer == 0 and block * width % piece == 0:
             copies[block * width // piece].wait()
         result = jnp.dot(
             gated,
@@ -282,7 +288,7 @@
         (a_log, layer),
         (skip_gain, None),
         (ssm_state, min(layer, ssm_state.shape[0] - 1)),
-        (far(out_weight), "far"),
+        (far(out_weight), "far") if layer == 0 else (out_weight, layer),
     ]
     aliases = {}
     if so_far is not None:
@@ -301,7 +307,9 @@
             ),
             ((a_log.shape[0], *ssm_state.shape[1:]), F32, layer),
         ],
-        [pltpu.VMEM(out_weight.shape[1:], jnp.bfloat16), pltpu.SemaphoreType.DMA((4,))],
+        [pltpu.VMEM(out_weight.shape[1:], jnp.bfloat16), pltpu.SemaphoreType.DMA((2,))]
+        if layer == 0
+        else [],
         aliases,
     )
     if layer:
@@ -371,8 +379,27 @@
 
 
 def attention_body(
-    arrived_ref, kv_ref, lengths_ref, table_ref, part_ref, pair_ref, questions_ref, scores_ref, *, block_len, dim
+    arrived_ref,
+    cache_ref,
+    lengths_ref,
+    table_ref,
+    part_ref,
+    pair_ref,
+    questions_ref,
+    scores_ref,
+    kv_ref,
+    done,
+    *,
+    block_len,
+    dim,
 ):
+    copies = []
+    for k in range(done.shape[0]):
+        slot_rows = pl.ds(k * 2 * block_len, 2 * block_len)
+        copies.append(
+            pltpu.make_async_copy(cache_ref.at[slot_rows, :], kv_ref.at[slot_rows, :], done.at[k])
+        )
+        copies[-1].start()
     summed = added_up(arrived_ref)
     requests = summed.shape[0]
     width = kv_ref.shape[1]
@@ -412,6 +439,7 @@
         filled = jnp.sum(jnp.where(table == first_slot + k, left, 0), axis=1, keepdims=True)
         visible = jnp.concatenate([(limit < filled).astype(F32)] * group_size, axis=0) > 0.5
         hidden_from.append(visible)
+        copies[k].wait()
         scores = against_rows(questions, kv_ref[k * chunk : (k + 1) * chunk, :]) * inv_sqrt
         scores = jnp.where(visible, scores, lowest_score)
         scores_ref[:, k * chunk : (k + 1) * chunk] = scores
@@ -538,7 +566,7 @@
         functools.partial(attention_body, block_len=block_len, dim=model_dim),
         [
             (exchange(copied(own, "z"), "z"), None),
-            (kv_rows, None),
+            (far(kv_rows), "far"),
             (lengths, "scalar"),
             (page_table, None),
         ],
@@ -546,7 +574,12 @@
             ((lax.axis_size("x"), rows + 8, width), WIRE, None),
             ((requests, 2 * width), F32, None),
         ],
-        [pltpu.VMEM((rows, width), F32), pltpu.VMEM((rows, kv_rows.shape[0]), F32)],
+        [
+            pltpu.VMEM((rows, width), F32),
+            pltpu.VMEM((rows, kv_rows.shape[0]), F32),
+            pltpu.VMEM(kv_rows.shape, jnp.bfloat16),
+            pltpu.SemaphoreType.DMA((pages_dev,)),
+        ],
     )
     (part,) = local_call(
         merge_body,
@@ -561,7 +594,7 @@
     added = jnp.sum(exchange(sums, CHAN_SUM).astype(F32), axis=0)
     stream_two = (stream_one.astype(F32) + added).astype(jnp.bfloat16)
     terms, signal, gate, new_conv = mamba_in(
-        exchange(copied(stream_two, SEQ), SEQ), 1, norm_gain, in_rows, *conv_args, new_conv
+        exchange(copied(stream_two, SEQ_SUM), SEQ_SUM), 1, norm_gain, in_rows, *conv_args, new_conv
     )
     arrived, new_ssm = mamba_out(
         sums_of_proj(terms), signal, gate, 1, dt_rows, ssm_state, *state_args, new_ssm

time: 176 us -> 176 us (level)
  no operation moved by 1% of the time
where the time goes in v6:
time: 176 us; the launch traced here: 175 us
  blocking collectives  159 us (90%)
  Pallas kernels  14.9 us (8%)
    all_to_all x13, blocking collectives, exchange(): return lax.all_to_all(copies, axes, split_axis=0, concat_axis=0, tiled=True)  159 us
    pallas_call x9, Pallas kernels, local_call(): pl.pallas_call(body, grid=(1,), in_specs=[spec(x.shape, layer) for x, lay...  14.9 us

profile of v6, /device:TPU:1, one launch (start us, length us, event | category | flops | bytes accessed | tf_op | source)
XLA Modules:
  0.0 175.3 jit_solution(17168681075987729739)
XLA Ops:
  0.6 0.0 copy-start.5
  0.6 0.0 copy-start.13
  0.7 0.0 copy-start.7
  0.7 0.0 copy-start.12
  0.7 0.0 copy-start.4
  0.7 0.0 copy-start.2
  0.7 0.0 copy-start.10
  0.7 0.0 copy-start.14
  0.7 3.7 %shard_map.201 = (bf16[16,8,544]{2,1,0:T(8,128)(2,1)S(1)}, f32[8,64]{1,0:T(8,128)S(1)}, f32[8,64]{1,0:T(8,128)S(1)}, bf16[2,3,8,64]{3,2,1,0:T(8,128)(2,1)}, bf16...) custom-call(bf16[8,8192]{1,0:T(8,128)(2,1)} %refs_0_.1, f32[3,8192]{1,0:T(4,128)} %refs_1_.3, ...), custom_call_target="tpu_custom_call" | custom-call | tf_op jit(solution)/shard_map/pallas_call | solution.py:52
  4.4 0.0 copy-start.6
  4.4 14.5 %all_to_all.65 = bf16[16,8,544]{2,1,0:T(8,128)(2,1)S(1)} all-to-all(bf16[16,8,544]{2,1,0:T(8,128)(2,1)S(1)} %get-tuple-element.24), channel_id=1, replica_groups=mesh['z'=8,'x'=4,'y'=4,'core'=2] {'x','y'}, dimensions={0} | all-to-all | bytes 278528 | tf_op jit(solution)/shard_map/all_to_all | solution.py:27
  18.9 0.0 copy-start.1
  18.9 0.0 copy-start.11
  19.0 18.2 %all_to_all.66.refs_0_ = bf16[16,8,544]{2,1,0:T(8,128)(2,1)S(1)} all-to-all(bf16[16,8,544]{2,1,0:T(8,128)(2,1)S(1)} %broadcast_in_dim.15), channel_id=1, replica_groups=mesh['z'=8,'x'=4,'y'=4,'core'=2] {'core','z'}, dimensions={0} | all-to-all | bytes 278528 | tf_op jit(solution)/shard_map/all_to_all | solution.py:27
  37.2 0.0 copy-done.5
  37.2 0.0 copy-done.13
  37.2 0.0 copy-done.7
  37.2 0.0 copy-done.12
  37.2 0.0 copy-done.4
  37.2 1.9 %shard_map.202 = (bf16[32,8,256]{2,1,0:T(8,128)(2,1)S(1)}, f32[2,8,16,64]{3,2,1,0:T(8,128)}) custom-call(bf16[16,8,544]{2,1,0:T(8,128)(2,1)S(1)} %all_to_all.66.refs_0_, f32[8,64]{1,0:T(8,128)S(1)} %get-tuple-element.25.refs_1_, f32[8,64]{1,0:T(8,128)S(1)} %get-tuple-element.26.refs_2_, bf16[2,64,512]{2,1,0:T(8,128)(2,1)S(1)} %bitcast.10, ...), custom_call_target="tpu_custom_call" | custom-call | tf_op jit(solution)/shard_map/pallas_call | solution.py:52
  39.1 13.7 %all_to_all.67 = bf16[32,8,256]{2,1,0:T(8,128)(2,1)S(1)} all-to-all(bf16[32,8,256]{2,1,0:T(8,128)(2,1)S(1)} %get-tuple-element.27), channel_id=1, replica_groups=mesh['z'=8,'x'=4,'y'=4,'core'=2] {'x','z'}, dimensions={0} | all-to-all | bytes 262144 | tf_op jit(solution)/shard_map/all_to_all | solution.py:27
  52.8 9.7 %all_to_all.68.arrived_ref = bf16[8,8,256]{2,1,0:T(8,128)(2,1)S(1)} all-to-all(bf16[8,8,256]{2,1,0:T(8,128)(2,1)S(1)} %broadcast_in_dim.16), channel_id=1, replica_groups=mesh['z'=8,'x'=4,'y'=4,'core'=2] {'core','y'}, dimensions={0} | all-to-all | bytes 65536 | tf_op jit(solution)/shard_map/all_to_all | solution.py:27
  62.5 0.0 copy-done.2
  62.5 0.2 shard_map.203
  62.7 7.0 %all_to_all.69 = bf16[4,8,1408]{2,1,0:T(8,128)(2,1)S(1)} all-to-all(bf16[4,8,1408]{2,1,0:T(8,128)(2,1)S(1)} %get-tuple-element.31), channel_id=1, replica_groups=mesh['z'=8,'x'=4,'y'=4,'core'=2] {'x'}, dimensions={0} | all-to-all | bytes 180224 | tf_op jit(solution)/shard_map/all_to_all | solution.py:27
  69.7 10.9 %all_to_all.70.arrived_ref = bf16[8,8,1408]{2,1,0:T(8,128)(2,1)S(1)} all-to-all(bf16[8,8,1408]{2,1,0:T(8,128)(2,1)S(1)} %broadcast_in_dim.17), channel_id=1, replica_groups=mesh['z'=8,'x'=4,'y'=4,'core'=2] {'z'}, dimensions={0} | all-to-all | bytes 360448 | tf_op jit(solution)/shard_map/all_to_all | solution.py:27
  80.7 0.0 copy-done.10
  80.7 0.0 copy-done.14
  80.7 4.2 %shard_map.204 = (bf16[4,72,128]{2,1,0:T(8,128)(2,1)S(1)}, f32[8,256]{1,0:T(8,128)S(1)}) custom-call(bf16[8,8,1408]{2,1,0:T(8,128)(2,1)S(1)} %all_to_all.70.arrived_ref, bf16[4096,128]{1,0:T(8,128)(2,1)} %bitcast.19, s32[8]{0:T(128)S(1)} %copy-done.14, s32[8,32]{1,0:T(8,128)S(1)} %copy-done.10), custom_call_target="tpu_custom_call" | custom-call | tf_op jit(solution)/shard_map/pallas_call | solution.py:52
  84.9 6.9 %all_to_all.71.arrived_ref = bf16[4,72,128]{2,1,0:T(8,128)(2,1)S(1)} all-to-all(bf16[4,72,128]{2,1,0:T(8,128)(2,1)S(1)} %get-tuple-element.32), channel_id=1, replica_groups=mesh['z'=8,'x'=4,'y'=4,'core'=2] {'x'}, dimensions={0} | all-to-all | bytes 147456 | tf_op jit(solution)/shard_map/all_to_all | solution.py:27
  91.8 0.1 shard_map.205
  91.9 10.5 %all_to_all.72.arrived_ref = bf16[8,72,128]{2,1,0:T(8,128)(2,1)S(1)} all-to-all(bf16[8,72,128]{2,1,0:T(8,128)(2,1)S(1)} %shard_map.205), channel_id=1, replica_groups=mesh['z'=8,'x'=4,'y'=4,'core'=2] {'z'}, dimensions={0} | all-to-all | bytes 294912 | tf_op jit(solution)/shard_map/all_to_all | solution.py:27
  102.4 0.0 copy-done.6
  102.4 0.3 shard_map.206
  102.7 12.3 %all_to_all.73 = bf16[8,8,256]{2,1,0:T(8,128)(2,1)S(1)} all-to-all(bf16[8,8,256]{2,1,0:T(8,128)(2,1)S(1)} %shard_map.206), channel_id=1, replica_groups=mesh['z'=8,'x'=4,'y'=4,'core'=2] {'core','y'}, dimensions={0} | all-to-all | bytes 65536 | tf_op jit(solution)/shard_map/all_to_all | solution.py:27
  115.1 12.1 %all_to_all.74.refs_0_ = bf16[32,8,256]{2,1,0:T(8,128)(2,1)S(1)} all-to-all(bf16[32,8,256]{2,1,0:T(8,128)(2,1)S(1)} %broadcast_in_dim.18), channel_id=1, replica_groups=mesh['z'=8,'x'=4,'y'=4,'core'=2] {'x','z'}, dimensions={0} | all-to-all | bytes 262144 | tf_op jit(solution)/shard_map/all_to_all | solution.py:27
  127.2 0.0 copy-done.1
  127.2 0.0 copy-done.3
  127.2 0.0 copy-done.8
  127.2 0.0 copy-done.9
  127.2 0.0 copy-done.11
  127.3 2.5 %shard_map.207 = (bf16[16,8,544]{2,1,0:T(8,128)(2,1)S(1)}, f32[8,64]{1,0:T(8,128)S(1)}, f32[8,64]{1,0:T(8,128)S(1)}, bf16[2,3,8,64]{3,2,1,0:T(8,128)(2,1)}) custom-call(bf16[32,8,256]{2,1,0:T(8,128)(2,1)S(1)} %all_to_all.74.refs_0_, f32[3,8192]{1,0:T(4,128)S(1)} %copy-done.3, bf16[2,2,64,8192]{3,2,1,0:T(8,128)(2,1)} %bitcast.18, ...), custom_call_target="tpu_custom_call", output_to_operand_aliasing={{3}: (7, {})} | custom-call | tf_op jit(solution)/shard_map/pallas_call | solution.py:52
  129.8 10.1 %all_to_all.75 = bf16[16,8,544]{2,1,0:T(8,128)(2,1)S(1)} all-to-all(bf16[16,8,544]{2,1,0:T(8,128)(2,1)S(1)} %get-tuple-element.34), channel_id=1, replica_groups=mesh['z'=8,'x'=4,'y'=4,'core'=2] {'x','y'}, dimensions={0} | all-to-all | bytes 278528 | tf_op jit(solution)/shard_map/all_to_all | solution.py:27
  140.0 13.4 %all_to_all.76.refs_0_ = bf16[16,8,544]{2,1,0:T(8,128)(2,1)S(1)} all-to-all(bf16[16,8,544]{2,1,0:T(8,128)(2,1)S(1)} %broadcast_in_dim.19), channel_id=1, replica_groups=mesh['z'=8,'x'=4,'y'=4,'core'=2] {'core','z'}, dimensions={0} | all-to-all | bytes 278528 | tf_op jit(solution)/shard_map/all_to_all | solution.py:27
  153.4 0.0 copy-done
  153.4 0.8 shard_map.208
  154.2 19.9 %all_to_all.77 = bf16[256,2,128]{2,1,0:T(2,128)(2,1)S(1)} all-to-all(bf16[256,2,128]{2,1,0:T(2,128)(2,1)S(1)} %bitcast.14), channel_id=1, replica_groups=mesh['z'=8,'x'=4,'y'=4,'core'=2] {'core','z','x','y'}, dimensions={0} | all-to-all | bytes 262144 | tf_op jit(solution)/shard_map/all_to_all | solution.py:27
  174.1 1.1 shard_map.209
  (15 shorter events, 0.2 us)
Async XLA Ops:
  0.6 36.5 %copy-start.5 = (f32[2,8,16,64]{3,2,1,0:T(8,128)S(1)}, f32[2,8,16,64]{3,2,1,0:T(8,128)}, u32[]{:S(2)}) copy-start(f32[2,8,16,64]{3,2,1,0:T(8,128)} %refs_7_.3) | copy-start | bytes 196612
  0.6 36.5 %copy-start.13 = (f32[2,64]{1,0:T(2,128)S(1)}, f32[2,64]{1,0:T(2,128)}, u32[]{:S(2)}) copy-start(f32[2,64]{1,0:T(2,128)} %refs_6_.7) | copy-start | bytes 1540
  0.7 36.5 %copy-start.7 = (f32[2,16,64]{2,1,0:T(8,128)S(1)}, f32[2,16,64]{2,1,0:T(8,128)}, u32[]{:S(2)}) copy-start(f32[2,16,64]{2,1,0:T(8,128)} %refs_5_.3) | copy-start | bytes 24580
  0.7 36.5 %copy-start.12 = (f32[2,64]{1,0:T(2,128)S(1)}, f32[2,64]{1,0:T(2,128)}, u32[]{:S(2)}) copy-start(f32[2,64]{1,0:T(2,128)} %refs_4_.7) | copy-start | bytes 1540
  0.7 36.5 %copy-start.4 = (bf16[2,512,64]{1,2,0:T(8,128)(2,1)S(1)}, bf16[2,512,64]{1,2,0:T(8,128)(2,1)}, u32[]{:S(2)}) copy-start(bf16[2,512,64]{1,2,0:T(8,128)(2,1)} %param.25) | copy-start | bytes 393220
  0.7 61.8 %copy-start.2 = (bf16[256,1,1280]{2,0,1:T(8,128)(2,1)S(1)}, bf16[256,1,1280]{2,0,1:T(8,128)(2,1)}, u32[]{:S(2)}) copy-start(bf16[256,1,1280]{2,0,1:T(8,128)(2,1)} %param.31) | copy-start | bytes 1966084
  0.7 80.0 %copy-start.10 = (s32[8,32]{1,0:T(8,128)S(1)}, s32[8,32]{1,0:T(8,128)}, u32[]{:S(2)}) copy-start(s32[8,32]{1,0:T(8,128)} %table_ref.1) | copy-start | bytes 3076
  0.7 80.0 %copy-start.14 = (s32[8]{0:T(128)S(1)}, s32[8]{0:T(128)}, u32[]{:S(2)}) copy-start(s32[8]{0:T(128)} %lengths_ref.1) | copy-start | bytes 100
  4.4 98.0 %copy-start.6 = (bf16[1,1024,256]{2,1,0:T(8,128)(2,1)S(1)}, bf16[1,1024,256]{2,1,0:T(8,128)(2,1)}, u32[]{:S(2)}) copy-start(bf16[1,1024,256]{2,1,0:T(8,128)(2,1)} %param.32) | copy-start | bytes 1572868
  18.9 108.3 %copy-start.1 = (bf16[2,64,544]{2,1,0:T(8,128)(2,1)S(1)}, bf16[2,64,544]{2,1,0:T(8,128)(2,1)}, u32[]{:S(2)}) copy-start(bf16[2,64,544]{2,1,0:T(8,128)(2,1)} %refs_6_.6) | copy-start | bytes 417796
  18.9 108.3 %copy-start.3 = (f32[3,8192]{1,0:T(4,128)S(1)}, f32[3,8192]{1,0:T(4,128)}, u32[]{:S(2)}) copy-start(f32[3,8192]{1,0:T(4,128)} %refs_1_.3) | copy-start | bytes 294916
  18.9 108.3 %copy-start.8 = (bf16[2,8,3,64]{3,1,2,0:T(8,128)(2,1)S(1)}, bf16[2,8,3,64]{3,1,2,0:T(8,128)(2,1)}, u32[]{:S(2)}) copy-start(bf16[2,8,3,64]{3,1,2,0:T(8,128)(2,1)} %param.23) | copy-start | bytes 18436
  18.9 108.3 %copy-start.9 = (f32[2,4,64]{2,1,0:T(4,128)S(1)}, f32[2,4,64]{2,1,0:T(4,128)}, u32[]{:S(2)}) copy-start(f32[2,4,64]{2,1,0:T(4,128)} %refs_3_.3) | copy-start | bytes 6148
  18.9 108.3 %copy-start.11 = (f32[2,64]{1,0:T(2,128)S(1)}, f32[2,64]{1,0:T(2,128)}, u32[]{:S(2)}) copy-start(f32[2,64]{1,0:T(2,128)} %refs_4_.6) | copy-start | bytes 1540
  80.7 72.7 %copy-start = (bf16[2,64,8192]{2,1,0:T(8,128)(2,1)S(1)}, bf16[2,64,8192]{2,1,0:T(8,128)(2,1)}, u32[]{:S(2)}) copy-start(bf16[2,64,8192]{2,1,0:T(8,128)(2,1)} %refs_8_.3) | copy-start | bytes 6291460

commit v7 on v5

--- a/solution.py
+++ b/solution.py
@@ -212,9 +212,13 @@
     arrived_ref, signal_ref, gate_ref, dt_ref, bias_ref, decay_ref, skip_ref, state_ref, out_ref = (
         refs[:9]
     )
-    blocks_ref, fresh_ref, held_ref, done = refs[-4:]
-    pieces = done.shape[0]
-    piece = held_ref.shape[1] // pieces
+    blocks_ref, fresh_ref = refs[9:11] if layer == 0 else refs[10:12]
+    if layer == 0:
+        held_ref, done = refs[11:]
+    else:
+        held_ref = out_ref.at[0]
+    pieces = 2 if layer == 0 else 0
+    piece = out_ref.shape[2] // max(pieces, 1)
     copies = [
         pltpu.make_async_copy(
             out_ref.at[layer, :, pl.ds(k * piece, piece)],
@@ -253,9 +257,9 @@
         readouts.append(jnp.sum(fresh * c_out, axis=0, keepdims=True))
     readout = jnp.concatenate(readouts, axis=0) + skip_ref[layer : layer + 1, :] * signal
     gated = (readout * gate_ref[...]).astype(jnp.bfloat16)
-    width = held_ref.shape[1] // len(order)
+    width = out_ref.shape[2] // len(order)
     for block in range(len(order)):
-        if block * width % piece == 0:
+        if layer == 0 and block * width % piece == 0:
             copies[block * width // piece].wait()
         result = jnp.dot(
             gated,
@@ -282,7 +286,7 @@
         (a_log, layer),
         (skip_gain, None),
         (ssm_state, min(layer, ssm_state.shape[0] - 1)),
-        (far(out_weight), "far"),
+        (far(out_weight), "far") if layer == 0 else (out_weight, layer),
     ]
     aliases = {}
     if so_far is not None:
@@ -301,7 +305,9 @@
             ),
             ((a_log.shape[0], *ssm_state.shape[1:]), F32, layer),
         ],
-        [pltpu.VMEM(out_weight.shape[1:], jnp.bfloat16), pltpu.SemaphoreType.DMA((4,))],
+        [pltpu.VMEM(out_weight.shape[1:], jnp.bfloat16), pltpu.SemaphoreType.DMA((2,))]
+        if layer == 0
+        else [],
         aliases,
     )
     if layer:

time: 176 us -> 175 us (level)
  Pallas kernels: 14.5 us -> 12.5 us
    pallas_call x9, Pallas kernels: 14.5 us -> 12.5 us  [local_call(): pl.pallas_call(body, grid=(1,), in_specs=[spec(x.shape, layer) for x, lay...]
where the time goes in v7:
time: 175 us; the launch traced here: 174 us
  blocking collectives  159 us (91%)
  Pallas kernels  12.5 us (7%)
    all_to_all x13, blocking collectives, exchange(): return lax.all_to_all(copies, axes, split_axis=0, concat_axis=0, tiled=True)  159 us
    pallas_call x9, Pallas kernels, local_call(): pl.pallas_call(body, grid=(1,), in_specs=[spec(x.shape, layer) for x, lay...  12.5 us

profile of v7, /device:TPU:1, one launch (start us, length us, event | category | flops | bytes accessed | tf_op | source)
XLA Modules:
  0.0 174.0 jit_solution(14710952456575265958)
XLA Ops:
  0.6 0.0 copy-start.7
  0.6 0.0 copy-start.16
  0.7 0.0 copy-start.10
  0.7 0.0 copy-start.15
  0.7 0.0 copy-start.5
  0.7 0.0 copy-start.3
  0.7 0.0 copy-start.1
  0.7 0.0 copy-start.13
  0.7 0.0 copy-start.17
  0.7 3.7 %shard_map.201 = (bf16[16,8,544]{2,1,0:T(8,128)(2,1)S(1)}, f32[8,64]{1,0:T(8,128)S(1)}, f32[8,64]{1,0:T(8,128)S(1)}, bf16[2,3,8,64]{3,2,1,0:T(8,128)(2,1)}, bf16...) custom-call(bf16[8,8192]{1,0:T(8,128)(2,1)} %refs_0_.1, f32[3,8192]{1,0:T(4,128)} %refs_1_.3, ...), custom_call_target="tpu_custom_call" | custom-call | tf_op jit(solution)/shard_map/pallas_call | solution.py:52
  4.4 14.4 %all_to_all.65 = bf16[16,8,544]{2,1,0:T(8,128)(2,1)S(1)} all-to-all(bf16[16,8,544]{2,1,0:T(8,128)(2,1)S(1)} %get-tuple-element.24), channel_id=1, replica_groups=mesh['z'=8,'x'=4,'y'=4,'core'=2] {'x','y'}, dimensions={0} | all-to-all | bytes 278528 | tf_op jit(solution)/shard_map/all_to_all | solution.py:27
  18.8 0.0 copy-start.14
  18.9 18.2 %all_to_all.66.refs_0_ = bf16[16,8,544]{2,1,0:T(8,128)(2,1)S(1)} all-to-all(bf16[16,8,544]{2,1,0:T(8,128)(2,1)S(1)} %broadcast_in_dim.15), channel_id=1, replica_groups=mesh['z'=8,'x'=4,'y'=4,'core'=2] {'core','z'}, dimensions={0} | all-to-all | bytes 278528 | tf_op jit(solution)/shard_map/all_to_all | solution.py:27
  37.1 0.0 copy-done.7
  37.1 0.0 copy-done.16
  37.1 0.0 copy-done.10
  37.1 0.0 copy-done.15
  37.1 0.0 copy-done.5
  37.1 1.9 %shard_map.202 = (bf16[32,8,256]{2,1,0:T(8,128)(2,1)S(1)}, f32[2,8,16,64]{3,2,1,0:T(8,128)}) custom-call(bf16[16,8,544]{2,1,0:T(8,128)(2,1)S(1)} %all_to_all.66.refs_0_, f32[8,64]{1,0:T(8,128)S(1)} %get-tuple-element.25.refs_1_, f32[8,64]{1,0:T(8,128)S(1)} %get-tuple-element.26.refs_2_, bf16[2,64,512]{2,1,0:T(8,128)(2,1)S(1)} %bitcast.11, ...), custom_call_target="tpu_custom_call" | custom-call | tf_op jit(solution)/shard_map/pallas_call | solution.py:52
  39.0 13.7 %all_to_all.67 = bf16[32,8,256]{2,1,0:T(8,128)(2,1)S(1)} all-to-all(bf16[32,8,256]{2,1,0:T(8,128)(2,1)S(1)} %get-tuple-element.27), channel_id=1, replica_groups=mesh['z'=8,'x'=4,'y'=4,'core'=2] {'x','z'}, dimensions={0} | all-to-all | bytes 262144 | tf_op jit(solution)/shard_map/all_to_all | solution.py:27
  52.7 9.6 %all_to_all.68.arrived_ref = bf16[8,8,256]{2,1,0:T(8,128)(2,1)S(1)} all-to-all(bf16[8,8,256]{2,1,0:T(8,128)(2,1)S(1)} %broadcast_in_dim.16), channel_id=1, replica_groups=mesh['z'=8,'x'=4,'y'=4,'core'=2] {'core','y'}, dimensions={0} | all-to-all | bytes 65536 | tf_op jit(solution)/shard_map/all_to_all | solution.py:27
  62.4 0.0 copy-done.3
  62.4 0.2 shard_map.203
  62.6 7.0 %all_to_all.69 = bf16[4,8,1408]{2,1,0:T(8,128)(2,1)S(1)} all-to-all(bf16[4,8,1408]{2,1,0:T(8,128)(2,1)S(1)} %get-tuple-element.31), channel_id=1, replica_groups=mesh['z'=8,'x'=4,'y'=4,'core'=2] {'x'}, dimensions={0} | all-to-all | bytes 180224 | tf_op jit(solution)/shard_map/all_to_all | solution.py:27
  69.6 10.9 %all_to_all.70.arrived_ref = bf16[8,8,1408]{2,1,0:T(8,128)(2,1)S(1)} all-to-all(bf16[8,8,1408]{2,1,0:T(8,128)(2,1)S(1)} %broadcast_in_dim.17), channel_id=1, replica_groups=mesh['z'=8,'x'=4,'y'=4,'core'=2] {'z'}, dimensions={0} | all-to-all | bytes 360448 | tf_op jit(solution)/shard_map/all_to_all | solution.py:27
  80.6 0.0 copy-done.1
  80.6 0.0 copy-done.13
  80.6 0.0 copy-done.17
  80.6 0.0 copy-start
  80.6 1.8 %shard_map.204 = (bf16[4,72,128]{2,1,0:T(8,128)(2,1)S(1)}, f32[8,256]{1,0:T(8,128)S(1)}) custom-call(bf16[8,8,1408]{2,1,0:T(8,128)(2,1)S(1)} %all_to_all.70.arrived_ref, bf16[4096,128]{1,0:T(8,128)(2,1)S(1)} %bitcast.9, s32[8]{0:T(128)S(1)} %copy-done.17, s32[8,32]{1,0:T(8,128)S(1)} %copy-done.13), custom_call_target="tpu_custom_call" | custom-call | tf_op jit(solution)/shard_map/pallas_call | solution.py:52
  82.4 0.0 copy-start.6
  82.4 0.0 copy-start.8
  82.4 7.0 %all_to_all.71.arrived_ref = bf16[4,72,128]{2,1,0:T(8,128)(2,1)S(1)} all-to-all(bf16[4,72,128]{2,1,0:T(8,128)(2,1)S(1)} %get-tuple-element.32), channel_id=1, replica_groups=mesh['z'=8,'x'=4,'y'=4,'core'=2] {'x'}, dimensions={0} | all-to-all | bytes 147456 | tf_op jit(solution)/shard_map/all_to_all | solution.py:27
  89.4 0.1 shard_map.205
  89.5 10.5 %all_to_all.72.arrived_ref = bf16[8,72,128]{2,1,0:T(8,128)(2,1)S(1)} all-to-all(bf16[8,72,128]{2,1,0:T(8,128)(2,1)S(1)} %shard_map.205), channel_id=1, replica_groups=mesh['z'=8,'x'=4,'y'=4,'core'=2] {'z'}, dimensions={0} | all-to-all | bytes 294912 | tf_op jit(solution)/shard_map/all_to_all | solution.py:27
  100.0 1.0 copy-done.9
  101.1 0.3 shard_map.206
  101.4 12.3 %all_to_all.73 = bf16[8,8,256]{2,1,0:T(8,128)(2,1)S(1)} all-to-all(bf16[8,8,256]{2,1,0:T(8,128)(2,1)S(1)} %shard_map.206), channel_id=1, replica_groups=mesh['z'=8,'x'=4,'y'=4,'core'=2] {'core','y'}, dimensions={0} | all-to-all | bytes 65536 | tf_op jit(solution)/shard_map/all_to_all | solution.py:27
  113.7 12.7 %all_to_all.74.refs_0_ = bf16[32,8,256]{2,1,0:T(8,128)(2,1)S(1)} all-to-all(bf16[32,8,256]{2,1,0:T(8,128)(2,1)S(1)} %broadcast_in_dim.18), channel_id=1, replica_groups=mesh['z'=8,'x'=4,'y'=4,'core'=2] {'z','x'}, dimensions={0} | all-to-all | bytes 262144 | tf_op jit(solution)/shard_map/all_to_all | solution.py:27
  126.5 0.0 copy-done.2
  126.5 0.0 copy-done.11
  126.5 2.5 %shard_map.207 = (bf16[16,8,544]{2,1,0:T(8,128)(2,1)S(1)}, f32[8,64]{1,0:T(8,128)S(1)}, f32[8,64]{1,0:T(8,128)S(1)}, bf16[2,3,8,64]{3,2,1,0:T(8,128)(2,1)}) custom-call(bf16[32,8,256]{2,1,0:T(8,128)(2,1)S(1)} %all_to_all.74.refs_0_, f32[3,8192]{1,0:T(4,128)S(1)} %copy-done.4, bf16[2,2,64,8192]{3,2,1,0:T(8,128)(2,1)} %bitcast.19, ...), custom_call_target="tpu_custom_call", output_to_operand_aliasing={{3}: (7, {})} | custom-call | tf_op jit(solution)/shard_map/pallas_call | solution.py:52
  129.1 9.7 %all_to_all.75 = bf16[16,8,544]{2,1,0:T(8,128)(2,1)S(1)} all-to-all(bf16[16,8,544]{2,1,0:T(8,128)(2,1)S(1)} %get-tuple-element.34), channel_id=1, replica_groups=mesh['z'=8,'x'=4,'y'=4,'core'=2] {'x','y'}, dimensions={0} | all-to-all | bytes 278528 | tf_op jit(solution)/shard_map/all_to_all | solution.py:27
  138.9 13.3 %all_to_all.76.refs_0_ = bf16[16,8,544]{2,1,0:T(8,128)(2,1)S(1)} all-to-all(bf16[16,8,544]{2,1,0:T(8,128)(2,1)S(1)} %broadcast_in_dim.19), channel_id=1, replica_groups=mesh['z'=8,'x'=4,'y'=4,'core'=2] {'core','z'}, dimensions={0} | all-to-all | bytes 278528 | tf_op jit(solution)/shard_map/all_to_all | solution.py:27
  152.1 0.0 copy-done.6
  152.2 0.8 shard_map.208
  153.0 19.9 %all_to_all.77 = bf16[256,2,128]{2,1,0:T(2,128)(2,1)S(1)} all-to-all(bf16[256,2,128]{2,1,0:T(2,128)(2,1)S(1)} %bitcast.15), channel_id=1, replica_groups=mesh['z'=8,'x'=4,'y'=4,'core'=2] {'core','z','x','y'}, dimensions={0} | all-to-all | bytes 262144 | tf_op jit(solution)/shard_map/all_to_all | solution.py:27
  172.9 1.1 shard_map.209
  (21 shorter events, 0.2 us)
Async XLA Ops:
  0.6 36.4 %copy-start.7 = (f32[2,8,16,64]{3,2,1,0:T(8,128)S(1)}, f32[2,8,16,64]{3,2,1,0:T(8,128)}, u32[]{:S(2)}) copy-start(f32[2,8,16,64]{3,2,1,0:T(8,128)} %refs_7_.3) | copy-start | bytes 196612
  0.6 36.4 %copy-start.16 = (f32[2,64]{1,0:T(2,128)S(1)}, f32[2,64]{1,0:T(2,128)}, u32[]{:S(2)}) copy-start(f32[2,64]{1,0:T(2,128)} %refs_6_.7) | copy-start | bytes 1540
  0.7 36.4 %copy-start.10 = (f32[2,16,64]{2,1,0:T(8,128)S(1)}, f32[2,16,64]{2,1,0:T(8,128)}, u32[]{:S(2)}) copy-start(f32[2,16,64]{2,1,0:T(8,128)} %refs_5_.3) | copy-start | bytes 24580
  0.7 36.4 %copy-start.15 = (f32[2,64]{1,0:T(2,128)S(1)}, f32[2,64]{1,0:T(2,128)}, u32[]{:S(2)}) copy-start(f32[2,64]{1,0:T(2,128)} %refs_4_.7) | copy-start | bytes 1540
  0.7 36.4 %copy-start.5 = (bf16[2,512,64]{1,2,0:T(8,128)(2,1)S(1)}, bf16[2,512,64]{1,2,0:T(8,128)(2,1)}, u32[]{:S(2)}) copy-start(bf16[2,512,64]{1,2,0:T(8,128)(2,1)} %param.25) | copy-start | bytes 393220
  0.7 61.7 %copy-start.3 = (bf16[256,1,1280]{2,0,1:T(8,128)(2,1)S(1)}, bf16[256,1,1280]{2,0,1:T(8,128)(2,1)}, u32[]{:S(2)}) copy-start(bf16[256,1,1280]{2,0,1:T(8,128)(2,1)} %param.31) | copy-start | bytes 1966084
  0.7 79.9 %copy-start.1 = (bf16[8,256,2,1,128]{4,2,3,1,0:T(2,128)(2,1)S(1)}, bf16[8,256,2,1,128]{4,2,3,1,0:T(2,128)(2,1)}, u32[]{:S(2)}) copy-start(bf16[8,256,2,1,128]{4,2,3,1,0:T(2,128)(2,1)} %param.33) | copy-start | bytes 3145732
  0.7 79.9 %copy-start.13 = (s32[8,32]{1,0:T(8,128)S(1)}, s32[8,32]{1,0:T(8,128)}, u32[]{:S(2)}) copy-start(s32[8,32]{1,0:T(8,128)} %table_ref.1) | copy-start | bytes 3076
  0.7 79.9 %copy-start.17 = (s32[8]{0:T(128)S(1)}, s32[8]{0:T(128)}, u32[]{:S(2)}) copy-start(s32[8]{0:T(128)} %lengths_ref.1) | copy-start | bytes 100
  18.8 107.7 %copy-start.2 = (bf16[2,64,544]{2,1,0:T(8,128)(2,1)S(1)}, bf16[2,64,544]{2,1,0:T(8,128)(2,1)}, u32[]{:S(2)}) copy-start(bf16[2,64,544]{2,1,0:T(8,128)(2,1)} %refs_6_.6) | copy-start | bytes 417796
  18.8 107.7 %copy-start.4 = (f32[3,8192]{1,0:T(4,128)S(1)}, f32[3,8192]{1,0:T(4,128)}, u32[]{:S(2)}) copy-start(f32[3,8192]{1,0:T(4,128)} %refs_1_.3) | copy-start | bytes 294916
  18.8 107.7 %copy-start.11 = (bf16[2,8,3,64]{3,1,2,0:T(8,128)(2,1)S(1)}, bf16[2,8,3,64]{3,1,2,0:T(8,128)(2,1)}, u32[]{:S(2)}) copy-start(bf16[2,8,3,64]{3,1,2,0:T(8,128)(2,1)} %param.23) | copy-start | bytes 18436
  18.8 107.7 %copy-start.12 = (f32[2,4,64]{2,1,0:T(4,128)S(1)}, f32[2,4,64]{2,1,0:T(4,128)}, u32[]{:S(2)}) copy-start(f32[2,4,64]{2,1,0:T(4,128)} %refs_3_.3) | copy-start | bytes 6148
  18.8 107.7 %copy-start.14 = (f32[2,64]{1,0:T(2,128)S(1)}, f32[2,64]{1,0:T(2,128)}, u32[]{:S(2)}) copy-start(f32[2,64]{1,0:T(2,128)} %refs_4_.6) | copy-start | bytes 1540
  80.6 71.6 %copy-start = (bf16[2,64,8192]{2,1,0:T(8,128)(2,1)S(1)}, bf16[2,64,8192]{2,1,0:T(8,128)(2,1)}, u32[]{:S(2)}) copy-start(bf16[2,64,8192]{2,1,0:T(8,128)(2,1)} %refs_8_.3) | copy-start | bytes 6291460
  82.4 69.8 %copy-start.6 = (bf16[2,512,64]{1,2,0:T(8,128)(2,1)S(1)}, bf16[2,512,64]{1,2,0:T(8,128)(2,1)}, u32[]{:S(2)}) copy-start(bf16[2,512,64]{1,2,0:T(8,128)(2,1)} %param.25) | copy-start | bytes 393220
  82.4 69.8 %copy-start.8 = (f32[2,8,16,64]{3,2,1,0:T(8,128)S(1)}, f32[2,8,16,64]{3,2,1,0:T(8,128)}, u32[]{:S(2)}) copy-start(f32[2,8,16,64]{3,2,1,0:T(8,128)} %refs_7_.3) | copy-start | bytes 196612
  100.0 1.0 copy-start.9

commit v8 on v7

--- a/solution.py
+++ b/solution.py
@@ -443,12 +443,15 @@
     store_part(part_ref, top, total, mixed)
 
 
-def attention_out_body(arrived_ref, weight_ref, sums_ref):
+def attention_out_body(arrived_ref, far_ref, sums_ref, weight_ref, done):
+    copy = pltpu.make_async_copy(far_ref, weight_ref, done.at[0])
+    copy.start()
     _, total, mixed = merged(arrived_ref)
     attended = (mixed / flip(total)).astype(jnp.bfloat16)
     requests = sums_ref.shape[1]
     width = attended.shape[1]
     result = jnp.zeros(sums_ref.shape[1:], F32)
+    copy.wait()
     for g in range(attended.shape[0] // requests):
         result = result + jnp.dot(
             attended[g * requests : (g + 1) * requests],
@@ -561,8 +564,9 @@
     )
     (sums,) = local_call(
         attention_out_body,
-        [(exchange(part, "z"), None), (o_weight[0], None)],
+        [(exchange(part, "z"), None), (far(o_weight[0]), "far")],
         [((lax.axis_size(CHAN), requests, block_cols), WIRE, None)],
+        [pltpu.VMEM(o_weight.shape[1:], jnp.bfloat16), pltpu.SemaphoreType.DMA((1,))],
     )
     added = jnp.sum(exchange(sums, CHAN_SUM).astype(F32), axis=0)
     stream_two = (stream_one.astype(F32) + added).astype(jnp.bfloat16)

time: 175 us -> 175 us (level)
  no operation moved by 1% of the time
where the time goes in v8:
time: 175 us; the launch traced here: 174 us
  blocking collectives  159 us (91%)
  Pallas kernels  13.4 us (8%)
    all_to_all x13, blocking collectives, exchange(): return lax.all_to_all(copies, axes, split_axis=0, concat_axis=0, tiled=True)  159 us
    pallas_call x9, Pallas kernels, local_call(): pl.pallas_call(body, grid=(1,), in_specs=[spec(x.shape, layer) for x, lay...  13.4 us

profile of v8, /device:TPU:1, one launch (start us, length us, event | category | flops | bytes accessed | tf_op | source)
XLA Modules:
  0.0 173.9 jit_solution(1611731525705469484)
XLA Ops:
  0.6 0.0 copy-start.7
  0.6 0.0 copy-start.15
  0.7 0.0 copy-start.9
  0.7 0.0 copy-start.14
  0.7 0.0 copy-start.5
  0.7 0.0 copy-start.3
  0.7 0.0 copy-start.1
  0.7 0.0 copy-start.12
  0.7 0.0 copy-start.16
  0.7 3.7 %shard_map.201 = (bf16[16,8,544]{2,1,0:T(8,128)(2,1)S(1)}, f32[8,64]{1,0:T(8,128)S(1)}, f32[8,64]{1,0:T(8,128)S(1)}, bf16[2,3,8,64]{3,2,1,0:T(8,128)(2,1)}, bf16...) custom-call(bf16[8,8192]{1,0:T(8,128)(2,1)} %refs_0_.1, f32[3,8192]{1,0:T(4,128)} %refs_1_.3, ...), custom_call_target="tpu_custom_call" | custom-call | tf_op jit(solution)/shard_map/pallas_call | solution.py:52
  4.4 14.4 %all_to_all.65 = bf16[16,8,544]{2,1,0:T(8,128)(2,1)S(1)} all-to-all(bf16[16,8,544]{2,1,0:T(8,128)(2,1)S(1)} %get-tuple-element.24), channel_id=1, replica_groups=mesh['z'=8,'x'=4,'y'=4,'core'=2] {'x','y'}, dimensions={0} | all-to-all | bytes 278528 | tf_op jit(solution)/shard_map/all_to_all | solution.py:27
  18.8 0.0 copy-start.13
  18.9 18.2 %all_to_all.66.refs_0_ = bf16[16,8,544]{2,1,0:T(8,128)(2,1)S(1)} all-to-all(bf16[16,8,544]{2,1,0:T(8,128)(2,1)S(1)} %broadcast_in_dim.15), channel_id=1, replica_groups=mesh['z'=8,'x'=4,'y'=4,'core'=2] {'core','z'}, dimensions={0} | all-to-all | bytes 278528 | tf_op jit(solution)/shard_map/all_to_all | solution.py:27
  37.1 0.0 copy-done.7
  37.1 0.0 copy-done.15
  37.1 0.0 copy-done.9
  37.1 0.0 copy-done.14
  37.1 0.0 copy-done.5
  37.1 1.9 %shard_map.202 = (bf16[32,8,256]{2,1,0:T(8,128)(2,1)S(1)}, f32[2,8,16,64]{3,2,1,0:T(8,128)}) custom-call(bf16[16,8,544]{2,1,0:T(8,128)(2,1)S(1)} %all_to_all.66.refs_0_, f32[8,64]{1,0:T(8,128)S(1)} %get-tuple-element.25.refs_1_, f32[8,64]{1,0:T(8,128)S(1)} %get-tuple-element.26.refs_2_, bf16[2,64,512]{2,1,0:T(8,128)(2,1)S(1)} %bitcast.11, ...), custom_call_target="tpu_custom_call" | custom-call | tf_op jit(solution)/shard_map/pallas_call | solution.py:52
  39.0 13.7 %all_to_all.67 = bf16[32,8,256]{2,1,0:T(8,128)(2,1)S(1)} all-to-all(bf16[32,8,256]{2,1,0:T(8,128)(2,1)S(1)} %get-tuple-element.27), channel_id=1, replica_groups=mesh['z'=8,'x'=4,'y'=4,'core'=2] {'x','z'}, dimensions={0} | all-to-all | bytes 262144 | tf_op jit(solution)/shard_map/all_to_all | solution.py:27
  52.7 9.6 %all_to_all.68.arrived_ref = bf16[8,8,256]{2,1,0:T(8,128)(2,1)S(1)} all-to-all(bf16[8,8,256]{2,1,0:T(8,128)(2,1)S(1)} %broadcast_in_dim.16), channel_id=1, replica_groups=mesh['z'=8,'x'=4,'y'=4,'core'=2] {'core','y'}, dimensions={0} | all-to-all | bytes 65536 | tf_op jit(solution)/shard_map/all_to_all | solution.py:27
  62.4 0.0 copy-done.3
  62.4 0.2 shard_map.203
  62.6 7.0 %all_to_all.69 = bf16[4,8,1408]{2,1,0:T(8,128)(2,1)S(1)} all-to-all(bf16[4,8,1408]{2,1,0:T(8,128)(2,1)S(1)} %get-tuple-element.31), channel_id=1, replica_groups=mesh['z'=8,'x'=4,'y'=4,'core'=2] {'x'}, dimensions={0} | all-to-all | bytes 180224 | tf_op jit(solution)/shard_map/all_to_all | solution.py:27
  69.6 10.9 %all_to_all.70.arrived_ref = bf16[8,8,1408]{2,1,0:T(8,128)(2,1)S(1)} all-to-all(bf16[8,8,1408]{2,1,0:T(8,128)(2,1)S(1)} %broadcast_in_dim.17), channel_id=1, replica_groups=mesh['z'=8,'x'=4,'y'=4,'core'=2] {'z'}, dimensions={0} | all-to-all | bytes 360448 | tf_op jit(solution)/shard_map/all_to_all | solution.py:27
  80.6 0.0 copy-done.1
  80.6 0.0 copy-done.12
  80.6 0.0 copy-done.16
  80.6 0.0 copy-start
  80.6 1.8 %shard_map.204 = (bf16[4,72,128]{2,1,0:T(8,128)(2,1)S(1)}, f32[8,256]{1,0:T(8,128)S(1)}) custom-call(bf16[8,8,1408]{2,1,0:T(8,128)(2,1)S(1)} %all_to_all.70.arrived_ref, bf16[4096,128]{1,0:T(8,128)(2,1)S(1)} %bitcast.9, s32[8]{0:T(128)S(1)} %copy-done.16, s32[8,32]{1,0:T(8,128)S(1)} %copy-done.12), custom_call_target="tpu_custom_call" | custom-call | tf_op jit(solution)/shard_map/pallas_call | solution.py:52
  82.4 0.0 copy-start.6
  82.4 0.0 copy-start.8
  82.4 7.0 %all_to_all.71.arrived_ref = bf16[4,72,128]{2,1,0:T(8,128)(2,1)S(1)} all-to-all(bf16[4,72,128]{2,1,0:T(8,128)(2,1)S(1)} %get-tuple-element.32), channel_id=1, replica_groups=mesh['z'=8,'x'=4,'y'=4,'core'=2] {'x'}, dimensions={0} | all-to-all | bytes 147456 | tf_op jit(solution)/shard_map/all_to_all | solution.py:27
  89.4 0.1 shard_map.205
  89.5 10.5 %all_to_all.72.arrived_ref = bf16[8,72,128]{2,1,0:T(8,128)(2,1)S(1)} all-to-all(bf16[8,72,128]{2,1,0:T(8,128)(2,1)S(1)} %shard_map.205), channel_id=1, replica_groups=mesh['z'=8,'x'=4,'y'=4,'core'=2] {'z'}, dimensions={0} | all-to-all | bytes 294912 | tf_op jit(solution)/shard_map/all_to_all | solution.py:27
  100.0 1.2 shard_map.206
  101.3 12.3 %all_to_all.73 = bf16[8,8,256]{2,1,0:T(8,128)(2,1)S(1)} all-to-all(bf16[8,8,256]{2,1,0:T(8,128)(2,1)S(1)} %shard_map.206), channel_id=1, replica_groups=mesh['z'=8,'x'=4,'y'=4,'core'=2] {'core','y'}, dimensions={0} | all-to-all | bytes 65536 | tf_op jit(solution)/shard_map/all_to_all | solution.py:27
  113.7 12.7 %all_to_all.74.refs_0_ = bf16[32,8,256]{2,1,0:T(8,128)(2,1)S(1)} all-to-all(bf16[32,8,256]{2,1,0:T(8,128)(2,1)S(1)} %broadcast_in_dim.18), channel_id=1, replica_groups=mesh['z'=8,'x'=4,'y'=4,'core'=2] {'z','x'}, dimensions={0} | all-to-all | bytes 262144 | tf_op jit(solution)/shard_map/all_to_all | solution.py:27
  126.4 0.0 copy-done.2
  126.4 0.0 copy-done.4
  126.4 2.5 %shard_map.207 = (bf16[16,8,544]{2,1,0:T(8,128)(2,1)S(1)}, f32[8,64]{1,0:T(8,128)S(1)}, f32[8,64]{1,0:T(8,128)S(1)}, bf16[2,3,8,64]{3,2,1,0:T(8,128)(2,1)}) custom-call(bf16[32,8,256]{2,1,0:T(8,128)(2,1)S(1)} %all_to_all.74.refs_0_, f32[3,8192]{1,0:T(4,128)S(1)} %copy-done.4, bf16[2,2,64,8192]{3,2,1,0:T(8,128)(2,1)} %bitcast.18, ...), custom_call_target="tpu_custom_call", output_to_operand_aliasing={{3}: (7, {})} | custom-call | tf_op jit(solution)/shard_map/pallas_call | solution.py:52
  129.0 9.7 %all_to_all.75 = bf16[16,8,544]{2,1,0:T(8,128)(2,1)S(1)} all-to-all(bf16[16,8,544]{2,1,0:T(8,128)(2,1)S(1)} %get-tuple-element.34), channel_id=1, replica_groups=mesh['z'=8,'x'=4,'y'=4,'core'=2] {'x','y'}, dimensions={0} | all-to-all | bytes 278528 | tf_op jit(solution)/shard_map/all_to_all | solution.py:27
  138.8 13.3 %all_to_all.76.refs_0_ = bf16[16,8,544]{2,1,0:T(8,128)(2,1)S(1)} all-to-all(bf16[16,8,544]{2,1,0:T(8,128)(2,1)S(1)} %broadcast_in_dim.19), channel_id=1, replica_groups=mesh['z'=8,'x'=4,'y'=4,'core'=2] {'core','z'}, dimensions={0} | all-to-all | bytes 278528 | tf_op jit(solution)/shard_map/all_to_all | solution.py:27
  152.0 0.0 copy-done
  152.1 0.0 copy-done.8
  152.1 0.8 shard_map.208
  152.9 19.9 %all_to_all.77 = bf16[256,2,128]{2,1,0:T(2,128)(2,1)S(1)} all-to-all(bf16[256,2,128]{2,1,0:T(2,128)(2,1)S(1)} %bitcast.14), channel_id=1, replica_groups=mesh['z'=8,'x'=4,'y'=4,'core'=2] {'core','z','x','y'}, dimensions={0} | all-to-all | bytes 262144 | tf_op jit(solution)/shard_map/all_to_all | solution.py:27
  172.8 1.1 shard_map.209
  (19 shorter events, 0.2 us)
Async XLA Ops:
  0.6 36.4 %copy-start.7 = (f32[2,8,16,64]{3,2,1,0:T(8,128)S(1)}, f32[2,8,16,64]{3,2,1,0:T(8,128)}, u32[]{:S(2)}) copy-start(f32[2,8,16,64]{3,2,1,0:T(8,128)} %refs_7_.3) | copy-start | bytes 196612
  0.6 36.4 %copy-start.15 = (f32[2,64]{1,0:T(2,128)S(1)}, f32[2,64]{1,0:T(2,128)}, u32[]{:S(2)}) copy-start(f32[2,64]{1,0:T(2,128)} %refs_6_.7) | copy-start | bytes 1540
  0.7 36.4 %copy-start.9 = (f32[2,16,64]{2,1,0:T(8,128)S(1)}, f32[2,16,64]{2,1,0:T(8,128)}, u32[]{:S(2)}) copy-start(f32[2,16,64]{2,1,0:T(8,128)} %refs_5_.3) | copy-start | bytes 24580
  0.7 36.4 %copy-start.14 = (f32[2,64]{1,0:T(2,128)S(1)}, f32[2,64]{1,0:T(2,128)}, u32[]{:S(2)}) copy-start(f32[2,64]{1,0:T(2,128)} %refs_4_.7) | copy-start | bytes 1540
  0.7 36.4 %copy-start.5 = (bf16[2,512,64]{1,2,0:T(8,128)(2,1)S(1)}, bf16[2,512,64]{1,2,0:T(8,128)(2,1)}, u32[]{:S(2)}) copy-start(bf16[2,512,64]{1,2,0:T(8,128)(2,1)} %param.25) | copy-start | bytes 393220
  0.7 61.7 %copy-start.3 = (bf16[256,1,1280]{2,0,1:T(8,128)(2,1)S(1)}, bf16[256,1,1280]{2,0,1:T(8,128)(2,1)}, u32[]{:S(2)}) copy-start(bf16[256,1,1280]{2,0,1:T(8,128)(2,1)} %param.31) | copy-start | bytes 1966084
  0.7 79.9 %copy-start.1 = (bf16[8,256,2,1,128]{4,2,3,1,0:T(2,128)(2,1)S(1)}, bf16[8,256,2,1,128]{4,2,3,1,0:T(2,128)(2,1)}, u32[]{:S(2)}) copy-start(bf16[8,256,2,1,128]{4,2,3,1,0:T(2,128)(2,1)} %param.33) | copy-start | bytes 3145732
  0.7 79.9 %copy-start.12 = (s32[8,32]{1,0:T(8,128)S(1)}, s32[8,32]{1,0:T(8,128)}, u32[]{:S(2)}) copy-start(s32[8,32]{1,0:T(8,128)} %table_ref.1) | copy-start | bytes 3076
  0.7 79.9 %copy-start.16 = (s32[8]{0:T(128)S(1)}, s32[8]{0:T(128)}, u32[]{:S(2)}) copy-start(s32[8]{0:T(128)} %lengths_ref.1) | copy-start | bytes 100
  18.8 107.6 %copy-start.2 = (bf16[2,64,544]{2,1,0:T(8,128)(2,1)S(1)}, bf16[2,64,544]{2,1,0:T(8,128)(2,1)}, u32[]{:S(2)}) copy-start(bf16[2,64,544]{2,1,0:T(8,128)(2,1)} %refs_6_.6) | copy-start | bytes 417796
  18.8 107.6 %copy-start.4 = (f32[3,8192]{1,0:T(4,128)S(1)}, f32[3,8192]{1,0:T(4,128)}, u32[]{:S(2)}) copy-start(f32[3,8192]{1,0:T(4,128)} %refs_1_.3) | copy-start | bytes 294916
  18.8 107.6 %copy-start.10 = (bf16[2,8,3,64]{3,1,2,0:T(8,128)(2,1)S(1)}, bf16[2,8,3,64]{3,1,2,0:T(8,128)(2,1)}, u32[]{:S(2)}) copy-start(bf16[2,8,3,64]{3,1,2,0:T(8,128)(2,1)} %param.23) | copy-start | bytes 18436
  18.8 107.6 %copy-start.11 = (f32[2,4,64]{2,1,0:T(4,128)S(1)}, f32[2,4,64]{2,1,0:T(4,128)}, u32[]{:S(2)}) copy-start(f32[2,4,64]{2,1,0:T(4,128)} %refs_3_.3) | copy-start | bytes 6148
  18.8 107.6 %copy-start.13 = (f32[2,64]{1,0:T(2,128)S(1)}, f32[2,64]{1,0:T(2,128)}, u32[]{:S(2)}) copy-start(f32[2,64]{1,0:T(2,128)} %refs_4_.6) | copy-start | bytes 1540
  80.6 71.5 %copy-start = (bf16[2,64,8192]{2,1,0:T(8,128)(2,1)S(1)}, bf16[2,64,8192]{2,1,0:T(8,128)(2,1)}, u32[]{:S(2)}) copy-start(bf16[2,64,8192]{2,1,0:T(8,128)(2,1)} %refs_8_.3) | copy-start | bytes 6291460
  82.4 69.7 %copy-start.6 = (bf16[2,512,64]{1,2,0:T(8,128)(2,1)S(1)}, bf16[2,512,64]{1,2,0:T(8,128)(2,1)}, u32[]{:S(2)}) copy-start(bf16[2,512,64]{1,2,0:T(8,128)(2,1)} %param.25) | copy-start | bytes 393220
  82.4 69.7 %copy-start.8 = (f32[2,8,16,64]{3,2,1,0:T(8,128)S(1)}, f32[2,8,16,64]{3,2,1,0:T(8,128)}, u32[]{:S(2)}) copy-start(f32[2,8,16,64]{3,2,1,0:T(8,128)} %refs_7_.3) | copy-start | bytes 196612
